TPU v7x, 32 devices: a whole 2x2x4 slice. The times are simulated.
32 devices in a mesh: fsdp: 4 (over y, x), cp: 8 (over z, core).
Axes of the slice: x: 2, y: 2, z: 4, core: 2. Of those that a mesh axis runs over, the one named last changes fastest.
Arguments:
- block_input: bfloat16 [4, 1024, 2048], P('fsdp', 'cp'), may hold values from -6 to 6
- cotangent: float32 [4, 1024, 2048], P('fsdp', 'cp'), may hold values from -6 to 6
- gain_attn: bfloat16 [2048], P(('fsdp', 'cp')), may hold values from 0.5 to 1.5
- w_query: bfloat16 [2048, 4096], P(('fsdp', 'cp')), may hold values from -0.125 to 0.125
- w_key: bfloat16 [2048, 512], P(('fsdp', 'cp')), may hold values from -0.125 to 0.125
- w_value: bfloat16 [2048, 512], P(('fsdp', 'cp')), may hold values from -0.125 to 0.125
- qk_gain: bfloat16 [2, 128], P(None, ('fsdp', 'cp')), as said below
- w_out: bfloat16 [4096, 2048], P(('fsdp', 'cp')), may hold values from -0.75 to 0.75
- gain_moe: bfloat16 [2048], P(('fsdp', 'cp')), may hold values from 0.5 to 1.5
- w_gate: bfloat16 [32, 2048, 768], P(('fsdp', 'cp')), may hold values from -0.125 to 0.125
- w_up: bfloat16 [32, 2048, 768], P(('fsdp', 'cp')), may hold values from -0.125 to 0.125
- w_down: bfloat16 [32, 768, 2048], P(('fsdp', 'cp')), may hold values from -0.4375 to 0.4375
- expert_ids: int32 [4, 1024, 8], P('fsdp', 'cp'), may hold values from 0 to 31, all different within a row; in each aligned block of 128 rows (0 to 127, 128 to 255, ..., all dimensions but the last counted through in order) at most 48 rows name the same one
- route_weight: bfloat16 [4, 1024, 8], P('fsdp', 'cp'), may hold values from 0.29882812 to 1
- pair_order: int32 [8], replicated, may hold values from 0 to 7, each once
Outputs:
- block_output: bfloat16 [4, 1024, 2048], P('fsdp', 'cp')
- grad_input: float32 [4, 1024, 2048], P('fsdp', 'cp')
- grad_gain_attn: float32 [2048], P(('fsdp', 'cp'))
- grad_w_query: float32 [2048, 4096], P(('fsdp', 'cp'))
- grad_w_key: float32 [2048, 512], P(('fsdp', 'cp'))
- grad_w_value: float32 [2048, 512], P(('fsdp', 'cp'))
- grad_qk_gain: float32 [2, 128], P(None, ('fsdp', 'cp'))
- grad_w_out: float32 [4096, 2048], P(('fsdp', 'cp'))
- grad_gain_moe: float32 [2048], P(('fsdp', 'cp'))
- grad_w_gate: float32 [32, 2048, 768], P(('fsdp', 'cp'))
- grad_w_up: float32 [32, 2048, 768], P(('fsdp', 'cp'))
- grad_w_down: float32 [32, 768, 2048], P(('fsdp', 'cp'))
Inputs may be any that keep to these rules, and one draw needn't show every extreme that they name: `expert_ids`: each row names 8 different experts. The rows of one device (aligned blocks of 128 rows of the first two dimensions taken together) name no expert more than 48 times, and in every draw some device's rows name some expert exactly 48 times. `pair_order`: each value appears once. `qk_gain`: the two rows are positive gains.
All inputs are finite; a program needn't handle non-finite values.
Results may differ from a plain program's by a relative error of at most 0.022.
The roundings to bfloat16 on the way count: a program that leaves them out, or rounds other values in their place, can miss the bound.
Values may be sent and summed in bfloat16 or wider, within the bound.
A program may use at most 320 MiB of HBM per device.

v0:
```python
import math

import jax
import jax.numpy as jnp
from jax import lax
from jax.sharding import PartitionSpec as P

BLOCK = 64


EPSILON = 1e-06
THETA = 1000000.0


def rms_scale(values, gain):
    return values * lax.rsqrt(jnp.mean(values * values, axis=-1, keepdims=True) + EPSILON) * gain


def rotate_half(values):
    half = values.shape[-1] // 2
    return jnp.concatenate([-values[..., half:], values[..., :half]], axis=-1)


def head_post(pre, gain, cosine, sine):
    normed = rms_scale(pre, gain)
    return normed * cosine[:, None, :] + rotate_half(normed) * sine[:, None, :]


def rope_tables(positions, head_dim):
    freqs = THETA ** (-(jnp.arange(head_dim // 2, dtype=jnp.float32) * 2.0 / head_dim))
    angles = positions.astype(jnp.float32)[:, None] * freqs[None, :]
    angles = jnp.concatenate([angles, angles], axis=-1)
    return (jnp.cos(angles), jnp.sin(angles))


def seq_positions(pair_order, block):
    blocks = 2 * pair_order.shape[0]
    rows = jnp.arange(blocks * block, dtype=jnp.int32)
    owner = rows // (2 * block)
    first = pair_order[owner]
    which = jnp.where(rows // block % 2 == 0, first, blocks - 1 - first)
    return which * block + rows % block


def route_tables(ids, weights, experts, capacity):
    flat = ids.reshape(-1)
    onehot = (flat[:, None] == jnp.arange(experts, dtype=jnp.int32)[None, :]).astype(jnp.int32)
    before = jnp.cumsum(onehot, axis=0) - onehot
    rank = jnp.sum(before * onehot, axis=1)
    slots = (flat * capacity + rank).reshape(ids.shape)
    columns = jnp.arange(experts * capacity, dtype=jnp.int32)
    hits = slots[:, :, None] == columns[None, None, :]
    place = jnp.sum(hits.astype(jnp.float32), axis=1).astype(jnp.bfloat16)
    mixing = jnp.sum(jnp.where(hits, weights[:, :, None].astype(jnp.float32), 0.0), axis=1).astype(
        jnp.bfloat16
    )
    return (place, mixing)


def attend_head(query, keys, values, allowed, scale):
    scores = jnp.einsum("grd,sd->grs", query, keys, preferred_element_type=jnp.float32) * scale
    scores = jnp.where(allowed[None], scores, -jnp.inf)
    top = jnp.max(scores, axis=-1, keepdims=True)
    lse = top[..., 0] + jnp.log(jnp.sum(jnp.exp(scores - top), axis=-1))
    probs = jnp.exp(scores - lse[..., None]).astype(jnp.bfloat16)
    output = jnp.einsum("grs,sd->grd", probs, values, preferred_element_type=jnp.float32)
    return (output.astype(jnp.bfloat16), lse)


def attend_back(query, keys, values, output, grad_out, lse, allowed, scale):
    scores = jnp.einsum("grd,sd->grs", query, keys, preferred_element_type=jnp.float32) * scale
    scores = jnp.where(allowed[None], scores, -jnp.inf)
    probs = jnp.exp(scores - lse[..., None])
    grad_values = jnp.einsum(
        "grs,grd->sd", probs.astype(jnp.bfloat16), grad_out, preferred_element_type=jnp.float32
    )
    grad_probs = jnp.einsum("grd,sd->grs", grad_out, values, preferred_element_type=jnp.float32)
    delta = jnp.sum(grad_out.astype(jnp.float32) * output.astype(jnp.float32), axis=-1)
    grad_scores = (probs * (grad_probs - delta[..., None])).astype(jnp.bfloat16)
    grad_query = (
        jnp.einsum("grs,sd->grd", grad_scores, keys, preferred_element_type=jnp.float32) * scale
    )
    grad_keys = (
        jnp.einsum("grs,grd->sd", grad_scores, query, preferred_element_type=jnp.float32) * scale
    )
    return (grad_query, grad_keys, grad_values)


def contract_rows(left, right):
    return lax.dot_general(
        left, right, (((0,), (0,)), ((), ())), preferred_element_type=jnp.float32
    )


def contract_cols(left, right):
    return lax.dot_general(
        left, right, (((1,), (1,)), ((), ())), preferred_element_type=jnp.float32
    )


def body(
    block_input,
    cotangent,
    gain_attn,
    w_query,
    w_key,
    w_value,
    qk_gain,
    w_out,
    gain_moe,
    w_gate,
    w_up,
    w_down,
    expert_ids,
    route_weight,
    pair_order,
):
    g_attn, wq_full, wk_full, wv_full, qk_full, wo_full, g_moe = (
        lax.all_gather(gain_attn, ("fsdp", "cp"), axis=0, tiled=True),
        lax.all_gather(w_query, ("fsdp", "cp"), axis=0, tiled=True),
        lax.all_gather(w_key, ("fsdp", "cp"), axis=0, tiled=True),
        lax.all_gather(w_value, ("fsdp", "cp"), axis=0, tiled=True),
        lax.all_gather(qk_gain, ("fsdp", "cp"), axis=1, tiled=True),
        lax.all_gather(w_out, ("fsdp", "cp"), axis=0, tiled=True),
        lax.all_gather(gain_moe, ("fsdp", "cp"), axis=0, tiled=True),
    )
    rows = block_input.shape[1]
    width = block_input.shape[2]
    head_dim = qk_full.shape[1]
    kv_heads = wk_full.shape[1] // head_dim
    heads = wq_full.shape[1] // head_dim
    group = heads // kv_heads
    experts = lax.axis_size(("fsdp", "cp"))
    capacity = max(2, 3 * BLOCK * expert_ids.shape[2] // experts)
    scale = 1.0 / math.sqrt(head_dim)
    resid = block_input[0].astype(jnp.float32)
    normed_in = rms_scale(resid, g_attn.astype(jnp.float32)).astype(jnp.bfloat16)
    q_pre = jnp.dot(normed_in, wq_full, preferred_element_type=jnp.float32).reshape(
        rows, heads, head_dim
    )
    k_pre = jnp.dot(normed_in, wk_full, preferred_element_type=jnp.float32).reshape(
        rows, kv_heads, head_dim
    )
    value_rows = jnp.dot(normed_in, wv_full, preferred_element_type=jnp.float32).astype(
        jnp.bfloat16
    )
    all_pos = seq_positions(pair_order, BLOCK)
    local_pos = lax.dynamic_slice_in_dim(all_pos, lax.axis_index("cp") * rows, rows)
    cosine, sine = rope_tables(local_pos, head_dim)
    gains32 = qk_full.astype(jnp.float32)
    query_rot = head_post(q_pre, gains32[0], cosine, sine).astype(jnp.bfloat16)
    key_rot = head_post(k_pre, gains32[1], cosine, sine).astype(jnp.bfloat16)
    keys_all, values_all = (
        lax.all_gather(key_rot.reshape(rows, kv_heads * head_dim), "cp", axis=0, tiled=True),
        lax.all_gather(value_rows, "cp", axis=0, tiled=True),
    )
    span = keys_all.shape[0]
    allowed = all_pos[None, :] <= local_pos[:, None]
    query_heads = query_rot.reshape(rows, kv_heads, group, head_dim).transpose(1, 2, 0, 3)
    key_heads = keys_all.reshape(span, kv_heads, head_dim).transpose(1, 0, 2)
    value_heads = values_all.reshape(span, kv_heads, head_dim).transpose(1, 0, 2)
    context_heads, lse = lax.map(
        lambda item: attend_head(item[0], item[1], item[2], allowed, scale),
        (query_heads, key_heads, value_heads),
    )
    context = context_heads.transpose(2, 0, 1, 3).reshape(rows, heads * head_dim)
    hidden_res = resid + jnp.dot(context, wo_full, preferred_element_type=jnp.float32)
    normed_mid = rms_scale(hidden_res, g_moe.astype(jnp.float32)).astype(jnp.bfloat16)
    place, mixing = route_tables(expert_ids[0], route_weight[0], experts, capacity)
    sent = contract_rows(place, normed_mid).astype(jnp.bfloat16)
    arrived = lax.all_to_all(
        sent.reshape(experts, capacity, width),
        ("fsdp", "cp"),
        split_axis=0,
        concat_axis=0,
        tiled=True,
    ).reshape(experts * capacity, width)
    gate_w = w_gate[0]
    up_w = w_up[0]
    down_w = w_down[0]
    gate_pre = jnp.dot(arrived, gate_w, preferred_element_type=jnp.float32)
    up_pre = jnp.dot(arrived, up_w, preferred_element_type=jnp.float32)
    gate_sig = jax.nn.sigmoid(gate_pre)
    gate_act = gate_pre * gate_sig
    expert_hidden = (gate_act * up_pre).astype(jnp.bfloat16)
    expert_out = jnp.dot(expert_hidden, down_w, preferred_element_type=jnp.float32).astype(
        jnp.bfloat16
    )
    returned = lax.all_to_all(
        expert_out.reshape(experts, capacity, width),
        ("fsdp", "cp"),
        split_axis=0,
        concat_axis=0,
        tiled=True,
    ).reshape(experts * capacity, width)
    mixed = jnp.dot(mixing, returned, preferred_element_type=jnp.float32)
    block_output = (hidden_res + mixed).astype(jnp.bfloat16)
    g_attn, wq_full, wk_full, wv_full, qk_full, wo_full, g_moe = (
        lax.all_gather(gain_attn, ("fsdp", "cp"), axis=0, tiled=True),
        lax.all_gather(w_query, ("fsdp", "cp"), axis=0, tiled=True),
        lax.all_gather(w_key, ("fsdp", "cp"), axis=0, tiled=True),
        lax.all_gather(w_value, ("fsdp", "cp"), axis=0, tiled=True),
        lax.all_gather(qk_gain, ("fsdp", "cp"), axis=1, tiled=True),
        lax.all_gather(w_out, ("fsdp", "cp"), axis=0, tiled=True),
        lax.all_gather(gain_moe, ("fsdp", "cp"), axis=0, tiled=True),
    )
    attn_gain = g_attn.astype(jnp.float32)
    moe_gain = g_moe.astype(jnp.float32)
    gains_back = qk_full.astype(jnp.float32)
    grad_top = cotangent[0]
    grad_top_b = grad_top.astype(jnp.bfloat16)
    grad_sent = contract_rows(mixing, grad_top_b).astype(jnp.bfloat16)
    grad_arrived = lax.all_to_all(
        grad_sent.reshape(experts, capacity, width),
        ("fsdp", "cp"),
        split_axis=0,
        concat_axis=0,
        tiled=True,
    ).reshape(experts * capacity, width)
    grad_hidden = contract_cols(grad_arrived, down_w)
    grad_down = contract_rows(expert_hidden, grad_arrived)
    grad_gate_pre = (grad_hidden * up_pre * gate_sig * (1.0 + gate_pre * (1.0 - gate_sig))).astype(
        jnp.bfloat16
    )
    grad_up_pre = (grad_hidden * gate_act).astype(jnp.bfloat16)
    grad_gate = contract_rows(arrived, grad_gate_pre)
    grad_up = contract_rows(arrived, grad_up_pre)
    grad_rows = (contract_cols(grad_gate_pre, gate_w) + contract_cols(grad_up_pre, up_w)).astype(
        jnp.bfloat16
    )
    grad_back = lax.all_to_all(
        grad_rows.reshape(experts, capacity, width),
        ("fsdp", "cp"),
        split_axis=0,
        concat_axis=0,
        tiled=True,
    ).reshape(experts * capacity, width)
    grad_mid = jnp.dot(place, grad_back, preferred_element_type=jnp.float32)
    _, mid_back = jax.vjp(rms_scale, hidden_res, moe_gain)
    grad_res_mid, grad_moe_gain = mid_back(grad_mid)
    grad_res = grad_top + grad_res_mid
    grad_res_b = grad_res.astype(jnp.bfloat16)
    grad_wo = contract_rows(context, grad_res_b)
    grad_context = contract_cols(grad_res_b, wo_full).astype(jnp.bfloat16)
    grad_ctx_heads = grad_context.reshape(rows, kv_heads, group, head_dim).transpose(1, 2, 0, 3)
    grad_q_heads, grad_k_heads, grad_v_heads = lax.map(
        lambda it: attend_back(it[0], it[1], it[2], it[3], it[4], it[5], allowed, scale),
        (query_heads, key_heads, value_heads, context_heads, grad_ctx_heads, lse),
    )
    grad_keys_all = grad_k_heads.transpose(1, 0, 2).reshape(span, kv_heads * head_dim)
    grad_values_all = grad_v_heads.transpose(1, 0, 2).reshape(span, kv_heads * head_dim)
    grad_key_rot, grad_values = (
        lax.psum_scatter(
            grad_keys_all.astype(jnp.bfloat16), "cp", scatter_dimension=0, tiled=True
        ).astype(jnp.float32),
        lax.psum_scatter(
            grad_values_all.astype(jnp.bfloat16), "cp", scatter_dimension=0, tiled=True
        ).astype(jnp.float32),
    )
    grad_query_rot = grad_q_heads.transpose(2, 0, 1, 3).reshape(rows, heads, head_dim)
    _, query_back = jax.vjp(
        lambda pre, gain: head_post(pre, gain, cosine, sine), q_pre, gains_back[0]
    )
    grad_q_pre, grad_q_gain = query_back(grad_query_rot)
    _, key_back = jax.vjp(
        lambda pre, gain: head_post(pre, gain, cosine, sine), k_pre, gains_back[1]
    )
    grad_k_pre, grad_k_gain = key_back(grad_key_rot.reshape(rows, kv_heads, head_dim))
    grad_q_b = grad_q_pre.reshape(rows, heads * head_dim).astype(jnp.bfloat16)
    grad_k_b = grad_k_pre.reshape(rows, kv_heads * head_dim).astype(jnp.bfloat16)
    grad_v_b = grad_values.astype(jnp.bfloat16)
    grad_wq = contract_rows(normed_in, grad_q_b)
    grad_wk = contract_rows(normed_in, grad_k_b)
    grad_wv = contract_rows(normed_in, grad_v_b)
    grad_in_norm = (
        contract_cols(grad_q_b, wq_full)
        + contract_cols(grad_k_b, wk_full)
        + contract_cols(grad_v_b, wv_full)
    )
    _, in_back = jax.vjp(rms_scale, resid, attn_gain)
    grad_res_in, grad_attn_gain = in_back(grad_in_norm)
    grad_input = grad_res + grad_res_in
    grad_qk = jnp.stack([grad_q_gain, grad_k_gain])
    owned_grads = (
        lax.psum_scatter(grad_attn_gain, ("fsdp", "cp"), scatter_dimension=0, tiled=True),
        lax.psum_scatter(grad_wq, ("fsdp", "cp"), scatter_dimension=0, tiled=True),
        lax.psum_scatter(grad_wk, ("fsdp", "cp"), scatter_dimension=0, tiled=True),
        lax.psum_scatter(grad_wv, ("fsdp", "cp"), scatter_dimension=0, tiled=True),
        lax.psum_scatter(grad_qk, ("fsdp", "cp"), scatter_dimension=1, tiled=True),
        lax.psum_scatter(grad_wo, ("fsdp", "cp"), scatter_dimension=0, tiled=True),
        lax.psum_scatter(grad_moe_gain, ("fsdp", "cp"), scatter_dimension=0, tiled=True),
    )
    return (
        block_output[None],
        grad_input[None],
        owned_grads[0],
        owned_grads[1],
        owned_grads[2],
        owned_grads[3],
        owned_grads[4],
        owned_grads[5],
        owned_grads[6],
        grad_gate[None],
        grad_up[None],
        grad_down[None],
    )


def solution(mesh):
    return jax.shard_map(
        body,
        mesh=mesh,
        in_specs=(
            P("fsdp", "cp", None),
            P("fsdp", "cp", None),
            P(("fsdp", "cp")),
            P(("fsdp", "cp"), None),
            P(("fsdp", "cp"), None),
            P(("fsdp", "cp"), None),
            P(None, ("fsdp", "cp")),
            P(("fsdp", "cp"), None),
            P(("fsdp", "cp")),
            P(("fsdp", "cp"), None, None),
            P(("fsdp", "cp"), None, None),
            P(("fsdp", "cp"), None, None),
            P("fsdp", "cp", None),
            P("fsdp", "cp", None),
            P(),
        ),
        out_specs=(
            P("fsdp", "cp", None),
            P("fsdp", "cp", None),
            P(("fsdp", "cp")),
            P(("fsdp", "cp"), None),
            P(("fsdp", "cp"), None),
            P(("fsdp", "cp"), None),
            P(None, ("fsdp", "cp")),
            P(("fsdp", "cp"), None),
            P(("fsdp", "cp")),
            P(("fsdp", "cp"), None, None),
            P(("fsdp", "cp"), None, None),
            P(("fsdp", "cp"), None, None),
        ),
        check_vma=False,
    )
```

profile of v0, /device:TPU:0, one launch (start us, length us, event | category | flops | bytes accessed | tf_op | source)
XLA Modules:
  0.0 2097.3 jit_solution(11717116536025852964)
XLA Ops:
  10.4 42.1 %all-reduce.10 = (bf16[2048]{0:T(1024)(128)(2,1)S(1)}, bf16[2048]{0:T(1024)(128)(2,1)}) all-reduce(bf16[2048]{0:T(1024)(128)(2,1)S(1)} %dynamic-update-slice, bf16[2048]{0:T(1024)(128)(2,1)S(1)} %dynamic-update-slice.1), channel_id=1, replica_groups=mesh['fsdp'=4,'cp'=8] {'fsdp','cp'}, use_global_device_ids=true, to_apply=%add.4 | all-reduce | flops 4096 | bytes 16384
  52.6 40.7 %all-gather = bf16[32,4,2]{1,2,0:T(2,128)(2,1)S(1)} all-gather(bf16[1,4,2]{1,2,0:T(2,128)(2,1)} %bitcast.362), channel_id=1, replica_groups=mesh['fsdp'=4,'cp'=8] {'fsdp','cp'}, dimensions={0}, use_global_device_ids=true | all-gather | bytes 528 | tf_op jit(solution)/shard_map/all_gather | solution.py:123
  95.2 4.5 compare_select_fusion.1
  103.2 3.9 copy.103
  111.9 16.5 all-gather.14.cloned.1.call-done
  136.2 9.0 reduce-window.6
  145.8 7.8 select_reduce_fusion
  156.0 20.6 all-gather.16.cloned.1.call-done
  179.0 114.5 %all-gather.8.cloned.1.call-done = bf16[2048,4096]{1,0:T(8,128)(2,1)} async-done(((bf16[64,4096]{1,0:T(8,128)(2,1)}), bf16[2048,4096]{1,0:T(8,128)(2,1)}) %all-gather.8.cloned.1.call-update) | async-done | bytes 16777232 | tf_op jit(solution)/shard_map/all_gather | solution.py:120
  293.4 22.7 %copy.99 = bf16[4096,2048]{1,0:T(8,128)(2,1)} copy(bf16[4096,2048]{0,1:T(8,128)(2,1)} %bitcast.333) | data formatting | bytes 33554432 | tf_op jit(solution)/shard_map/dot_general | solution.py:138
  316.1 8.4 multiply_reduce_fusion.2
  329.8 26.2 %while.28 = (s32[]{:T(128)}, bf16[4,8,128,128]{3,2,1,0:T(8,128)(2,1)}, f32[4,8,128]{2,1,0:T(8,128)}, bf16[4,8,128,128]{3,2,1,0:T(8,128)(2,1)}, bf16[4,1024,128]{...) while((s32[]{:T(128)}, ...), condition=%wide.region_6.7_spmd.clone, body=%wide.region_3.6_spmd.clone.sunk | while | flops 548666368 | bytes 14195305 | solution.py:162
  358.9 50.0 %all-gather.18.cloned.1.call-done = bf16[4096,2048]{1,0:T(8,128)(2,1)} async-done(((bf16[128,2048]{1,0:T(8,128)(2,1)}), bf16[4096,2048]{1,0:T(8,128)(2,1)}) %all-gather.18.cloned.1.call-update) | async-done | bytes 16777232 | tf_op jit(solution)/shard_map/all_gather | solution.py:124
  408.9 8.6 multiply_reduce_fusion.5
  417.6 4.6 convolution_convert_fusion.2
  425.8 5.7 fusion.147
  431.6 134.1 %all-to-all-done = bf16[32,48,2048]{2,1,0:T(8,128)(2,1)} async-done(((bf16[32,48,2048]{2,1,0:T(8,128)(2,1)}), bf16[32,48,2048]{2,1,0:T(8,128)(2,1)}, u32[]{:S(2)}, u32[]{:S(2)}) %all-to-all-start) | async-done | bytes 6291488 | tf_op jit(solution)/shard_map/all_to_all | solution.py:171
  569.3 9.6 fusion.67
  578.9 8.5 fusion.63
  587.5 121.7 %all-to-all-done.2 = bf16[32,48,2048]{2,1,0:T(8,128)(2,1)} async-done(((bf16[32,48,2048]{2,1,0:T(8,128)(2,1)}), bf16[32,48,2048]{2,1,0:T(8,128)(2,1)}, u32[]{:S(2)}, u32[]{:S(2)}) %all-to-all-start.2) | async-done | bytes 6291488 | tf_op jit(solution)/shard_map/all_to_all | solution.py:213
  709.2 12.2 multiply_convert_fusion.1
  721.4 8.2 fusion.65
  729.6 10.0 add_convert_fusion
  743.6 139.6 %all-to-all-done.3 = bf16[32,48,2048]{2,1,0:T(8,128)(2,1)} async-done(((bf16[32,48,2048]{2,1,0:T(8,128)(2,1)}), bf16[32,48,2048]{2,1,0:T(8,128)(2,1)}, u32[]{:S(2)}, u32[]{:S(2)}) %all-to-all-start.3) | async-done | bytes 6291488 | tf_op jit(solution)/shard_map/all_to_all | solution.py:231
  883.2 5.1 multiply_reduce_fusion.3
  889.7 12.7 fusion.75
  905.3 69.5 %while.29 = (s32[]{:T(128)}, f32[4,8,128,128]{3,2,1,0:T(8,128)}, bf16[4,1024,128]{1,2,0:T(8,128)(2,1)}, bf16[4,1024,128]{1,2,0:T(8,128)(2,1)}, bf16[4,8,128,128]...) while((s32[]{:T(128)}, f32[4,8,128,128]{3,2,1,0:T(8,128)}, ...), condition=%wide.region_16.17_spmd.clone, body=%wide.region_14.16_spmd.clone.sunk | while | flops 1353710592 | bytes 44991180 | solution.py:246
  918.5 4.1 fusion.225
  935.9 4.1 fusion.225
  953.3 4.1 fusion.225
  970.6 4.1 fusion.225
  979.5 28.0 %reduce-scatter.20.cloned.1.call-done = bf16[128,512]{1,0:T(8,128)(2,1)} async-done(((bf16[1024,512]{1,0:T(8,128)(2,1)}), bf16[128,512]{1,0:T(8,128)(2,1)}) %reduce-scatter.20.cloned.1.call-update) | async-done | bytes 131088
  1017.3 23.9 %reduce-scatter.22.cloned.1.call-done = bf16[128,512]{1,0:T(8,128)(2,1)} async-done(((bf16[1024,512]{1,0:T(8,128)(2,1)}), bf16[128,512]{1,0:T(8,128)(2,1)}) %reduce-scatter.22.cloned.1.call-update) | async-done | bytes 131088
  1041.2 3.9 fusion.113
  1054.5 13.3 fusion.97
  1067.8 17.3 fusion.105
  1085.1 8.7 convolution_convert_fusion
  1093.8 4.0 all-to-all-start.1
  1097.8 9.8 convolution_bitcast_fusion.3
  1107.7 10.0 convolution_bitcast_fusion.2
  1117.7 10.0 convolution_bitcast_fusion.1
  1127.8 151.3 %all-to-all-done.1 = bf16[32,48,2048]{2,1,0:T(8,128)(2,1)} async-done(((bf16[32,48,2048]{2,1,0:T(8,128)(2,1)}), bf16[32,48,2048]{2,1,0:T(8,128)(2,1)}, u32[]{:S(2)}, u32[]{:S(2)}) %all-to-all-start.1) | async-done | bytes 6291488 | tf_op jit(solution)/shard_map/all_to_all | solution.py:189
  1279.1 4.8 fusion.70
  1283.9 12.9 fusion.150
  1301.6 38.7 %all-reduce.9 = (f32[2048]{0:T(1024)S(1)}, f32[2,128]{1,0:T(2,128)S(1)}, f32[2048]{0:T(1024)S(1)}) all-reduce(f32[2048]{0:T(1024)S(1)} %get-tuple-element.246, f32[2,128]{1,0:T(2,128)S(1)} %pad_maximum_fusion.1, f32[2048]{0:T(1024)S(1)} %copy-done.37), channel_id=4, replica_groups=mesh['fsdp'=4,'cp'=8] {'fsdp','cp'}, use_global_device_ids=true, to_apply=%region_23.24.clone | all-reduce | flops 4352 | bytes 34816
  1345.2 24.2 %reduce-scatter.16.cloned.1.call-done = f32[64,512]{1,0:T(8,128)} async-done(((f32[2048,512]{1,0:T(8,128)}), f32[64,512]{1,0:T(8,128)}) %reduce-scatter.16.cloned.1.call-update) | async-done | bytes 131088 | tf_op jit(solution)/shard_map/reduce_scatter | solution.py:288
  1369.4 360.5 %reduce-scatter.12.cloned.1.call-done = f32[64,4096]{1,0:T(8,128)} async-done(((f32[2048,4096]{1,0:T(8,128)}), f32[64,4096]{1,0:T(8,128)}) %reduce-scatter.12.cloned.1.call-update) | async-done | bytes 1048592 | tf_op jit(solution)/shard_map/reduce_scatter | solution.py:286
  1729.9 360.4 %reduce-scatter.18.cloned.1.call-done = f32[128,2048]{1,0:T(8,128)} async-done(((f32[4096,2048]{1,0:T(8,128)}), f32[128,2048]{1,0:T(8,128)}) %reduce-scatter.18.cloned.1.call-update) | async-done | bytes 1048592 | tf_op jit(solution)/shard_map/reduce_scatter | solution.py:290
  (297 shorter events, 162.3 us)
Async XLA Ops:
  7.2 702.0 %copy-start = (bf16[1,768,2048]{2,1,0:T(8,128)(2,1)S(1)}, bf16[1,768,2048]{2,1,0:T(8,128)(2,1)}, u32[]{:S(2)}) copy-start(bf16[1,768,2048]{2,1,0:T(8,128)(2,1)} %param.30) | copy-start | bytes 9437188
  7.2 96.0 %all-gather.10.cloned.1.call-start = ((), (), s32[]{:S(2)}) async-start(), calls=%async_computation.11 | async-start | bytes 2162688 | tf_op jit(solution)/shard_map/all_gather | solution.py:121
  7.9 120.4 %all-gather.14.cloned.1.call-start = ((), (), s32[]{:S(2)}) async-start(), calls=%async_computation.13 | async-start | bytes 2162688 | tf_op jit(solution)/shard_map/all_gather | solution.py:122
  8.7 144.9 %all-gather.12.cloned.1.call-start = ((), (), s32[]{:S(2)}) async-start(), calls=%async_computation.12 | async-start | bytes 1179648 | tf_op jit(solution)/shard_map/all_gather | solution.py:154
  52.6 263.6 %copy-start.27 = (f32[2048]{0:T(1024)}, f32[2048]{0:T(1024)S(1)}, u32[]{:S(2)}) copy-start(f32[2048]{0:T(1024)S(1)} %convert_element_type.169) | copy-start | bytes 24580
  100.8 9.6 copy-start.18
  100.8 9.6 copy-start.22
  102.6 7.1 copy-start.38
  103.2 6.5 copy-start.40
  111.8 64.7 %all-gather.16.cloned.1.call-start = ((), (), s32[]{:S(2)}) async-start(), calls=%async_computation.14 | async-start | bytes 1179648 | tf_op jit(solution)/shard_map/all_gather | solution.py:155
  131.3 162.1 %all-gather.8.cloned.1.call-start = ((), (), s32[]{:S(2)}) async-start(), calls=%async_computation.10 | async-start | bytes 17301504 | tf_op jit(solution)/shard_map/all_gather | solution.py:120
  131.9 277.0 %all-gather.18.cloned.1.call-start = ((), (), s32[]{:S(2)}) async-start(), calls=%async_computation.15 | async-start | bytes 17301504 | tf_op jit(solution)/shard_map/all_gather | solution.py:124
  153.6 272.2 %copy-start.10 = (bf16[128,1536]{1,0:T(8,128)(2,1)}, bf16[128,1536]{1,0:T(8,128)(2,1)S(1)}, u32[]{:S(2)}) copy-start(bf16[128,1536]{1,0:T(8,128)(2,1)S(1)} %get-tuple-element.250) | copy-start | bytes 1179652
  316.1 8.5 copy-start.41
  408.9 8.7 copy-start.12
  408.9 8.7 copy-start.34
  422.2 143.5 %all-to-all-start = ((bf16[32,48,2048]{2,1,0:T(8,128)(2,1)}), bf16[32,48,2048]{2,1,0:T(8,128)(2,1)}, u32[]{:S(2)}, u32[]{:S(2)}) async-start(bf16[32,48,2048]{2,1,0:T(8,128)(2,1)} %bitcast.335), calls=%async_computation | async-start | bytes 12582912 | tf_op jit(solution)/shard_map/all_to_all | solution.py:171
  565.7 143.5 %all-to-all-start.2 = ((bf16[32,48,2048]{2,1,0:T(8,128)(2,1)}), bf16[32,48,2048]{2,1,0:T(8,128)(2,1)}, u32[]{:S(2)}, u32[]{:S(2)}) async-start(bf16[32,48,2048]{2,1,0:T(8,128)(2,1)} %bitcast.334), calls=%async_computation.2 | async-start | bytes 12582912 | tf_op jit(solution)/shard_map/all_to_all | solution.py:213
  569.3 9.6 copy-start.53
  709.2 12.2 copy-start.52
  721.4 8.2 copy-start.56
  721.4 8.2 copy-start.57
  721.4 8.2 copy-start.54
  739.6 143.6 %copy-start.13 = (bf16[128,1536]{1,0:T(8,128)(2,1)S(1)}, bf16[128,1536]{1,0:T(8,128)(2,1)}, u32[]{:S(2)}) copy-start(bf16[128,1536]{1,0:T(8,128)(2,1)} %get-tuple-element.251) | copy-start | bytes 1179652
  739.6 143.6 %all-to-all-start.3 = ((bf16[32,48,2048]{2,1,0:T(8,128)(2,1)}), bf16[32,48,2048]{2,1,0:T(8,128)(2,1)}, u32[]{:S(2)}, u32[]{:S(2)}) async-start(bf16[32,48,2048]{2,1,0:T(8,128)(2,1)} %bitcast.343), calls=%async_computation.3 | async-start | bytes 12582912 | tf_op jit(solution)/shard_map/all_to_all | solution.py:231
  743.4 264.1 %reduce-scatter.20.cloned.1.call-start = ((), (), s32[]{:S(2)}) async-start(), calls=%async_computation.20 | async-start | bytes 1179648
  883.2 5.2 copy-start.51
  883.2 5.2 copy-start.7
  883.2 5.2 copy-start.15
  883.2 5.2 copy-start.45
  974.7 34.7 %copy-start.17 = (f32[128,4,128]{0,2,1:T(8,128)S(1)}, f32[128,4,128]{0,2,1:T(8,128)}, u32[]{:S(2)}) copy-start(f32[128,4,128]{0,2,1:T(8,128)} %copy-done.16) | copy-start | bytes 786436
  974.7 34.7 %copy-start.36 = (f32[128,4]{0,1:T(4,128)S(1)}, f32[128,4]{0,1:T(4,128)}, u32[]{:S(2)}) copy-start(f32[128,4]{0,1:T(4,128)} %copy-done.35) | copy-start | bytes 6148
  974.7 38.5 %copy-start.28 = (f32[2048]{0:T(1024)S(1)}, f32[2048]{0:T(1024)}, u32[]{:S(2)}) copy-start(f32[2048]{0:T(1024)} %copy-done.27) | copy-start | bytes 24580
  974.8 38.5 %copy-start.39 = (f32[128]{0:T(128)S(1)}, f32[128]{0:T(128)}, u32[]{:S(2)}) copy-start(f32[128]{0:T(128)} %copy-done.38) | copy-start | bytes 1540
  977.1 64.1 %reduce-scatter.22.cloned.1.call-start = ((), (), s32[]{:S(2)}) async-start(), calls=%async_computation.21 | async-start | bytes 1179648
  979.5 365.7 %reduce-scatter.14.cloned.1.call-start = ((), (), s32[]{:S(2)}) async-start(), calls=%async_computation.17 | async-start | bytes 4325376 | tf_op jit(solution)/shard_map/reduce_scatter | solution.py:287
  1017.1 352.3 %reduce-scatter.16.cloned.1.call-start = ((), (), s32[]{:S(2)}) async-start(), calls=%async_computation.18 | async-start | bytes 4325376 | tf_op jit(solution)/shard_map/reduce_scatter | solution.py:288
  1045.1 684.8 %reduce-scatter.12.cloned.1.call-start = ((), (), s32[]{:S(2)}) async-start(), calls=%async_computation.16 | async-start | bytes 34603008 | tf_op jit(solution)/shard_map/reduce_scatter | solution.py:286
  1067.8 1022.5 %reduce-scatter.18.cloned.1.call-start = ((), (), s32[]{:S(2)}) async-start(), calls=%async_computation.19 | async-start | bytes 34603008 | tf_op jit(solution)/shard_map/reduce_scatter | solution.py:290
  1093.8 185.3 %all-to-all-start.1 = ((bf16[32,48,2048]{2,1,0:T(8,128)(2,1)}), bf16[32,48,2048]{2,1,0:T(8,128)(2,1)}, u32[]{:S(2)}, u32[]{:S(2)}) async-start(bf16[32,48,2048]{2,1,0:T(8,128)(2,1)} %bitcast.342), calls=%async_computation.1 | async-start | bytes 12582912 | tf_op jit(solution)/shard_map/all_to_all | solution.py:189
  1097.8 9.9 copy-start.58
  1107.7 10.0 copy-start.55
  1117.7 161.3 %copy-start.11 = (bf16[128,1536]{1,0:T(8,128)(2,1)S(1)}, bf16[128,1536]{1,0:T(8,128)(2,1)}, u32[]{:S(2)}) copy-start(bf16[128,1536]{1,0:T(8,128)(2,1)} %copy-done.10) | copy-start | bytes 1179652
  1283.9 12.9 copy-start.46
  1283.9 12.9 copy-start.47
  1283.9 12.9 copy-start.26
  1296.8 4.8 copy-start.37
  1296.8 45.3 %copy-start.49 = (f32[128]{0:T(128)S(1)}, f32[128]{0:T(128)}, u32[]{:S(2)}) copy-start(f32[128]{0:T(128)} %copy-done.48) | copy-start | bytes 1540
  (33 other events, 80.7 us)
Sparse Core Ops, SparseCore 0:
  11.0 59.0 all-gather.9
  73.1 55.2 all-gather.13
  130.5 22.7 all-gather.11
  155.4 21.1 all-gather.15
  179.4 113.9 all-gather.7
  296.3 112.5 all-gather.17
  977.2 30.2 reduce-scatter.19
  1010.3 30.8 reduce-scatter.21
  1044.1 161.5 reduce-scatter.13
  1208.3 160.9 reduce-scatter.15
  1372.2 357.6 reduce-scatter.11
  1732.6 357.6 reduce-scatter.17
where the time goes:
time: 2100 us
  waiting for transfers between devices  1550 us (74%)
  matrix products  270 us (13%)
  blocking collectives  122 us (6%)
  local copies, waits for them, and re-layouts  70.3 us (3%)
  other arithmetic  55.9 us (3%)
    reduce_scatter x1, waiting for transfers between devices, body(): lax.psum_scatter(grad_wq, ('fsdp', 'cp'), scatter_dimension=0, tiled=True)  361 us
    reduce_scatter x1, waiting for transfers between devices, body(): lax.psum_scatter(grad_wo, ('fsdp', 'cp'), scatter_dimension=0, tiled=True)  360 us
    all_to_all x1, waiting for transfers between devices, body(): lax.all_to_all(expert_out.reshape(experts, capacity, width), ('fsdp', 'cp...  151 us
    all_to_all x1, waiting for transfers between devices, body(): lax.all_to_all(grad_rows.reshape(experts, capacity, width), ('fsdp', 'cp'...  140 us
    all_to_all x1, waiting for transfers between devices, body(): lax.all_to_all(sent.reshape(experts, capacity, width), ('fsdp', 'cp'), sp...  134 us
    all_to_all x1, waiting for transfers between devices, body(): lax.all_to_all(grad_sent.reshape(experts, capacity, width), ('fsdp', 'cp'...  122 us
    all_gather x1, waiting for transfers between devices, body(): lax.all_gather(w_query, ('fsdp', 'cp'), axis=0, tiled=True)  114 us
    unnamed x2, blocking collectives  80.8 us
  transfers between devices with their start and end apart: 16, of which 13 were waited for; matrix products, arithmetic and copies ran while one was open for 12% of the time, Pallas kernels for 0%

commit v1 on v0

--- a/solution.py
+++ b/solution.py
@@ -1,8 +1,11 @@
+import functools
 import math
 
 import jax
 import jax.numpy as jnp
 from jax import lax
+from jax.experimental import pallas as pl
+from jax.experimental.pallas import tpu as pltpu
 from jax.sharding import PartitionSpec as P
 
 BLOCK = 64
@@ -98,7 +101,7 @@
     )
 
 
-def body(
+def wide_body(
     block_input,
     cotangent,
     gain_attn,
@@ -306,9 +309,841 @@
     )
 
 
+MESH = pl.DeviceIdType.MESH
+ANY = pl.BlockSpec(memory_space=pl.ANY)
+VM = pl.BlockSpec(memory_space=pltpu.VMEM)
+
+
+def place_of():
+    f = lax.axis_index("fsdp")
+    c = lax.axis_index("cp")
+    return f, c, c // 2, c % 2
+
+
+def flip(f, bit):
+    return f + bit - 2 * bit * ((f // bit) % 2)
+
+
+class Wire:
+    def __init__(self):
+        self.sent = []
+
+    def send(self, src, dst, ssem, rsem, dev, when=None):
+        copy = pltpu.make_async_remote_copy(
+            src_ref=src, dst_ref=dst, send_sem=ssem, recv_sem=rsem, device_id=dev, device_id_type=MESH
+        )
+        if when is None:
+            copy.start()
+        else:
+            pl.when(when)(copy.start)
+        self.sent.append((copy, when))
+
+    def drain(self):
+        for copy, when in self.sent:
+            if when is None:
+                copy.wait_send()
+            else:
+                pl.when(when)(copy.wait_send)
+
+
+def got(dst, ssem, rsem, dev, when=None):
+    copy = pltpu.make_async_remote_copy(
+        src_ref=dst, dst_ref=dst, send_sem=ssem, recv_sem=rsem, device_id=dev, device_id_type=MESH
+    )
+    if when is None:
+        copy.wait_recv()
+    else:
+        pl.when(when)(copy.wait_recv)
+
+
+def greet(f, c, z, zs, planes):
+    bar = pltpu.get_barrier_semaphore()
+    k = c % 2
+    sib = c + 1 - 2 * k
+    near = [((f, sib), None), ((f, c + 2), z < zs - 1), ((f, c - 2), z > 0)]
+    if planes:
+        near += [((flip(f, 1), c), None), ((flip(f, 2), c), None)]
+    for dev, when in near:
+        def hello(dev=dev):
+            pl.semaphore_signal(bar, inc=1, device_id=dev, device_id_type=MESH)
+        if when is None:
+            hello()
+        else:
+            pl.when(when)(hello)
+    base = 3 if planes else 1
+    inner = jnp.logical_and(z > 0, z < zs - 1)
+    pl.semaphore_wait(bar, base + jnp.where(inner, 2, 1))
+
+
+def ag_kernel(zs, planes, x_ref, o_ref, loc, sl, szr, szl, rz, sp1, rp1, sp2, rp2, ssib, rsib):
+    f, c, z, k = place_of()
+    half = x_ref.shape[1] // 2
+    sib = (f, c + 1 - 2 * k)
+    b1 = 1 + k
+    b2 = 2 - k
+    f1 = flip(f, b1)
+    f2 = flip(f, b2)
+    cols = [f, f1, f2, flip(f1, b2)] if planes else [0]
+    cs = 2 * zs
+
+    def chunk(col, zz):
+        at = (cols[col] * cs if planes else 0) + 2 * zz
+        return o_ref.at[pl.ds(at, 2), :, pl.ds(pl.multiple_of(k * half, 128), half)]
+
+    def other(col, zz):
+        at = (cols[col] * cs if planes else 0) + 2 * zz
+        return o_ref.at[pl.ds(at, 2), :, pl.ds(pl.multiple_of((1 - k) * half, 128), half)]
+
+    mine = (f * cs if planes else 0) + c
+    theirs = (f * cs if planes else 0) + c + 1 - 2 * k
+    own = pltpu.make_async_copy(x_ref, o_ref.at[mine], loc)
+    own.start()
+    greet(f, c, z, zs, planes)
+    w = Wire()
+    w.send(x_ref, o_ref.at[mine], sl.at[0], sl.at[1], sib)
+    own.wait()
+    got(o_ref.at[theirs], sl.at[0], sl.at[1], sib)
+
+    def spread(zz, when):
+        if planes:
+            w.send(chunk(0, zz), chunk(0, zz), sp1.at[zz], rp1.at[zz], (f1, c), when)
+            w.send(chunk(0, zz), chunk(0, zz), sp2.at[zz], rp2.at[zz], (f2, c), when)
+
+    def relay(zz, when):
+        if planes:
+            got(chunk(1, zz), sp1.at[zz], rp1.at[zz], (f1, c), when)
+            w.send(chunk(1, zz), chunk(1, zz), sp2.at[zs + zz], rp2.at[zs + zz], (f2, c), when)
+            w.send(chunk(1, zz), chunk(1, zz), ssib.at[zs + zz], rsib.at[zs + zz], sib, when)
+
+    w.send(chunk(0, z), chunk(0, z), szr.at[z], rz.at[z], (f, c + 2), z < zs - 1)
+    w.send(chunk(0, z), chunk(0, z), szl.at[z], rz.at[z], (f, c - 2), z > 0)
+    spread(z, None)
+    order = []
+    for h in range(1, zs):
+        for zz, when, on, dz, sem in (
+            (z - h, z - h >= 0, z < zs - 1, 2, szr),
+            (z + h, z + h < zs, z > 0, -2, szl),
+        ):
+            got(chunk(0, zz), sem.at[zz], rz.at[zz], (f, c), when)
+            w.send(chunk(0, zz), chunk(0, zz), sem.at[zz], rz.at[zz], (f, c + dz), jnp.logical_and(when, on))
+            spread(zz, when)
+            w.send(chunk(0, zz), chunk(0, zz), ssib.at[zz], rsib.at[zz], sib, when)
+            order.append((zz, when))
+        if h == 1:
+            relay(z, None)
+    for zz, when in order:
+        relay(zz, when)
+    if planes:
+        for col, base in ((2, 0), (3, zs)):
+            for zz, when in [(z, None)] + order:
+                got(chunk(col, zz), sp2.at[base + zz], rp2.at[base + zz], (f2, c), when)
+                w.send(chunk(col, zz), chunk(col, zz), ssib.at[col * zs + zz], rsib.at[col * zs + zz], sib, when)
+    if planes:
+        for mycol, theircol in ((0, 0), (1, 2), (2, 1), (3, 3)):
+            for zz, when in ([(z, None)] if mycol else []) + order:
+                got(other(mycol, zz), ssib.at[theircol * zs + zz], rsib.at[theircol * zs + zz], sib, when)
+    else:
+        for zz, when in order:
+            got(other(0, zz), ssib.at[zz], rsib.at[zz], sib, when)
+    w.drain()
+
+
+def gather(x, zs, planes, cid, nf=4):
+    rows, width = x.shape
+    n = (nf if planes else 1) * 2 * zs
+    D = pltpu.SemaphoreType.DMA
+    return pl.pallas_call(
+        functools.partial(ag_kernel, zs, planes),
+        out_shape=jax.ShapeDtypeStruct((n, rows, width), x.dtype),
+        in_specs=[VM],
+        out_specs=ANY,
+        scratch_shapes=[D(()), D((2,)), D((zs,)), D((zs,)), D((zs,)), D((zs,)), D((zs,)), D((2 * zs,)), D((2 * zs,)), D((4 * zs,)), D((4 * zs,))],
+        compiler_params=pltpu.CompilerParams(collective_id=cid, has_side_effects=True),
+        name="gather_all" if planes else "gather_seq",
+    )(x)
+
+
+def add_into(dst, src, rows=32):
+    n, r, wd = dst.shape
+
+    def step(i, _):
+        a = pl.ds(pl.multiple_of(i % (r // rows) * rows, rows), rows)
+        j = i // (r // rows)
+        dst[j, a, :] = (dst[j, a, :].astype(jnp.float32) + src[j, a, :].astype(jnp.float32)).astype(dst.dtype)
+        return 0
+
+    lax.fori_loop(0, n * (r // rows), step, 0)
+
+
+def rs_kernel(zs, planes, x_ref, o_ref, t, r0, r1, r2, ral, rar, fin, lsem, s0, q0, s1, q1, s2, q2, szr, szl, rzr, rzl, sf):
+    f, c, z, k = place_of()
+    half = o_ref.shape[1] // 2
+    sib = (f, c + 1 - 2 * k)
+    b1 = 2 - k
+    b2 = 1 + k
+    f1 = flip(f, b1)
+    f2 = flip(f, b2)
+    f3 = flip(f1, b2)
+    cs = 2 * zs
+    cols = [f3, f1, f2, f] if planes else [0]
+    nc = len(cols)
+    last = zs - 1
+    low = z < zs // 2
+    zord = []
+    for i in range(zs - 1):
+        far_low = jnp.where(i < zs - 1 - z, last - i, zs - 2 - i)
+        far_high = jnp.where(i < z, i, i + 1)
+        zord.append(jnp.where(low, far_low, far_high))
+    zord.append(z)
+
+    def src(col, zz, kk):
+        at = (col * cs if planes else 0) + 2 * zz
+        return x_ref.at[pl.ds(at, 2), :, pl.ds(pl.multiple_of(kk * half, 128), half)]
+
+    greet(f, c, z, zs, planes)
+    w = Wire()
+    locals_ = []
+    for ci in range(nc):
+        for zi in range(zs):
+            i = ci * zs + zi
+            col = cols[ci]
+            zz = zord[zi]
+            slot = (ci if not planes else {0: 0, 1: 2, 2: 1, 3: 3}[ci]) * zs + zz
+            w.send(src(col, zz, 1 - k), r0.at[slot], s0.at[slot], q0.at[slot], sib)
+            cp = pltpu.make_async_copy(src(col, zz, k), t.at[ci * zs + zz], lsem.at[i])
+            cp.start()
+            locals_.append(cp)
+
+    def first(ci, zi):
+        zz = zord[zi]
+        locals_[ci * zs + zi].wait()
+        got(r0.at[ci * zs + zz], s0.at[ci * zs + zz], q0.at[ci * zs + zz], sib)
+        add_into(t.at[ci * zs + zz], r0.at[ci * zs + zz])
+
+    if planes:
+        for ci in (0, 1):
+            for zi in range(zs):
+                zz = zord[zi]
+                first(ci, zi)
+                m = ci * zs + zz
+                w.send(t.at[m], r1.at[m], s1.at[m], q1.at[m], (f1, c))
+        for zi in range(zs):
+            zz = zord[zi]
+            first(2, zi)
+            got(r1.at[zz], s1.at[zz], q1.at[zz], (f1, c))
+            add_into(t.at[2 * zs + zz], r1.at[zz])
+            w.send(t.at[2 * zs + zz], r2.at[zz], s2.at[zz], q2.at[zz], (f2, c))
+        for zi in range(zs):
+            first(3, zi)
+        base = 3 * zs
+    else:
+        base = 0
+
+    def complete(zi):
+        zz = zord[zi]
+        if planes:
+            got(r1.at[zs + zz], s1.at[zs + zz], q1.at[zs + zz], (f1, c))
+            add_into(t.at[base + zz], r1.at[zs + zz])
+            got(r2.at[zz], s2.at[zz], q2.at[zz], (f2, c))
+            add_into(t.at[base + zz], r2.at[zz])
+        else:
+            first(0, zi)
+
+    for zi in range(zs - 1):
+        zz = zord[zi]
+        complete(zi)
+        right = zz > z
+        from_left = jnp.logical_and(right, z > 0)
+        from_right = jnp.logical_and(jnp.logical_not(right), z < zs - 1)
+        got(ral.at[zz], szr.at[zz], rzr.at[zz], (f, c), from_left)
+        got(rar.at[zz], szl.at[zz], rzl.at[zz], (f, c), from_right)
+
+        @pl.when(from_left)
+        def _():
+            add_into(t.at[base + zz], ral.at[zz])
+
+        @pl.when(from_right)
+        def _():
+            add_into(t.at[base + zz], rar.at[zz])
+
+        w.send(t.at[base + zz], ral.at[zz], szr.at[zz], rzr.at[zz], (f, c + 2), right)
+        w.send(t.at[base + zz], rar.at[zz], szl.at[zz], rzl.at[zz], (f, c - 2), jnp.logical_not(right))
+    complete(zs - 1)
+    got(ral.at[z], szr.at[z], rzr.at[z], (f, c), z > 0)
+    got(rar.at[z], szl.at[z], rzl.at[z], (f, c), z < zs - 1)
+
+    @pl.when(z > 0)
+    def _():
+        add_into(t.at[base + z], ral.at[z])
+
+    @pl.when(z < zs - 1)
+    def _():
+        add_into(t.at[base + z], rar.at[z])
+
+    w.send(t.at[base + z, 1 - k], fin, sf.at[0], sf.at[1], sib)
+    o_ref[:, pl.ds(pl.multiple_of(k * half, 128), half)] = t[base + z, k]
+    got(fin, sf.at[0], sf.at[1], sib)
+    o_ref[:, pl.ds(pl.multiple_of((1 - k) * half, 128), half)] = fin[...]
+    w.drain()
+
+
+def scatter(x, zs, planes, cid, nf=4):
+    n, rows, width = x.shape
+    D = pltpu.SemaphoreType.DMA
+    half = width // 2
+    nc = (nf if planes else 1) * zs
+    V = lambda m: pltpu.VMEM((m, 2, rows, half), x.dtype)
+    return pl.pallas_call(
+        functools.partial(rs_kernel, zs, planes),
+        out_shape=jax.ShapeDtypeStruct((rows, width), x.dtype),
+        in_specs=[ANY],
+        out_specs=VM,
+        scratch_shapes=[V(nc), V(nc), V(2 * zs), V(zs), V(zs), V(zs), pltpu.VMEM((rows, half), x.dtype),
+            D((nc,)), D((nc,)), D((nc,)), D((2 * zs,)), D((2 * zs,)), D((zs,)), D((zs,)), D((zs,)), D((zs,)), D((zs,)), D((zs,)), D((2,))],
+        compiler_params=pltpu.CompilerParams(collective_id=cid, has_side_effects=True, vmem_limit_bytes=60 * 2**20),
+        name="scatter_all" if planes else "scatter_seq",
+    )(x)
+
+
+def greet_all(f, c, nf, nc):
+    bar = pltpu.get_barrier_semaphore()
+    n = nf * nc
+    me = f * nc + c
+
+    def hello(i, _):
+        j = (me + i) % n
+        pl.semaphore_signal(bar, inc=1, device_id=(j // nc, j % nc), device_id_type=MESH)
+        return 0
+
+    lax.fori_loop(1, n, hello, 0)
+    pl.semaphore_wait(bar, n - 1)
+
+
+def deal_tiles(src, dst, ssem, rsem, f, c, nf, nc):
+    n = nf * nc
+    me = f * nc + c
+
+    def go(i, _):
+        j = (me + i) % n
+        pltpu.make_async_remote_copy(
+            src_ref=src.at[j], dst_ref=dst.at[me], send_sem=ssem, recv_sem=rsem,
+            device_id=(j // nc, j % nc), device_id_type=MESH,
+        ).start()
+        return 0
+
+    lax.fori_loop(1, n, go, 0)
+    dst[me] = src[me]
+
+
+def await_tiles(src, dst, ssem, rsem, f, c, nf, nc):
+    n = nf * nc
+    every = pltpu.make_async_remote_copy(
+        src_ref=src.at[pl.ds(0, n - 1)], dst_ref=dst.at[pl.ds(0, n - 1)], send_sem=ssem, recv_sem=rsem,
+        device_id=(f, c), device_id_type=MESH,
+    )
+    every.wait_send()
+    every.wait_recv()
+
+
+def front_kernel(nf, zs, x_ref, wp_ref, tl_ref, o_ref, w_ref, to_ref, loc, wloc, sl, szr, szl, rz, ssib, rsib, ts, tr, sw, rw, swx, swy):
+    f, c, z, k = place_of()
+    nc = 2 * zs
+    half = x_ref.shape[1] // 2
+    sib_c = c + 1 - 2 * k
+    sib = (f, sib_c)
+    fx, fy = flip(f, 1), flip(f, 2)
+    fr = [f, fx, fy, flip(fx, 2)]
+
+    def chunk(zz, kk):
+        return o_ref.at[pl.ds(2 * zz, 2), :, pl.ds(pl.multiple_of(kk * half, 128), half)]
+
+    def piece(rel, cc):
+        return w_ref.at[fr[rel] * nc + cc]
+
+    own = pltpu.make_async_copy(x_ref, o_ref.at[c], loc)
+    own.start()
+    wown = pltpu.make_async_copy(wp_ref.at[c], piece(0, c), wloc)
+    wown.start()
+    greet_all(f, c, nf, nc)
+    w = Wire()
+    w.send(x_ref, o_ref.at[c], sl.at[0], sl.at[1], sib)
+    w.send(wp_ref.at[sib_c], piece(0, c), sw.at[sib_c], rw.at[c], sib)
+    for h in range(1, zs):
+        for zz, when in ((z - h, z - h >= 0), (z + h, z + h < zs)):
+            for kk in (0, 1):
+                cc = 2 * zz + kk
+                w.send(wp_ref.at[cc], piece(0, c), sw.at[cc], rw.at[c], (f, cc), when)
+    own.wait()
+    got(o_ref.at[sib_c], sl.at[0], sl.at[1], sib)
+    w.send(chunk(z, k), chunk(z, k), szr.at[z], rz.at[z], (f, c + 2), z < zs - 1)
+    w.send(chunk(z, k), chunk(z, k), szl.at[z], rz.at[z], (f, c - 2), z > 0)
+    deal_tiles(tl_ref, to_ref, ts, tr, f, c, nf, nc)
+
+    def plane(cc, when):
+        w.send(piece(0, cc), piece(0, cc), swx.at[cc], rw.at[nc + cc], (fx, c), when)
+        w.send(piece(0, cc), piece(0, cc), swy.at[cc], rw.at[2 * nc + cc], (fy, c), when)
+
+    def onward(cc, kk, when):
+        if kk == 0:
+            got(piece(1, cc), swx.at[cc], rw.at[nc + cc], (fx, c), when)
+            w.send(piece(1, cc), piece(1, cc), swy.at[nc + cc], rw.at[3 * nc + cc], (fy, c), when)
+        else:
+            got(piece(2, cc), swy.at[cc], rw.at[2 * nc + cc], (fy, c), when)
+            w.send(piece(2, cc), piece(2, cc), swx.at[nc + cc], rw.at[3 * nc + cc], (fx, c), when)
+
+    wown.wait()
+    plane(c, None)
+    got(piece(0, sib_c), sw.at[sib_c], rw.at[sib_c], sib)
+    plane(sib_c, None)
+    far = []
+    for h in range(1, zs):
+        for zz, when, on, dz, sem in (
+            (z - h, z - h >= 0, z < zs - 1, 2, szr),
+            (z + h, z + h < zs, z > 0, -2, szl),
+        ):
+            for kk in (0, 1):
+                cc = 2 * zz + kk
+                got(piece(0, cc), sw.at[cc], rw.at[cc], (f, cc), when)
+                plane(cc, when)
+            far.append((zz, when))
+        for zz, when, on, dz, sem in (
+            (z - h, z - h >= 0, z < zs - 1, 2, szr),
+            (z + h, z + h < zs, z > 0, -2, szl),
+        ):
+            got(chunk(zz, k), sem.at[zz], rz.at[zz], (f, c), when)
+            w.send(chunk(zz, k), chunk(zz, k), sem.at[zz], rz.at[zz], (f, c + dz), jnp.logical_and(when, on))
+            w.send(chunk(zz, k), chunk(zz, k), ssib.at[zz], rsib.at[zz], sib, when)
+    everyone = [(z, None)] + far
+    for zz, when in everyone:
+        for kk in (0, 1):
+            onward(2 * zz + kk, kk, when)
+    for zz, when in everyone:
+        e, o = 2 * zz, 2 * zz + 1
+        got(piece(2, e), swy.at[e], rw.at[2 * nc + e], (fy, c), when)
+        got(piece(1, o), swx.at[o], rw.at[nc + o], (fx, c), when)
+        got(piece(3, e), swy.at[nc + e], rw.at[3 * nc + e], (fy, c), when)
+        got(piece(3, o), swx.at[nc + o], rw.at[3 * nc + o], (fx, c), when)
+    for zz, when in far:
+        got(chunk(zz, 1 - k), ssib.at[zz], rsib.at[zz], sib, when)
+    await_tiles(tl_ref, to_ref, ts, tr, f, c, nf, nc)
+    w.drain()
+
+
+def front(x, wp, tl, nf, zs, cid):
+    rows, width = x.shape
+    nc = 2 * zs
+    D = pltpu.SemaphoreType.DMA
+    return pl.pallas_call(
+        functools.partial(front_kernel, nf, zs),
+        out_shape=(
+            jax.ShapeDtypeStruct((nc, rows, width), x.dtype),
+            jax.ShapeDtypeStruct((nf * nc,) + wp.shape[1:], wp.dtype),
+            jax.ShapeDtypeStruct(tl.shape, tl.dtype),
+        ),
+        in_specs=[VM, VM, VM],
+        out_specs=(ANY, ANY, VM),
+        scratch_shapes=[D(()), D(()), D((2,)), D((zs,)), D((zs,)), D((zs,)), D((zs,)), D((zs,)), D(()), D(()), D((nc,)), D((4 * nc,)), D((2 * nc,)), D((2 * nc,))],
+        compiler_params=pltpu.CompilerParams(collective_id=cid, has_side_effects=True),
+        name="front",
+    )(x, wp, tl)
+
+
+def tail_kernel(nf, zs, x_ref, g_ref, tl_ref, o_ref, go_ref, to_ref, t, r0, ral, rar, fin, gt, ga, gb, lsem, s0, q0, szr, szl, rzr, rzl, sf, ts, tr, gl, sg, rg, sa, ra):
+    f, c, z, k = place_of()
+    nc = 2 * zs
+    half = o_ref.shape[1] // 2
+    sib_c = c + 1 - 2 * k
+    sib = (f, sib_c)
+    low = z < zs // 2
+    zord = []
+    for i in range(zs - 1):
+        far_low = jnp.where(i < zs - 1 - z, zs - 1 - i, zs - 2 - i)
+        far_high = jnp.where(i < z, i, i + 1)
+        zord.append(jnp.where(low, far_low, far_high))
+    zord.append(z)
+
+    def src(zz, kk):
+        return x_ref.at[pl.ds(2 * zz, 2), :, pl.ds(pl.multiple_of(kk * half, 128), half)]
+
+    hc = nc // 2
+    parts = []
+    for p in (0, 1):
+        fa = flip(f, 1 + p)
+        fb = flip(f, 2 - p)
+        parts.append((fa, fb, flip(fa, 2 - p)))
+    gcopies = []
+    for p, (fa, fb, fc) in enumerate(parts):
+        for i, col in enumerate((fb, f)):
+            cp = pltpu.make_async_copy(g_ref.at[col, pl.ds(p * hc, hc)], gt.at[p, i], gl.at[2 * p + i])
+            cp.start()
+            gcopies.append(cp)
+    greet_all(f, c, nf, nc)
+    w = Wire()
+    for p, (fa, fb, fc) in enumerate(parts):
+        for i, col in enumerate((fc, fa)):
+            w.send(g_ref.at[col, pl.ds(p * hc, hc)], ga.at[p, i], sg.at[2 * p + i], rg.at[2 * p + i], (fa, c))
+    locals_ = []
+    for zi in range(zs):
+        zz = zord[zi]
+        w.send(src(zz, 1 - k), r0.at[zz], s0.at[zz], q0.at[zz], sib)
+        cp = pltpu.make_async_copy(src(zz, k), t.at[zz], lsem.at[zi])
+        cp.start()
+        locals_.append(cp)
+    deal_tiles(tl_ref, to_ref, ts, tr, f, c, nf, nc)
+
+    def complete(zi):
+        zz = zord[zi]
+        locals_[zi].wait()
+        got(r0.at[zz], s0.at[zz], q0.at[zz], sib)
+        add_into(t.at[zz], r0.at[zz])
+
+    for zi in range(zs - 1):
+        zz = zord[zi]
+        complete(zi)
+        right = zz > z
+        from_left = jnp.logical_and(right, z > 0)
+        from_right = jnp.logical_and(jnp.logical_not(right), z < zs - 1)
+        got(ral.at[zz], szr.at[zz], rzr.at[zz], (f, c), from_left)
+        got(rar.at[zz], szl.at[zz], rzl.at[zz], (f, c), from_right)
+
+        @pl.when(from_left)
+        def _():
+            add_into(t.at[zz], ral.at[zz])
+
+        @pl.when(from_right)
+        def _():
+            add_into(t.at[zz], rar.at[zz])
+
+        w.send(t.at[zz], ral.at[zz], szr.at[zz], rzr.at[zz], (f, c + 2), right)
+        w.send(t.at[zz], rar.at[zz], szl.at[zz], rzl.at[zz], (f, c - 2), jnp.logical_not(right))
+        if zi == 0:
+            for p, (fa, fb, fc) in enumerate(parts):
+                for i in (0, 1):
+                    gcopies[2 * p + i].wait()
+                    got(ga.at[p, i], sg.at[2 * p + i], rg.at[2 * p + i], (fa, c))
+                    add_into(gt.at[p, i], ga.at[p, i])
+                    if i == 0:
+                        w.send(gt.at[p, 0], gb.at[p], sg.at[4 + p], rg.at[4 + p], (fb, c))
+        if zi == 1:
+            for p, (fa, fb, fc) in enumerate(parts):
+                got(gb.at[p], sg.at[4 + p], rg.at[4 + p], (fb, c))
+                add_into(gt.at[p, 1], gb.at[p])
+            for cc in range(nc):
+                w.send(gt.at[cc // hc, 1, cc % hc], go_ref.at[c], sa.at[cc], ra.at[c], (f, cc), c != cc)
+
+            def keep(cc):
+                @pl.when(c == cc)
+                def _():
+                    go_ref[cc] = gt[cc // hc, 1, cc % hc]
+
+            for cc in range(nc):
+                keep(cc)
+    complete(zs - 1)
+    got(ral.at[z], szr.at[z], rzr.at[z], (f, c), z > 0)
+    got(rar.at[z], szl.at[z], rzl.at[z], (f, c), z < zs - 1)
+
+    @pl.when(z > 0)
+    def _():
+        add_into(t.at[z], ral.at[z])
+
+    @pl.when(z < zs - 1)
+    def _():
+        add_into(t.at[z], rar.at[z])
+
+    w.send(t.at[z, 1 - k], fin, sf.at[0], sf.at[1], sib)
+    o_ref[:, pl.ds(pl.multiple_of(k * half, 128), half)] = t[z, k]
+    for cc in range(nc):
+        got(go_ref.at[cc], sa.at[cc], ra.at[cc], (f, c), c != cc)
+    got(fin, sf.at[0], sf.at[1], sib)
+    o_ref[:, pl.ds(pl.multiple_of((1 - k) * half, 128), half)] = fin[...]
+    await_tiles(tl_ref, to_ref, ts, tr, f, c, nf, nc)
+    w.drain()
+
+
+def tail(x, g, tl, nf, zs, cid):
+    n, rows, width = x.shape
+    nc = 2 * zs
+    D = pltpu.SemaphoreType.DMA
+    half = width // 2
+    V = lambda m: pltpu.VMEM((m, 2, rows, half), x.dtype)
+    gs = g.shape[2:]
+    G = lambda *lead: pltpu.VMEM(lead + (nc // 2,) + gs, g.dtype)
+    return pl.pallas_call(
+        functools.partial(tail_kernel, nf, zs),
+        out_shape=(
+            jax.ShapeDtypeStruct((rows, width), x.dtype),
+            jax.ShapeDtypeStruct((nc,) + gs, g.dtype),
+            jax.ShapeDtypeStruct(tl.shape, tl.dtype),
+        ),
+        in_specs=[ANY, ANY, VM],
+        out_specs=(VM, VM, VM),
+        scratch_shapes=[V(zs), V(zs), V(zs), V(zs), pltpu.VMEM((rows, half), x.dtype), G(2, 2), G(2, 2), G(2),
+            D((zs,)), D((zs,)), D((zs,)), D((zs,)), D((zs,)), D((zs,)), D((zs,)), D((2,)), D(()), D(()), D((4,)), D((6,)), D((6,)), D((nc,)), D((nc,))],
+        compiler_params=pltpu.CompilerParams(collective_id=cid, has_side_effects=True, vmem_limit_bytes=60 * 2**20),
+        name="tail",
+    )(x, g, tl)
+
+
+def attend_kernel(scale, qb, q_ref, k_ref, v_ref, pr_ref, pc_ref, o_ref, l_ref):
+    rows = q_ref.shape[0]
+    keys = k_ref[...]
+    values = v_ref[...]
+    for i in range(rows // qb):
+        at = pl.ds(i * qb, qb)
+        s = lax.dot_general(q_ref[at, :], keys, (((1,), (1,)), ((), ())), preferred_element_type=jnp.float32) * scale
+        s = jnp.where(pc_ref[...] <= pr_ref[at, :], s, -jnp.inf)
+        top = jnp.max(s, axis=-1, keepdims=True)
+        e = jnp.exp(s - top)
+        total = jnp.sum(e, axis=-1, keepdims=True)
+        p = (e * (1.0 / total)).astype(jnp.bfloat16)
+        o_ref[at, :] = jnp.dot(p, values, preferred_element_type=jnp.float32).astype(jnp.bfloat16)
+        l_ref[at, :] = jnp.broadcast_to(top + jnp.log(total), (qb, l_ref.shape[1]))
+
+
+def attend(q, keys, values, pos, scale):
+    rows, width = q.shape
+    hd = keys.shape[1]
+    col = pl.BlockSpec((rows, hd), lambda h: (0, h))
+    full = pl.BlockSpec((rows, hd), lambda h: (0, 0))
+    return pl.pallas_call(
+        functools.partial(attend_kernel, scale, 256),
+        grid=(width // hd,),
+        out_shape=(jax.ShapeDtypeStruct((rows, width), jnp.bfloat16), jax.ShapeDtypeStruct((rows, width), jnp.float32)),
+        in_specs=[col, full, full, pl.BlockSpec((rows, 1), lambda h: (0, 0)), pl.BlockSpec((1, rows), lambda h: (0, 0))],
+        out_specs=(col, col),
+        name="attend",
+    )(q, keys, values, pos[:, None], pos[None, :])
+
+
+def attend_grad_kernel(scale, qb, q_ref, k_ref, v_ref, c_ref, g_ref, l_ref, pr_ref, pc_ref, gq_ref, gk_ref, gv_ref):
+    rows = q_ref.shape[0]
+    keys = k_ref[...]
+    values = v_ref[...]
+
+    @pl.when(pl.program_id(0) == 0)
+    def _():
+        gk_ref[...] = jnp.zeros_like(gk_ref)
+        gv_ref[...] = jnp.zeros_like(gv_ref)
+
+    for i in range(rows // qb):
+        at = pl.ds(i * qb, qb)
+        q = q_ref[at, :]
+        g = g_ref[at, :]
+        s = lax.dot_general(q, keys, (((1,), (1,)), ((), ())), preferred_element_type=jnp.float32) * scale
+        p = jnp.where(pc_ref[...] <= pr_ref[at, :], jnp.exp(s - l_ref[at, 0:1]), 0.0)
+        gv_ref[...] += lax.dot_general(p.astype(jnp.bfloat16), g, (((0,), (0,)), ((), ())), preferred_element_type=jnp.float32)
+        gp = lax.dot_general(g, values, (((1,), (1,)), ((), ())), preferred_element_type=jnp.float32)
+        delta = jnp.sum(g.astype(jnp.float32) * c_ref[at, :].astype(jnp.float32), axis=-1, keepdims=True)
+        ds = (p * (gp - delta)).astype(jnp.bfloat16)
+        gq_ref[at, :] = jnp.dot(ds, keys, preferred_element_type=jnp.float32) * scale
+        gk_ref[...] += lax.dot_general(ds, q, (((0,), (0,)), ((), ())), preferred_element_type=jnp.float32) * scale
+
+
+def attend_grad(q, keys, values, ctx, grad, lse, pos, scale):
+    rows, width = q.shape
+    hd = keys.shape[1]
+    col = pl.BlockSpec((rows, hd), lambda h: (0, h))
+    full = pl.BlockSpec((rows, hd), lambda h: (0, 0))
+    return pl.pallas_call(
+        functools.partial(attend_grad_kernel, scale, 256),
+        grid=(width // hd,),
+        out_shape=(jax.ShapeDtypeStruct((rows, width), jnp.float32), jax.ShapeDtypeStruct((rows, hd), jnp.float32), jax.ShapeDtypeStruct((rows, hd), jnp.float32)),
+        in_specs=[col, full, full, col, col, col, pl.BlockSpec((rows, 1), lambda h: (0, 0)), pl.BlockSpec((1, rows), lambda h: (0, 0))],
+        out_specs=(col, full, full),
+        name="attend_grad",
+    )(q, keys, values, ctx, grad, lse, pos[:, None], pos[None, :])
+
+
+def head_body(
+    nf,
+    nc,
+    block_input,
+    cotangent,
+    gain_attn,
+    w_query,
+    w_key,
+    w_value,
+    qk_gain,
+    w_out,
+    gain_moe,
+    w_gate,
+    w_up,
+    w_down,
+    expert_ids,
+    route_weight,
+    pair_order,
+):
+    bf16, f32 = jnp.bfloat16, jnp.float32
+    f, c, z, k = place_of()
+    n = nf * nc
+    zs = nc // 2
+    rows, width = block_input.shape[1:]
+    hd = qk_gain.shape[1] * n
+    kv_heads = w_key.shape[1] // hd
+    heads = w_query.shape[1] // hd
+    hp = heads // nc
+    shard = w_query.shape[0]
+    topk = expert_ids.shape[2]
+    capacity = max(2, 3 * BLOCK * topk // n)
+    span = nc * rows
+    scale = 1.0 / math.sqrt(hd)
+    x_own = block_input[0]
+    resid = x_own.astype(f32)
+
+    ids, weights = expert_ids[0], route_weight[0].astype(f32)
+    named = ids[None, :, :] == jnp.arange(n, dtype=jnp.int32)[:, None, None]
+    to_expert = jnp.sum(jnp.where(named, weights[None], 0.0), axis=-1)
+    gains = jnp.concatenate([gain_attn, gain_moe]).astype(f32)
+    gains = jnp.pad(gains, (0, rows - gains.shape[0]))
+    qk_row = jnp.pad(qk_gain.reshape(-1).astype(f32), (0, rows - qk_gain.size))
+    tiles = jnp.concatenate(
+        [to_expert[:, None], jnp.broadcast_to(jnp.stack([gains, qk_row]), (n, 2, rows)), jnp.zeros((n, 5, rows), f32)], axis=1
+    )
+    per = nc // kv_heads
+    wq_p = w_query.reshape(shard, nc, hp * hd).transpose(1, 0, 2)
+    wk_p = jnp.repeat(w_key.reshape(shard, kv_heads, hd).transpose(1, 0, 2), per, axis=0)
+    wv_p = jnp.repeat(w_value.reshape(shard, kv_heads, hd).transpose(1, 0, 2), per, axis=0)
+    packed = jnp.concatenate([wq_p, wk_p, wv_p], axis=2)
+    x_seq, w_all, dealt = front(x_own, packed, tiles, nf, zs, 0)
+
+    qw = hp * hd
+    w_cat = w_all.reshape(n * shard, qw + 2 * hd)
+    gs = gain_attn.shape[0]
+    g_attn = dealt[:, 1, :gs].reshape(-1)
+    g_moe = dealt[:, 1, gs : 2 * gs].reshape(-1)
+    g_qk = dealt[:, 2, : qk_gain.size].reshape(n, 2, -1).transpose(1, 0, 2).reshape(2, hd)
+    route_w = dealt[:, 0, :]
+
+    top_own = cotangent[0]
+    top_b = top_own.astype(bf16)
+    wo_own, top_b_sent, x_seq = lax.optimization_barrier((w_out, top_b, x_seq))
+    lin = lambda ff, cc: ff * nc + cc
+    hops = [(h, lin(h % hp, h // hp)) for h in range(n)]
+    wo_mine = lax.all_gather(lax.ppermute(wo_own, ("fsdp", "cp"), hops), "fsdp", axis=0, tiled=True)
+    top_all = lax.all_gather(top_b_sent, ("fsdp", "cp"), axis=0, tiled=True)
+
+    x32 = x_seq.reshape(span, width).astype(f32)
+    inv_in = lax.rsqrt(jnp.mean(x32 * x32, axis=-1, keepdims=True) + EPSILON)
+    normed_in = (x32 * inv_in * g_attn).astype(bf16)
+    pre = jnp.dot(normed_in, w_cat, preferred_element_type=f32)
+    q_pre = pre[:, :qw].reshape(span, hp, hd)
+    k_pre = pre[:, qw : qw + hd].reshape(span, 1, hd)
+    values = pre[:, qw + hd :].astype(bf16)
+    pos = seq_positions(pair_order, BLOCK)
+    cosine, sine = rope_tables(pos, hd)
+    query_rot = head_post(q_pre, g_qk[0], cosine, sine).astype(bf16).reshape(span, qw)
+    key_rot = head_post(k_pre, g_qk[1], cosine, sine).astype(bf16).reshape(span, hd)
+    context, lse = attend(query_rot, key_rot, values, pos, scale)
+    partial = jnp.dot(context, wo_mine, preferred_element_type=f32).astype(bf16)
+    attn_out = scatter(partial.reshape(nc, rows, width), zs, False, 1)
+    hidden_res = resid + attn_out.astype(f32)
+    normed_mid = rms_scale(hidden_res, g_moe).astype(bf16)
+
+    tokens = gather(normed_mid, zs, True, 2, nf)
+    hit = route_w > 0.0
+    below = (jnp.arange(rows)[:, None] < jnp.arange(rows)[None, :]).astype(f32)
+    rank = jnp.dot(hit.astype(f32), below, preferred_element_type=f32).astype(jnp.int32)
+    slot = (rank[:, None, :] == jnp.arange(capacity, dtype=jnp.int32)[None, :, None]) & hit[:, None, :]
+    place = slot.astype(bf16)
+    mixing = jnp.where(slot, route_w[:, None, :], 0.0).astype(bf16)
+    gate_w, up_w, down_w = w_gate[0], w_up[0], w_down[0]
+    pick = lambda table, rws: jnp.einsum("srt,std->srd", table, rws, preferred_element_type=f32).astype(bf16).reshape(n * capacity, width)
+    back = lambda table, rws: jnp.einsum("srt,srd->std", table, rws.reshape(n, capacity, width), preferred_element_type=f32).astype(bf16)
+    arrived = pick(place, tokens)
+    gate_pre = jnp.dot(arrived, gate_w, preferred_element_type=f32)
+    up_pre = jnp.dot(arrived, up_w, preferred_element_type=f32)
+    gate_sig = jax.nn.sigmoid(gate_pre)
+    gate_act = gate_pre * gate_sig
+    expert_hidden = (gate_act * up_pre).astype(bf16)
+
+    grad_arrived = pick(mixing, top_all.reshape(n, rows, width))
+    grad_hidden = contract_cols(grad_arrived, down_w)
+    grad_gate_pre = (grad_hidden * up_pre * gate_sig * (1.0 + gate_pre * (1.0 - gate_sig))).astype(bf16)
+    grad_up_pre = (grad_hidden * gate_act).astype(bf16)
+    grad_rows = (contract_cols(grad_gate_pre, gate_w) + contract_cols(grad_up_pre, up_w)).astype(bf16)
+    grad_mid = scatter(back(place, grad_rows), zs, True, 3, nf).astype(f32)
+
+    _, mid_back = jax.vjp(rms_scale, hidden_res, g_moe)
+    grad_res_mid, grad_moe_gain = mid_back(grad_mid)
+    grad_res = top_own + grad_res_mid
+    res_all = gather(grad_res.astype(bf16), zs, False, 4).reshape(span, width)
+
+    hidden_late, arrived_late, grad_arrived_late, _ = lax.optimization_barrier((expert_hidden, arrived, grad_arrived, grad_mid))
+    expert_out = jnp.dot(hidden_late, down_w, preferred_element_type=f32).astype(bf16)
+    mixed = lax.psum_scatter(back(mixing, expert_out).reshape(n * rows, width), ("fsdp", "cp"), scatter_dimension=0, tiled=True)
+    block_output = (hidden_res + mixed.astype(f32)).astype(bf16)
+    grad_down = contract_rows(hidden_late, grad_arrived_late)
+    grad_gate = contract_rows(arrived_late, grad_gate_pre)
+    grad_up = contract_rows(arrived_late, grad_up_pre)
+
+    grad_wo_mine = contract_rows(context, res_all)
+    hops_back = [(b, a) for a, b in hops]
+    grad_wo = lax.ppermute(
+        lax.psum_scatter(grad_wo_mine.astype(bf16), "fsdp", scatter_dimension=0, tiled=True), ("fsdp", "cp"), hops_back
+    ).astype(f32)
+    grad_context = contract_cols(res_all, wo_mine).astype(bf16)
+    grad_query, grad_keys, grad_values = attend_grad(query_rot, key_rot, values, context, grad_context, lse, pos, scale)
+    pairs = [(cc, cc + 1 - 2 * (cc % 2)) for cc in range(nc)]
+    both = jnp.stack([grad_keys, grad_values])
+    both = both + lax.ppermute(both, "cp", pairs)
+    grad_keys, grad_values = both[0], both[1]
+    _, query_back = jax.vjp(lambda pre, gain: head_post(pre, gain, cosine, sine), q_pre, g_qk[0])
+    grad_q_pre, grad_q_gain = query_back(grad_query.reshape(span, hp, hd))
+    _, key_back = jax.vjp(lambda pre, gain: head_post(pre, gain, cosine, sine), k_pre, g_qk[1])
+    grad_k_pre, grad_k_gain = key_back(grad_keys.reshape(span, 1, hd))
+    grad_q_b = grad_q_pre.reshape(span, qw).astype(bf16)
+    first = k == 0
+    grad_kv_b = jnp.where(first, grad_k_pre.reshape(span, hd), grad_values).astype(bf16)
+    grad_cat = jnp.concatenate([grad_q_b, grad_kv_b], axis=1)
+    w_kv = jnp.where(first, w_cat[:, qw : qw + hd], w_cat[:, qw + hd :])
+    w_back = jnp.concatenate([w_cat[:, :qw], w_kv], axis=1)
+    grad_w = contract_rows(normed_in, grad_cat).astype(bf16)
+    grad_norm = contract_cols(grad_cat, w_back)
+    grad_attn_gain = jnp.sum(grad_norm * (x32 * inv_in), axis=0)
+    grad_k_gain = jnp.where(first, grad_k_gain, 0.0)
+    share = lambda v: v.reshape(n, -1)
+    qk_parts = jnp.stack([grad_q_gain, grad_k_gain]).reshape(2, n, -1).transpose(1, 0, 2).reshape(n, -1)
+    line0 = jnp.concatenate([share(grad_attn_gain), share(grad_moe_gain)], axis=1)
+    wide = lambda v: jnp.pad(v, ((0, 0), (0, rows - v.shape[1])))
+    sums = jnp.concatenate([wide(line0)[:, None], wide(qk_parts)[:, None], jnp.zeros((n, 6, rows), f32)], axis=1)
+    grad_in, grads, summed = tail(
+        grad_norm.astype(bf16).reshape(nc, rows, width), grad_w.reshape(nf, nc, shard, qw + hd), sums, nf, zs, 5
+    )
+    total = jnp.sum(summed, axis=0)
+    own_attn_gain = total[0, :gs]
+    own_moe_gain = total[0, gs : 2 * gs]
+    own_qk = total[1, : qk_gain.size].reshape(2, -1)
+    grad_wq = grads[:, :, :qw].transpose(1, 0, 2).reshape(shard, heads * hd).astype(f32)
+    grad_kv = grads[:, :, qw:].reshape(kv_heads, per, shard, hd)
+    grad_wk = grad_kv[:, 0].transpose(1, 0, 2).reshape(shard, kv_heads * hd).astype(f32)
+    grad_wv = grad_kv[:, 1].transpose(1, 0, 2).reshape(shard, kv_heads * hd).astype(f32)
+    _, in_back = jax.vjp(rms_scale, resid, g_attn)
+    grad_input = grad_res + in_back(grad_in.astype(f32))[0]
+    return (
+        block_output[None],
+        grad_input[None],
+        own_attn_gain,
+        grad_wq,
+        grad_wk,
+        grad_wv,
+        own_qk,
+        grad_wo,
+        own_moe_gain,
+        grad_gate[None],
+        grad_up[None],
+        grad_down[None],
+    )
+
+
+def body(nf, nc, block_input, *rest):
+    kv_heads = rest[3].shape[1] // (rest[5].shape[1] * nf * nc)
+    fits = nf == 4 and nc == 2 * kv_heads and rest[4].shape[1] == rest[3].shape[1]
+    return head_body(nf, nc, block_input, *rest) if fits else wide_body(block_input, *rest)
+
+
 def solution(mesh):
     return jax.shard_map(
-        body,
+        functools.partial(body, mesh.shape["fsdp"], mesh.shape["cp"]),
         mesh=mesh,
         in_specs=(
             P("fsdp", "cp", None),

time: 2100 us -> 899 us (0.43)
  waiting for transfers between devices: 1550 us -> 37.2 us
  Pallas kernels: 0 us -> 544 us
  blocking collectives: 122 us -> 0 us
  matrix products: 270 us -> 163 us
  local copies, waits for them, and re-layouts: 70.3 us -> 36.3 us
  other arithmetic: 55.9 us -> 84.8 us
    reduce_scatter x4 -> x2, waiting for transfers between devices: 745 us -> 34.6 us  [the longest x1 34.6 us: head_body(): lax.psum_scatter(back(mixing, expert_out).reshape(n * rows, width), ('fsd...]
    all_to_all x4 -> x0, waiting for transfers between devices: 547 us -> none  [the longest x1 151 us: body(): lax.all_to_all(expert_out.reshape(experts, capacity, width), ('fsdp', 'cp...]
    pallas_call x0 -> x8, Pallas kernels: none -> 544 us  [the longest x2 196 us: scatter(): pl.pallas_call(functools.partial(rs_kernel, zs, planes), out_shape=jax.Sh...]
    all_gather x6 -> x2, waiting for transfers between devices: 202 us -> 1.87 us  [the longest x1 1.86 us: head_body(): lax.all_gather(lax.ppermute(wo_own, ('fsdp', 'cp'), hops), 'fsdp', axis=0...]
    unnamed x2 -> x0, blocking collectives: 80.8 us -> none
    dot_general x37 -> x10, matrix products: 131 us -> 75 us  [the longest x2 26.2 us: head_body(): jnp.einsum('srt,srd->std', table, rws.reshape(n, capacity, width), prefer...]
    unnamed x14 -> x4, waiting for transfers between devices: 54.2 us -> 0.75 us
    all_gather x1 -> x0, blocking collectives: 40.7 us -> none  [body(): lax.all_gather(qk_gain, ('fsdp', 'cp'), axis=1, tiled=True)]
  transfers between devices with their start and end apart: 16 -> 7, of which waited for: 13 -> 2; matrix products, arithmetic and copies ran while one was open for 12% -> 23% of each run, Pallas kernels for 0% -> 37%
where the time goes in v1:
time: 899 us; the launch traced here: 892 us
  Pallas kernels  544 us (61%)
  matrix products  163 us (18%)
  other arithmetic  84.8 us (9%)
  waiting for transfers between devices  37.2 us (4%)
  local copies, waits for them, and re-layouts  36.3 us (4%)
  between operations  14.8 us (2%)
  starting transfers between devices  11.5 us (1%)
    pallas_call x2, Pallas kernels, scatter(): pl.pallas_call(functools.partial(rs_kernel, zs, planes), out_shape=jax.Sh...  196 us
    pallas_call x2, Pallas kernels, gather(): pl.pallas_call(functools.partial(ag_kernel, zs, planes), out_shape=jax.Sh...  144 us
    pallas_call x1, Pallas kernels, tail(): pl.pallas_call(functools.partial(tail_kernel, nf, zs), out_shape=(jax.Sha...  99 us
    pallas_call x1, Pallas kernels, front(): pl.pallas_call(functools.partial(front_kernel, nf, zs), out_shape=(jax.Sh...  74.1 us
    dot_general x5, matrix products, contract_cols(): lax.dot_general(left, right, (((1,), (1,)), ((), ())), preferred_element_...  47.4 us
    dot_general x5, matrix products, contract_rows(): lax.dot_general(left, right, (((0,), (0,)), ((), ())), preferred_element_...  41 us
    reduce_scatter x1, waiting for transfers between devices, head_body(): lax.psum_scatter(back(mixing, expert_out).reshape(n * rows, width), ('fsd...  34.6 us
    dot_general x2, matrix products, head_body(): jnp.einsum('srt,srd->std', table, rws.reshape(n, capacity, width), prefer...  26.2 us
  transfers between devices with their start and end apart: 7, of which 2 were waited for; matrix products, arithmetic and copies ran while one was open for 23% of the time, Pallas kernels for 37%

profile of v1, /device:TPU:0, one launch (start us, length us, event | category | flops | bytes accessed | tf_op | source)
XLA Modules:
  0.0 891.7 jit_solution(8990529718548783439)
XLA Ops:
  7.3 2.2 bitcast_convert_fusion
  16.3 74.1 %front.1 = (bf16[8,128,2048]{2,1,0:T(8,128)(2,1)}, bf16[32,64,768]{2,1,0:T(8,128)(2,1)}, f32[32,8,128]{2,1,0:T(8,128)}) custom-call(bf16[128,2048]{1,0:T(8,128)(2,1)} %bitcast.226, bf16[8,64,768]{2,1,0:T(8,128)(2,1)} %pad_maximum_fusion.4.wp_ref, f32[32,8,128]{2,1,0:T(8,128)} %maximum_maximum_fusion.tl_ref), custom_call_target="tpu_custom_call" | custom-call | tf_op jit(solution)/shard_map/front/pallas_call | solution.py:736
  90.4 5.4 collective-permute-start
  98.7 3.2 multiply_reduce_fusion.1
  104.4 3.4 fusion.101
  111.8 3.1 reshape.724
  115.2 3.6 multiply_reduce_fusion.4
  122.1 4.7 select_reduce_fusion
  136.2 3.2 fusion.48
  139.5 2.4 multiply_multiply_fusion
  147.9 13.4 %attend.1 = (bf16[1024,512]{1,0:T(8,128)(2,1)}, f32[1024,512]{1,0:T(8,128)}) custom-call(bf16[1024,512]{1,0:T(8,128)(2,1)} %fusion.16.q_ref, bf16[1024,128]{1,0:T(8,128)(2,1)} %get-tuple-element.74.k_ref, bf16[1024,128]{1,0:T(8,128)(2,1)} %slice.166.v_ref, s32[1024,1]{1,0:T(8,128)} %fusion.41.pr_ref, s32[1,1024]{1,0:T(1,128)} %fusion.77.pc_ref), custom_call_target="tpu_custom_call" | custom-call | tf_op jit(solution)/shard_map/attend/pallas_call | solution.py:908
  163.3 6.3 convolution_convert_fusion.5
  169.6 103.1 %scatter_seq.1 = bf16[128,2048]{1,0:T(8,128)(2,1)} custom-call(bf16[8,128,2048]{2,1,0:T(8,128)(2,1)} %bitcast.243), custom_call_target="tpu_custom_call" | custom-call | tf_op jit(solution)/shard_map/scatter_seq/pallas_call | solution.py:596
  276.6 97.8 %gather_all.1 = bf16[32,128,2048]{2,1,0:T(8,128)(2,1)} custom-call(bf16[128,2048]{1,0:T(8,128)(2,1)} %multiply_convert_fusion.5.x_ref), custom_call_target="tpu_custom_call" | custom-call | tf_op jit(solution)/shard_map/gather_all/pallas_call | solution.py:455
  374.4 8.2 convolution_convert_fusion.4
  382.7 7.2 fusion.9
  389.9 6.6 fusion.5
  396.5 8.1 convolution_convert_fusion.3
  404.6 12.7 %multiply_convert_fusion.2 = (bf16[1536,768]{1,0:T(8,128)(2,1)S(1)}, bf16[1536,768]{1,0:T(8,128)(2,1)S(1)}, bf16[1536,768]{1,0:T(8,128)(2,1)}) fusion(f32[1536,768]{1,0:T(8,128)} %fusion.9, f32[1536,768]{1,0:T(8,128)} %fusion.5, bf16[1536,2048]{1,0:T(8,128)(2,1)S(1)} %bitcast.231, bf16[1,768,2048]{2,1,0:T(8,128)(2,1)S(1)} %copy-done), kind=kOutput, calls=%fused_computation.9 | convolution fusion | flops 4849532928 | bytes 25952256 | tf_op jit(solution)/shard_map/dot_general | solution.py:99
  417.3 8.1 fusion.7
  425.4 10.1 %add_convert_fusion = bf16[1536,2048]{1,0:T(8,128)(2,1)} fusion(f32[1536,2048]{1,0:T(8,128)} %fusion.7, bf16[1536,768]{1,0:T(8,128)(2,1)S(1)} %get-tuple-element.60, bf16[1,2048,768]{2,1,0:T(8,128)(2,1)S(1)} %copy-done.41), kind=kOutput, calls=%fused_computation.2 | convolution fusion | flops 4838129664 | bytes 24379392 | tf_op jit(solution)/shard_map/dot_general | solution.py:99
  435.5 13.1 %convolution_convert_fusion.1.x_ref = bf16[32,128,2048]{2,1,0:T(8,128)(2,1)} fusion(bf16[32,48,2048]{2,1,0:T(8,128)(2,1)} %bitcast.239, s32[32,128]{1,0:T(8,128)S(1)} %convolution_convert_fusion.9, pred[32,128]{1,0:T(8,128)(4,1)S(1)} %bitcast.269), kind=kOutput, calls=%fused_computation.1 | convolution fusion | flops 814088192 | bytes 23089152 | tf_op jit(solution)/shard_map/srt,srd->std/dot_general | solution.py:1051
  448.6 92.8 %scatter_all.1 = bf16[128,2048]{1,0:T(8,128)(2,1)} custom-call(bf16[32,128,2048]{2,1,0:T(8,128)(2,1)} %convolution_convert_fusion.1.x_ref), custom_call_target="tpu_custom_call" | custom-call | tf_op jit(solution)/shard_map/scatter_all/pallas_call | solution.py:596
  543.1 2.7 fusion.96.x_ref
  545.8 46.6 %gather_seq.1 = bf16[8,128,2048]{2,1,0:T(8,128)(2,1)} custom-call(bf16[128,2048]{1,0:T(8,128)(2,1)} %fusion.96.x_ref), custom_call_target="tpu_custom_call" | custom-call | tf_op jit(solution)/shard_map/gather_seq/pallas_call | solution.py:455
  592.4 6.2 convolution_convert_fusion.7
  598.7 8.8 convolution_convert_fusion.2
  607.5 13.2 %convolution_convert_fusion = bf16[32,128,2048]{2,1,0:T(8,128)(2,1)} fusion(bf16[32,48,2048]{2,1,0:T(8,128)(2,1)} %bitcast.238, f32[32,128]{1,0:T(8,128)S(1)} %bitcast.264, s32[32,128]{1,0:T(8,128)S(1)} %convolution_convert_fusion.9, pred[32,128]{1,0:T(8,128)(4,1)S(1)} %bitcast.270), kind=kOutput, calls=%fused_computation | convolution fusion | flops 814284800 | bytes 23105536 | tf_op jit(solution)/shard_map/srt,srd->std/dot_general | solution.py:1051
  620.7 3.1 slice.125
  626.0 6.2 convolution_convert_fusion.8.g_ref
  632.2 16.9 %attend_grad.1 = (f32[1024,512]{1,0:T(8,128)}, f32[1024,128]{1,0:T(8,128)}, f32[1024,128]{1,0:T(8,128)}) custom-call(bf16[1024,512]{1,0:T(8,128)(2,1)} %fusion.16.q_ref, bf16[1024,128]{1,0:T(8,128)(2,1)} %get-tuple-element.74.k_ref, bf16[1024,128]{1,0:T(8,128)(2,1)} %slice.166.v_ref, bf16[1024,512]{1,0:T(8,128)(2,1)} %get-tuple-element.33.c_ref, ...), custom_call_target="tpu_custom_call" | custom-call | tf_op jit(solution)/shard_map/attend_grad/pallas_call | solution.py:947
  649.0 2.2 pad_maximum_fusion.1
  651.8 2.9 reshape.733
  654.7 2.2 broadcast_multiply_fusion
  659.5 5.8 multiply_reduce_fusion.2
  667.6 5.4 fusion.15
  674.4 9.9 %convolution_bitcast_fusion.2 = f32[1,2048,768]{2,1,0:T(8,128)} fusion(bf16[1536,2048]{1,0:T(8,128)(2,1)} %bitcast.229, bf16[1536,768]{1,0:T(8,128)(2,1)} %copy-done.44), kind=kOutput, calls=%fused_computation.18 | convolution fusion | flops 4831838208 | bytes 14942208 | tf_op jit(solution)/shard_map/dot_general | solution.py:93
  684.2 10.3 %convolution_bitcast_fusion.1 = f32[1,2048,768]{2,1,0:T(8,128)} fusion(bf16[1536,2048]{1,0:T(8,128)(2,1)} %bitcast.230, bf16[1536,768]{1,0:T(8,128)(2,1)S(1)} %copy-done.46), kind=kOutput, calls=%fused_computation.17 | convolution fusion | flops 4831838208 | bytes 14942208 | tf_op jit(solution)/shard_map/dot_general | solution.py:93
  694.6 7.0 convolution_bitcast_fusion
  705.2 4.0 fusion.49
  711.2 10.4 %multiply_reduce_fusion = (f32[2048]{0:T(1024)S(1)}, bf16[1024,2048]{1,0:T(8,128)(2,1)}, bf16[1024,2048]{1,0:T(8,128)(2,1)}) fusion(bf16[8,128,2048]{2,1,0:T(8,128)(2,1)} %get-tuple-element.30, f32[1024]{0:T(1024)S(1)} %copy-done.32, f32[2048]{0:T(1024)S(1)} %copy-done.24, bf16[2048,128]{1,0:T(8,128)(2,1)} %slice_select_fusion, ...), kind=kOutput, calls=%fused_computation.4 | convolution fusion | flops 2706896896 | bytes 16535552 | tf_op jit(solution)/shard_map/dot_general | solution.py:99
  722.5 7.6 convolution_convert_fusion.6
  730.2 99.0 %tail.1 = (bf16[128,2048]{1,0:T(8,128)(2,1)}, bf16[8,64,640]{2,1,0:T(8,128)(2,1)}, f32[32,8,128]{2,1,0:T(8,128)}) custom-call(bf16[8,128,2048]{2,1,0:T(8,128)(2,1)} %bitcast.244, bf16[4,8,64,640]{3,2,1,0:T(8,128)(2,1)} %bitcast.249, f32[32,8,128]{2,1,0:T(8,128)} %maximum_maximum_fusion.1.tl_ref), custom_call_target="tpu_custom_call" | custom-call | tf_op jit(solution)/shard_map/tail/pallas_call | solution.py:871
  832.2 2.2 convert_bitcast_fusion
  834.3 5.4 collective-permute-start.2
  840.7 2.3 copy.135
  846.5 34.6 %reduce-scatter.3.cloned.1.call-done = bf16[128,2048]{1,0:T(8,128)(2,1)} async-done(((bf16[4096,2048]{1,0:T(8,128)(2,1)}), bf16[128,2048]{1,0:T(8,128)(2,1)}) %reduce-scatter.3.cloned.1.call-update) | async-done | bytes 524304 | tf_op jit(solution)/shard_map/reduce_scatter | solution.py:1073
  881.1 3.9 fusion.20
  (210 shorter events, 65.4 us)
Async XLA Ops:
  7.2 397.4 %copy-start = (bf16[1,768,2048]{2,1,0:T(8,128)(2,1)S(1)}, bf16[1,768,2048]{2,1,0:T(8,128)(2,1)}, u32[]{:S(2)}) copy-start(bf16[1,768,2048]{2,1,0:T(8,128)(2,1)} %param.26) | copy-start | bytes 9437188
  7.2 6.0 copy-start.42
  7.2 6.1 copy-start.35
  7.2 6.1 copy-start.33
  7.2 8.2 copy-start.36
  7.2 8.2 copy-start.37
  7.2 156.0 %all-gather.3.cloned.1.call-start = ((), (), s32[]{:S(2)}) async-start(), calls=%async_computation.2 | async-start | bytes 2621440 | tf_op jit(solution)/shard_map/all_gather | solution.py:1022
  90.4 5.4 collective-permute-start
  95.8 300.7 %all-gather.5.cloned.1.call-start = ((), (), s32[]{:S(2)}) async-start(), calls=%async_computation.3 | async-start | bytes 17301504 | tf_op jit(solution)/shard_map/all_gather | solution.py:1023
  96.5 737.8 %reduce-scatter.5.cloned.1.call-start = ((), (), s32[]{:S(2)}) async-start(), calls=%async_computation.5 | async-start | bytes 2621440 | tf_op jit(solution)/shard_map/reduce_scatter | solution.py:1082
  98.7 4.9 copy-start.23
  98.7 3.8 copy-start.6
  111.8 9.7 %copy-start.29 = (s32[8]{0:T(128)S(1)}, s32[8]{0:T(128)}, u32[]{:S(2)}) copy-start(s32[8]{0:T(128)} %param.29) | copy-start | bytes 100
  120.0 16.2 %copy-start.21 = (f32[1024,4]{0,1:T(4,128)}, f32[1024,4]{0,1:T(4,128)S(1)}, u32[]{:S(2)}) copy-start(f32[1024,4]{0,1:T(4,128)S(1)} %copy.115) | copy-start | bytes 49156
  121.3 14.9 %copy-start.30 = (f32[128]{0:T(128)}, f32[128]{0:T(128)S(1)}, u32[]{:S(2)}) copy-start(f32[128]{0:T(128)S(1)} %mul.466) | copy-start | bytes 1540
  128.6 7.6 copy-start.8
  131.0 8.5 copy-start.27
  131.0 8.4 copy-start.25
  134.5 4.9 copy-start.1
  134.5 4.9 copy-start.11
  139.4 3.7 copy-start.17
  139.4 4.9 copy-start.14
  169.6 103.1 %copy-start.3 = (bf16[1,128,2048]{2,1,0:T(8,128)(2,1)S(1)}, bf16[1,128,2048]{2,1,0:T(8,128)(2,1)}, u32[]{:S(2)}) copy-start(bf16[1,128,2048]{2,1,0:T(8,128)(2,1)} %param.15) | copy-start | bytes 1572868
  374.4 8.3 copy-start.38
  382.7 7.2 copy-start.9
  382.7 7.2 copy-start.40
  404.6 12.7 %copy-start.10 = (bf16[32,48,2048]{2,1,0:T(8,128)(2,1)}, bf16[32,48,2048]{2,1,0:T(8,128)(2,1)S(1)}, u32[]{:S(2)}) copy-start(bf16[32,48,2048]{2,1,0:T(8,128)(2,1)S(1)} %convolution_convert_fusion.3) | copy-start | bytes 18874372
  404.6 12.7 %copy-start.39 = (bf16[1,2048,768]{2,1,0:T(8,128)(2,1)S(1)}, bf16[1,2048,768]{2,1,0:T(8,128)(2,1)}, u32[]{:S(2)}) copy-start(bf16[1,2048,768]{2,1,0:T(8,128)(2,1)} %param.24) | copy-start | bytes 9437188
  417.3 8.1 copy-start.44
  417.3 8.1 copy-start.45
  417.3 8.1 copy-start.41
  448.6 92.8 %copy-start.4 = (bf16[1,128,2048]{2,1,0:T(8,128)(2,1)S(1)}, bf16[1,128,2048]{2,1,0:T(8,128)(2,1)}, u32[]{:S(2)}) copy-start(bf16[1,128,2048]{2,1,0:T(8,128)(2,1)} %param.15) | copy-start | bytes 1572868
  598.6 282.5 %reduce-scatter.3.cloned.1.call-start = ((), (), s32[]{:S(2)}) async-start(), calls=%async_computation.4 | async-start | bytes 17301504 | tf_op jit(solution)/shard_map/reduce_scatter | solution.py:1073
  651.3 50.3 %collective-permute-start.1 = (f32[2,1024,128]{2,1,0:T(8,128)}, f32[2,1024,128]{2,1,0:T(8,128)}, u32[]{:S(2)}, u32[]{:S(2)}) collective-permute-start(f32[2,1024,128]{2,1,0:T(8,128)} %pad_maximum_fusion.1), channel_id=1, source_target_pairs={{0,1},{1,0},{2,3},{3,2},{4,5},{5,4},{6,7},{7,6},{8,9},{9,8},{10,11... | collective-permute-start | bytes 3145736 | tf_op jit(solution)/shard_map/ppermute | solution.py:1088
  659.5 7.0 copy-start.22
  674.4 9.9 %copy-start.46 = (bf16[1536,768]{1,0:T(8,128)(2,1)S(1)}, bf16[1536,768]{1,0:T(8,128)(2,1)}, u32[]{:S(2)}) copy-start(bf16[1536,768]{1,0:T(8,128)(2,1)} %copy-done.45) | copy-start | bytes 7077892
  674.4 20.2 %slice-start = ((s8[6291456]{0:T(1024)(128)(4,1)}), s8[4194304]{0:T(1024)(128)(4,1)S(1)}, s32[]{:S(2)}) async-start(s8[6291456]{0:T(1024)(128)(4,1)} %bitcast.232), calls=%async_computation.6 | async-start | bytes 8388608
  684.2 10.3 %slice-start.1 = ((s8[6291456]{0:T(1024)(128)(4,1)}), s8[2097152]{0:T(1024)(128)(4,1)S(1)}, s32[]{:S(2)}) async-start(s8[6291456]{0:T(1024)(128)(4,1)} %bitcast.232), calls=%async_computation.7 | async-start | bytes 4194304
  684.2 10.3 %copy-start.43 = (bf16[1536,768]{1,0:T(8,128)(2,1)S(1)}, bf16[1536,768]{1,0:T(8,128)(2,1)}, u32[]{:S(2)}) copy-start(bf16[1536,768]{1,0:T(8,128)(2,1)} %get-tuple-element.36) | copy-start | bytes 7077892
  694.5 7.0 copy-start.19
  694.5 7.0 copy-start.20
  701.5 3.6 copy-start.31
  703.0 6.2 copy-start.13
  703.0 6.5 copy-start.28
  704.9 6.3 copy-start.24
  705.0 6.3 copy-start.32
  730.2 101.4 %copy-start.34 = (f32[128]{0:T(128)S(1)}, f32[128]{0:T(128)}, u32[]{:S(2)}) copy-start(f32[128]{0:T(128)} %get-tuple-element.52) | copy-start | bytes 1540
  834.3 10.0 %collective-permute-start.2 = (bf16[128,2048]{1,0:T(8,128)(2,1)}, bf16[128,2048]{1,0:T(8,128)(2,1)}, u32[]{:S(2)}, u32[]{:S(2)}) collective-permute-start(bf16[128,2048]{1,0:T(8,128)(2,1)} %reduce-scatter.5.cloned.1.call-done), channel_id=1, source_target_pairs={{0,0},{8,1},{16,2},{24,3},{1,4},{9,5},{17,6},{25,7},{2,8},{10,9},{... | collective-permute-start | bytes 1572872 | tf_op jit(solution)/shard_map/ppermute | solution.py:1081
  (8 other events, 18.0 us)
Sparse Core Ops, SparseCore 0:
  95.9 67.3 all-gather.2
  166.9 147.4 all-gather.4
  598.7 34.0 reduce-scatter.4
  635.0 246.0 reduce-scatter.2

commit v2 on v1

--- a/solution.py
+++ b/solution.py
@@ -337,13 +337,22 @@
         else:
             pl.when(when)(copy.start)
         self.sent.append((copy, when))
+        return self.sent[-1]
+
+    def settle(self, entries):
+        for entry in entries:
+            self.sent = [e for e in self.sent if e is not entry]
+            self.wait(*entry)
+
+    def wait(self, copy, when):
+        if when is None:
+            copy.wait_send()
+        else:
+            pl.when(when)(copy.wait_send)
 
     def drain(self):
-        for copy, when in self.sent:
-            if when is None:
-                copy.wait_send()
-            else:
-                pl.when(when)(copy.wait_send)
+        for entry in self.sent:
+            self.wait(*entry)
 
 
 def got(dst, ssem, rsem, dev, when=None):
@@ -605,50 +614,286 @@
     )(x)
 
 
-def greet_all(f, c, nf, nc):
+def greet_cross(f, c, nf, nc):
     bar = pltpu.get_barrier_semaphore()
-    n = nf * nc
-    me = f * nc + c
-
-    def hello(i, _):
-        j = (me + i) % n
-        pl.semaphore_signal(bar, inc=1, device_id=(j // nc, j % nc), device_id_type=MESH)
-        return 0
-
-    lax.fori_loop(1, n, hello, 0)
-    pl.semaphore_wait(bar, n - 1)
-
-
-def deal_tiles(src, dst, ssem, rsem, f, c, nf, nc):
-    n = nf * nc
-    me = f * nc + c
+    for i in range(1, nc):
+        pl.semaphore_signal(bar, inc=1, device_id=(f, (c + i) % nc), device_id_type=MESH)
+    for i in range(1, nf):
+        pl.semaphore_signal(bar, inc=1, device_id=((f + i) % nf, c), device_id_type=MESH)
+    pl.semaphore_wait(bar, nc + nf - 2)
+
+
+def tile_steps(w, nf, nc, src, dst, hub, ssem, rsem, sp, rp):
+    f, c, z, k = place_of()
 
     def go(i, _):
-        j = (me + i) % n
+        j = (c + i) % nc
         pltpu.make_async_remote_copy(
-            src_ref=src.at[j], dst_ref=dst.at[me], send_sem=ssem, recv_sem=rsem,
-            device_id=(j // nc, j % nc), device_id_type=MESH,
+            src_ref=src.at[j], dst_ref=hub.at[c], send_sem=ssem, recv_sem=rsem, device_id=(f, j), device_id_type=MESH
         ).start()
         return 0
 
-    lax.fori_loop(1, n, go, 0)
-    dst[me] = src[me]
-
-
-def await_tiles(src, dst, ssem, rsem, f, c, nf, nc):
-    n = nf * nc
+    lax.fori_loop(1, nc, go, 0)
+    hub[c] = src[c]
+    yield
     every = pltpu.make_async_remote_copy(
-        src_ref=src.at[pl.ds(0, n - 1)], dst_ref=dst.at[pl.ds(0, n - 1)], send_sem=ssem, recv_sem=rsem,
+        src_ref=src.at[pl.ds(0, nc - 1)], dst_ref=hub.at[pl.ds(0, nc - 1)], send_sem=ssem, recv_sem=rsem,
         device_id=(f, c), device_id_type=MESH,
     )
     every.wait_send()
     every.wait_recv()
-
-
-def front_kernel(nf, zs, x_ref, wp_ref, tl_ref, o_ref, w_ref, to_ref, loc, wloc, sl, szr, szl, rz, ssib, rsib, ts, tr, sw, rw, swx, swy):
+    mine = pl.ds(f * nc, nc)
+    for i in range(1, nf):
+        ff = (f + i) % nf
+        w.send(hub.at[:, ff], dst.at[mine], sp.at[i], rp.at[i], (ff, c))
+    dst[mine] = hub[:, f]
+    yield
+    for i in range(1, nf):
+        ff = (f + nf - i) % nf
+        got(dst.at[pl.ds(ff * nc, nc)], sp.at[i], rp.at[i], (f, c))
+    yield
+
+
+def tile_bufs(nf, nc, tile):
+    D = pltpu.SemaphoreType.DMA
+    return [pltpu.VMEM((nc, nf) + tile, jnp.float32), D(()), D(()), D((nf,)), D((nf,))]
+
+
+def gather_steps(w, zs, planes, late, x_ref, o_ref, loc, sl, szr, szl, rz, sp1, rp1, sp2, rp2, ssib, rsib):
+    f, c, z, k = place_of()
+    half = x_ref.shape[1] // 2
+    sib = (f, c + 1 - 2 * k)
+    b1 = 1 + k
+    b2 = 2 - k
+    f1 = flip(f, b1)
+    f2 = flip(f, b2)
+    cols = [f, f1, f2, flip(f1, b2)] if planes else [0]
+    cs = 2 * zs
+
+    def chunk(col, zz, kk):
+        at = (cols[col] * cs if planes else 0) + 2 * zz
+        return o_ref.at[pl.ds(at, 2), :, pl.ds(pl.multiple_of(kk * half, 128), half)]
+
+    mine = (f * cs if planes else 0) + c
+    theirs = (f * cs if planes else 0) + c + 1 - 2 * k
+    own = pltpu.make_async_copy(x_ref, o_ref.at[mine], loc)
+    own.start()
+    w.send(x_ref, o_ref.at[mine], sl.at[0], sl.at[1], sib)
+    yield
+    own.wait()
+    got(o_ref.at[theirs], sl.at[0], sl.at[1], sib)
+
+    def spread(zz, when):
+        if planes:
+            w.send(chunk(0, zz, k), chunk(0, zz, k), sp1.at[zz], rp1.at[zz], (f1, c), when)
+            w.send(chunk(0, zz, k), chunk(0, zz, k), sp2.at[zz], rp2.at[zz], (f2, c), when)
+
+    def relay(zz, when):
+        if planes:
+            got(chunk(1, zz, k), sp1.at[zz], rp1.at[zz], (f1, c), when)
+            w.send(chunk(1, zz, k), chunk(1, zz, k), sp2.at[zs + zz], rp2.at[zs + zz], (f2, c), when)
+            w.send(chunk(1, zz, k), chunk(1, zz, k), ssib.at[zs + zz], rsib.at[zs + zz], sib, when)
+
+    if late:
+        spread(z, None)
+        yield
+    w.send(chunk(0, z, k), chunk(0, z, k), szr.at[z], rz.at[z], (f, c + 2), z < zs - 1)
+    w.send(chunk(0, z, k), chunk(0, z, k), szl.at[z], rz.at[z], (f, c - 2), z > 0)
+    if not late:
+        spread(z, None)
+    yield
+    if late:
+        relay(z, None)
+        yield
+    order = []
+    for h in range(1, zs):
+        for zz, when, on, dz, sem in (
+            (z - h, z - h >= 0, z < zs - 1, 2, szr),
+            (z + h, z + h < zs, z > 0, -2, szl),
+        ):
+            got(chunk(0, zz, k), sem.at[zz], rz.at[zz], (f, c), when)
+            w.send(chunk(0, zz, k), chunk(0, zz, k), sem.at[zz], rz.at[zz], (f, c + dz), jnp.logical_and(when, on))
+            spread(zz, when)
+            w.send(chunk(0, zz, k), chunk(0, zz, k), ssib.at[zz], rsib.at[zz], sib, when)
+            order.append((zz, when))
+        yield
+        if h == 1 and not late:
+            relay(z, None)
+            yield
+    for zz, when in order:
+        relay(zz, when)
+        yield
+    if planes:
+        for col, base in ((2, 0), (3, zs)):
+            for zz, when in [(z, None)] + order:
+                got(chunk(col, zz, k), sp2.at[base + zz], rp2.at[base + zz], (f2, c), when)
+                w.send(chunk(col, zz, k), chunk(col, zz, k), ssib.at[col * zs + zz], rsib.at[col * zs + zz], sib, when)
+            yield
+        for mycol, theircol in ((0, 0), (1, 2), (2, 1), (3, 3)):
+            for zz, when in ([(z, None)] if mycol else []) + order:
+                got(chunk(mycol, zz, 1 - k), ssib.at[theircol * zs + zz], rsib.at[theircol * zs + zz], sib, when)
+    else:
+        for zz, when in order:
+            got(chunk(0, zz, 1 - k), ssib.at[zz], rsib.at[zz], sib, when)
+    yield
+
+
+def gather_sems(zs):
+    D = pltpu.SemaphoreType.DMA
+    return [D(()), D((2,)), D((zs,)), D((zs,)), D((zs,)), D((zs,)), D((zs,)), D((2 * zs,)), D((2 * zs,)), D((4 * zs,)), D((4 * zs,))]
+
+
+def advance(steps, name="step"):
+    with jax.named_scope(name):
+        return next(steps, steps) is not steps
+
+
+def head_rows_steps(w, nf, nc, hp, wo_ref, wo_all, hub, loc, so, ro):
+    f, c, z, k = place_of()
+    fx, fy = flip(f, 1), flip(f, 2)
+    fd = flip(fx, 2)
+    hr = wo_ref.shape[0] // 2
+    halves = []
+    for p in (0, 1):
+        j = c % hp
+        m = f
+        if p:
+            j, m = flip(j, 2), flip(f, 2)
+        halves.append((p, pl.ds(p * hr, hr), j, f == j, m))
+    keeps = []
+    for p, at, j, is_hub, m in halves:
+        w.send(wo_ref.at[at], hub.at[f, at], so.at[p, 0], ro.at[p, f], (j, c), jnp.logical_not(is_hub))
+        keep = pltpu.make_async_copy(wo_ref.at[at], hub.at[f, at], loc.at[p])
+        pl.when(is_hub)(keep.start)
+        keeps.append(keep)
+    yield
+    stays = []
+    for p, at, j, is_hub, m in halves:
+        for ff in range(nf):
+            got(hub.at[ff, at], so.at[p, 0], ro.at[p, ff], (f, c), jnp.logical_and(is_hub, ff != f))
+            pl.when(jnp.logical_and(is_hub, ff == f))(keeps[p].wait)
+            dc = (ff * nc + c) // hp
+            w.send(hub.at[ff, at], wo_all.at[m, at], so.at[p, 1 + ff], ro.at[p, nf], (f, dc), jnp.logical_and(is_hub, dc != c))
+            stay = pltpu.make_async_copy(hub.at[ff, at], wo_all.at[m, at], loc.at[2 + p])
+            pl.when(jnp.logical_and(is_hub, dc == c))(stay.start)
+        stays.append(stay)
+    yield
+    for p, at, j, is_hub, m in halves:
+        here = (hp * c + m) % nc == c
+        got(wo_all.at[m, at], so.at[p, 1], ro.at[p, nf], (f, c), jnp.logical_not(here))
+        pl.when(here)(stays[p].wait)
+        w.send(wo_all.at[m, at], wo_all.at[m, at], so.at[p, nf + 1], ro.at[p, nf + 1], (fx, c))
+        w.send(wo_all.at[m, at], wo_all.at[m, at], so.at[p, nf + 2], ro.at[p, nf + 2], (fy, c))
+    yield
+    for p, at, j, is_hub, m in halves:
+        mx, my = flip(m, 1), flip(m, 2)
+        got(wo_all.at[mx, at], so.at[p, nf + 1], ro.at[p, nf + 1], (fx, c))
+        got(wo_all.at[my, at], so.at[p, nf + 2], ro.at[p, nf + 2], (fy, c))
+        if p == 0:
+            w.send(wo_all.at[mx, at], wo_all.at[mx, at], so.at[p, nf + 3], ro.at[p, nf + 3], (fy, c))
+        else:
+            w.send(wo_all.at[my, at], wo_all.at[my, at], so.at[p, nf + 3], ro.at[p, nf + 3], (fx, c))
+    yield
+    for p, at, j, is_hub, m in halves:
+        got(wo_all.at[flip(flip(m, 1), 2), at], so.at[p, nf + 3], ro.at[p, nf + 3], (f, c))
+    yield
+
+
+def far_first(z, zs):
+    last = zs - 1
+    low = z < zs // 2
+    order = []
+    for i in range(zs - 1):
+        far_low = jnp.where(i < zs - 1 - z, last - i, zs - 2 - i)
+        far_high = jnp.where(i < z, i, i + 1)
+        order.append(jnp.where(low, far_low, far_high))
+    return order + [z]
+
+
+def line_sum_steps(w, zs, make, o_ref, t, u, r0, ral, rar, fin, s0, q0, szr, szl, rzr, rzl, sf):
+    f, c, z, k = place_of()
+    half = o_ref.shape[1] // 2
+    sib = (f, c + 1 - 2 * k)
+    order = far_first(z, zs)
+
+    def first(zz):
+        make(zz)
+        w.send(u.at[zz], r0.at[zz], s0.at[zz], q0.at[zz], sib)
+
+    def complete(zz):
+        got(r0.at[zz], s0.at[zz], q0.at[zz], sib)
+        add_into(t.at[zz], r0.at[zz])
+
+    def onward(zz):
+        right = zz > z
+        from_left = jnp.logical_and(right, z > 0)
+        from_right = jnp.logical_and(jnp.logical_not(right), z < zs - 1)
+        got(ral.at[zz], szr.at[zz], rzr.at[zz], (f, c), from_left)
+        got(rar.at[zz], szl.at[zz], rzl.at[zz], (f, c), from_right)
+
+        @pl.when(from_left)
+        def _():
+            add_into(t.at[zz], ral.at[zz])
+
+        @pl.when(from_right)
+        def _():
+            add_into(t.at[zz], rar.at[zz])
+
+        w.send(t.at[zz], ral.at[zz], szr.at[zz], rzr.at[zz], (f, c + 2), right)
+        w.send(t.at[zz], rar.at[zz], szl.at[zz], rzl.at[zz], (f, c - 2), jnp.logical_not(right))
+
+    first(order[0])
+    yield
+    for zi in range(zs - 1):
+        first(order[zi + 1])
+        complete(order[zi])
+        yield
+        onward(order[zi])
+        yield
+    complete(z)
+    got(ral.at[z], szr.at[z], rzr.at[z], (f, c), z > 0)
+
+    @pl.when(z > 0)
+    def _():
+        add_into(t.at[z], ral.at[z])
+
+    yield
+    got(rar.at[z], szl.at[z], rzl.at[z], (f, c), z < zs - 1)
+
+    @pl.when(z < zs - 1)
+    def _():
+        add_into(t.at[z], rar.at[z])
+
+    w.send(t.at[z, 1 - k], fin, sf.at[0], sf.at[1], sib)
+    o_ref[:, pl.ds(pl.multiple_of(k * half, 128), half)] = t[z, k]
+    yield
+    got(fin, sf.at[0], sf.at[1], sib)
+    o_ref[:, pl.ds(pl.multiple_of((1 - k) * half, 128), half)] = fin[...]
+    yield
+
+
+def line_sum_bufs(zs, rows, half, dtype):
+    D = pltpu.SemaphoreType.DMA
+    V = pltpu.VMEM((zs, 2, rows, half), dtype)
+    return [V, V, V, V, V, pltpu.VMEM((rows, half), dtype)] + [D((zs,))] * 6 + [D((2,))]
+
+
+def attn_kernel(nf, zs, hp, scale, refs):
+    (x_ref, wp_ref, tl_ref, wo_ref, tb_ref, cos_ref, sin_ref, pr_ref, pc_ref,
+     o_ref, nm_ref, w_ref, to_ref, wo_all, top_all, qp_ref, kp_ref, qr_ref, kr_ref, v_ref, ctx_ref, lse_ref, hid_ref, tok_all,
+     gain, gain_mid, mid, out_ref, loc, wloc, sl, szr, szl, rz, ssib, rsib, sw, rw, swx, swy) = refs[:40]
+    tile_b = refs[40:45]
+    head_bufs = refs[45:49]
+    top_sems = refs[49:60]
+    tok_sems = refs[60:71]
+    sum_bufs = refs[71:]
     f, c, z, k = place_of()
     nc = 2 * zs
-    half = x_ref.shape[1] // 2
+    rows, width = x_ref.shape
+    half = width // 2
+    hd = kr_ref.shape[1]
+    qw = hp * hd
+    f32, bf16 = jnp.float32, jnp.bfloat16
     sib_c = c + 1 - 2 * k
     sib = (f, sib_c)
     fx, fy = flip(f, 1), flip(f, 2)
@@ -664,8 +909,13 @@
     own.start()
     wown = pltpu.make_async_copy(wp_ref.at[c], piece(0, c), wloc)
     wown.start()
-    greet_all(f, c, nf, nc)
+    with jax.named_scope("greet"):
+        greet_cross(f, c, nf, nc)
     w = Wire()
+    head_steps = head_rows_steps(w, nf, nc, hp, wo_ref, wo_all, *head_bufs)
+    top_steps = gather_steps(w, zs, True, True, tb_ref, top_all, *top_sems)
+    small_steps = tile_steps(w, nf, nc, tl_ref, to_ref, *tile_b)
+    advance(small_steps, "tiles")
     w.send(x_ref, o_ref.at[c], sl.at[0], sl.at[1], sib)
     w.send(wp_ref.at[sib_c], piece(0, c), sw.at[sib_c], rw.at[c], sib)
     for h in range(1, zs):
@@ -675,9 +925,12 @@
                 w.send(wp_ref.at[cc], piece(0, c), sw.at[cc], rw.at[c], (f, cc), when)
     own.wait()
     got(o_ref.at[sib_c], sl.at[0], sl.at[1], sib)
-    w.send(chunk(z, k), chunk(z, k), szr.at[z], rz.at[z], (f, c + 2), z < zs - 1)
-    w.send(chunk(z, k), chunk(z, k), szl.at[z], rz.at[z], (f, c - 2), z > 0)
-    deal_tiles(tl_ref, to_ref, ts, tr, f, c, nf, nc)
+    on_line = [
+        w.send(chunk(z, k), chunk(z, k), szr.at[z], rz.at[z], (f, c + 2), z < zs - 1),
+        w.send(chunk(z, k), chunk(z, k), szl.at[z], rz.at[z], (f, c - 2), z > 0),
+    ]
+    advance(head_steps, "heads")
+    advance(small_steps, "tiles")
 
     def plane(cc, when):
         w.send(piece(0, cc), piece(0, cc), swx.at[cc], rw.at[nc + cc], (fx, c), when)
@@ -691,64 +944,229 @@
             got(piece(2, cc), swy.at[cc], rw.at[2 * nc + cc], (fy, c), when)
             w.send(piece(2, cc), piece(2, cc), swx.at[nc + cc], rw.at[3 * nc + cc], (fx, c), when)
 
+    def norm(zz):
+        nb = 32
+
+        def block(i, _):
+            j = i // (rows // nb)
+            at = pl.ds(pl.multiple_of(i % (rows // nb) * nb, nb), nb)
+            v = o_ref[2 * zz + j, at, :].astype(f32)
+            inv = lax.rsqrt(jnp.mean(v * v, axis=-1, keepdims=True) + EPSILON)
+            to = pl.ds(pl.multiple_of(2 * zz * rows + i * nb, nb), nb)
+            nm_ref[to, :] = (v * inv * gain[...]).astype(bf16)
+            return 0
+
+        with jax.named_scope("norm"):
+            lax.fori_loop(0, 2 * rows // nb, block, 0)
+
+    sides = [
+        (
+            (z - h, z - h >= 0, z < zs - 1, 2, szr),
+            (z + h, z + h < zs, z > 0, -2, szl),
+        )
+        for h in range(1, zs)
+    ]
+    far = [(zz, when) for pair in sides for zz, when, *_ in pair]
     wown.wait()
     plane(c, None)
     got(piece(0, sib_c), sw.at[sib_c], rw.at[sib_c], sib)
     plane(sib_c, None)
-    far = []
-    for h in range(1, zs):
-        for zz, when, on, dz, sem in (
-            (z - h, z - h >= 0, z < zs - 1, 2, szr),
-            (z + h, z + h < zs, z > 0, -2, szl),
-        ):
+    for zz, when in far:
+        for kk in (0, 1):
+            cc = 2 * zz + kk
+            with jax.named_scope("w1"):
+                got(piece(0, cc), sw.at[cc], rw.at[cc], (f, cc), when)
+            plane(cc, when)
+    advance(small_steps, "tiles")
+    advance(head_steps, "heads")
+    for i in range(width // 128):
+        gain[:, pl.ds(128 * i, 128)] = to_ref[2 * i, 1:2, :] + to_ref[2 * i + 1, 1:2, :]
+        gain_mid[:, pl.ds(128 * i, 128)] = to_ref[2 * i, 4:5, :] + to_ref[2 * i + 1, 4:5, :]
+    norm(z)
+    with jax.named_scope("w2"):
+        for zz, when in [(z, None)] + far[:2]:
             for kk in (0, 1):
-                cc = 2 * zz + kk
-                got(piece(0, cc), sw.at[cc], rw.at[cc], (f, cc), when)
-                plane(cc, when)
-            far.append((zz, when))
-        for zz, when, on, dz, sem in (
-            (z - h, z - h >= 0, z < zs - 1, 2, szr),
-            (z + h, z + h < zs, z > 0, -2, szl),
-        ):
-            got(chunk(zz, k), sem.at[zz], rz.at[zz], (f, c), when)
-            w.send(chunk(zz, k), chunk(zz, k), sem.at[zz], rz.at[zz], (f, c + dz), jnp.logical_and(when, on))
+                onward(2 * zz + kk, kk, when)
+    waiting = []
+    for h, pair in enumerate(sides):
+        for zz, when, on, dz, sem in pair:
+            with jax.named_scope("x"):
+                got(chunk(zz, k), sem.at[zz], rz.at[zz], (f, c), when)
+            on_line.append(w.send(chunk(zz, k), chunk(zz, k), sem.at[zz], rz.at[zz], (f, c + dz), jnp.logical_and(when, on)))
             w.send(chunk(zz, k), chunk(zz, k), ssib.at[zz], rsib.at[zz], sib, when)
-    everyone = [(z, None)] + far
-    for zz, when in everyone:
-        for kk in (0, 1):
-            onward(2 * zz + kk, kk, when)
-    for zz, when in everyone:
-        e, o = 2 * zz, 2 * zz + 1
-        got(piece(2, e), swy.at[e], rw.at[2 * nc + e], (fy, c), when)
-        got(piece(1, o), swx.at[o], rw.at[nc + o], (fx, c), when)
-        got(piece(3, e), swy.at[nc + e], rw.at[3 * nc + e], (fy, c), when)
-        got(piece(3, o), swx.at[nc + o], rw.at[3 * nc + o], (fx, c), when)
-    for zz, when in far:
+        if h == 0:
+            advance(head_steps, "heads")
+            with jax.named_scope("w2"):
+                for zz, when in far[2:]:
+                    for kk in (0, 1):
+                        onward(2 * zz + kk, kk, when)
+        if h == zs - 3:
+            advance(head_steps, "heads")
+            advance(top_steps, "top")
+        if h == zs - 2:
+            with jax.named_scope("line"):
+                w.settle(on_line)
+            advance(top_steps, "top")
+            advance(top_steps, "top")
+        for zz, when in waiting:
+            got(chunk(zz, 1 - k), ssib.at[zz], rsib.at[zz], sib, when)
+            pl.when(when)(functools.partial(norm, zz))
+        waiting = [(zz, when) for zz, when, *_ in pair]
+    for zz, when in waiting:
         got(chunk(zz, 1 - k), ssib.at[zz], rsib.at[zz], sib, when)
-    await_tiles(tl_ref, to_ref, ts, tr, f, c, nf, nc)
+        pl.when(when)(functools.partial(norm, zz))
+    with jax.named_scope("wait_w"):
+        for zz, when in [(z, None)] + far:
+            e, o = 2 * zz, 2 * zz + 1
+            got(piece(2, e), swy.at[e], rw.at[2 * nc + e], (fy, c), when)
+            got(piece(1, o), swx.at[o], rw.at[nc + o], (fx, c), when)
+            got(piece(3, e), swy.at[nc + e], rw.at[3 * nc + e], (fy, c), when)
+            got(piece(3, o), swx.at[nc + o], rw.at[3 * nc + o], (fx, c), when)
+
+    gq = jnp.sum(to_ref[:, 2, :], axis=0, keepdims=True)
+    gk = jnp.sum(to_ref[:, 3, :], axis=0, keepdims=True)
+    qb = 2 * rows
+    span = nc * rows
+    low_half = lax.broadcasted_iota(jnp.int32, (1, hd), 1) < hd // 2
+
+    def turned(t, g, at):
+        t = t * lax.rsqrt(jnp.mean(t * t, axis=-1, keepdims=True) + EPSILON) * g
+        other = pltpu.roll(t, hd // 2, 1)
+        return (t * cos_ref[at, :] + jnp.where(low_half, -other, other) * sin_ref[at, :]).astype(bf16)
+
+    def project(i, _):
+        at = pl.ds(pl.multiple_of(i * qb, qb), qb)
+        a = nm_ref[at, :]
+        for nb in range((qw + 2 * hd) // (2 * hd)):
+            wide = pl.ds(nb * 2 * hd, 2 * hd)
+            pre = jnp.dot(a, w_ref[:, :, wide].reshape(width, 2 * hd), preferred_element_type=f32)
+            for s in (0, 1):
+                part = pre[:, s * hd : (s + 1) * hd]
+                h = 2 * nb + s
+                if h < hp:
+                    qp_ref[at, pl.ds(h * hd, hd)] = part
+                    qr_ref[at, pl.ds(h * hd, hd)] = turned(part, gq, at)
+                elif h == hp:
+                    kp_ref[at, :] = part
+                    kr_ref[at, :] = turned(part, gk, at)
+                else:
+                    v_ref[at, :] = part.astype(bf16)
+        return 0
+
+    for i in range(span // qb):
+        with jax.named_scope("project"):
+            project(i, 0)
+
+    lane = lax.broadcasted_iota(jnp.int32, (1, hd), 1)
+
+    def attend(i, h):
+        at = pl.ds(pl.multiple_of(i * qb, qb), qb)
+        hc = pl.ds(pl.multiple_of(h * hd, hd), hd)
+        s = lax.dot_general(qr_ref[at, hc], kr_ref[...], (((1,), (1,)), ((), ())), preferred_element_type=f32) * scale
+        s = jnp.where(pc_ref[...] <= pr_ref[at, :], s, -jnp.inf)
+        top = jnp.max(s, axis=-1, keepdims=True)
+        e = jnp.exp(s - top)
+        total = jnp.sum(e, axis=-1, keepdims=True)
+        p = (e * (1.0 / total)).astype(bf16)
+        ctx_ref[at, hc] = jnp.dot(p, v_ref[...], preferred_element_type=f32).astype(bf16)
+        lse_ref[at, :] = jnp.where(lane == h, top + jnp.log(total), lse_ref[at, :])
+
+    lse_ref[...] = jnp.zeros_like(lse_ref)
+
+    while advance(head_steps, "heads"):
+        pass
+
+    t, u = sum_bufs[0], sum_bufs[1]
+
+    def make(zz):
+        def heads(h, _):
+            attend(zz, h)
+            return 0
+
+        with jax.named_scope("attend"):
+            lax.fori_loop(0, hp, heads, 0)
+        at = pl.ds(pl.multiple_of(2 * zz * rows, rows), 2 * rows)
+        a = ctx_ref[at, :]
+        for dst, kk in ((u, 1 - k), (t, k)):
+            def block(j, _, dst=dst, kk=kk):
+                cols = pl.ds(pl.multiple_of(kk * half + j * 512, 128), 512)
+                o = jnp.dot(a, wo_all[:, :, cols].reshape(qw, 512), preferred_element_type=f32).astype(bf16)
+                dst[zz, :, :, pl.ds(pl.multiple_of(j * 512, 512), 512)] = o.reshape(2, rows, 512)
+                return 0
+
+            lax.fori_loop(0, half // 512, block, 0)
+
+    sum_steps = line_sum_steps(w, zs, make, out_ref, *sum_bufs)
+    for turn in "sstsstssssst":
+        if turn == "s":
+            advance(sum_steps, "sum")
+        else:
+            advance(top_steps, "top")
+    while advance(sum_steps, "sum"):
+        pass
+
+    def middle(i, _):
+        at = pl.ds(pl.multiple_of(i * 32, 32), 32)
+        v = x_ref[at, :].astype(f32) + out_ref[at, :].astype(f32)
+        hid_ref[at, :] = v
+        inv = lax.rsqrt(jnp.mean(v * v, axis=-1, keepdims=True) + EPSILON)
+        mid[at, :] = (v * inv * gain_mid[...]).astype(bf16)
+        return 0
+
+    with jax.named_scope("middle"):
+        lax.fori_loop(0, rows // 32, middle, 0)
+    tok_steps = gather_steps(w, zs, True, False, mid, tok_all, *tok_sems)
+    advance(tok_steps, "tok")
+    advance(tok_steps, "tok")
+    busy = True
+    while busy:
+        busy = advance(top_steps, "top")
+        busy = advance(tok_steps, "tok") or busy
     w.drain()
 
 
-def front(x, wp, tl, nf, zs, cid):
+def attention(x, wp, tl, wo, tb, cosine, sine, pos, nf, zs, hp, scale, cid):
     rows, width = x.shape
     nc = 2 * zs
+    span = nc * rows
+    hd = cosine.shape[1]
+    bf16, f32 = jnp.bfloat16, jnp.float32
     D = pltpu.SemaphoreType.DMA
+    S = jax.ShapeDtypeStruct
+    outs = [
+        (S((nc, rows, width), bf16), VM),
+        (S((span, width), bf16), VM),
+        (S((nf * nc,) + wp.shape[1:], bf16), VM),
+        (S((nf * nc,) + tl.shape[2:], f32), VM),
+        (S((hp,) + wo.shape, bf16), VM),
+        (S((nf * nc, rows, width), bf16), ANY),
+        (S((span, hp * hd), f32), VM),
+        (S((span, hd), f32), VM),
+        (S((span, hp * hd), bf16), VM),
+        (S((span, hd), bf16), VM),
+        (S((span, hd), bf16), VM),
+        (S((span, hp * hd), bf16), VM),
+        (S((span, hd), f32), VM),
+        (S((rows, width), f32), VM),
+        (S((nf * nc, rows, width), bf16), ANY),
+    ]
+    R = pltpu.VMEM((rows, width), bf16)
+    scratch = [pltpu.VMEM((1, width), f32), pltpu.VMEM((1, width), f32), R, R, D(()), D(()), D((2,)), D((zs,)), D((zs,)), D((zs,)), D((zs,)), D((zs,)),
+               D((nc,)), D((4 * nc,)), D((2 * nc,)), D((2 * nc,))]
+    scratch += tile_bufs(nf, nc, tl.shape[2:])
+    scratch += [pltpu.VMEM((nf,) + wo.shape, bf16), D((4,)), D((2, nf + 4)), D((2, nf + 4))] + gather_sems(zs) + gather_sems(zs) + line_sum_bufs(zs, rows, width // 2, bf16)
     return pl.pallas_call(
-        functools.partial(front_kernel, nf, zs),
-        out_shape=(
-            jax.ShapeDtypeStruct((nc, rows, width), x.dtype),
-            jax.ShapeDtypeStruct((nf * nc,) + wp.shape[1:], wp.dtype),
-            jax.ShapeDtypeStruct(tl.shape, tl.dtype),
-        ),
-        in_specs=[VM, VM, VM],
-        out_specs=(ANY, ANY, VM),
-        scratch_shapes=[D(()), D(()), D((2,)), D((zs,)), D((zs,)), D((zs,)), D((zs,)), D((zs,)), D(()), D(()), D((nc,)), D((4 * nc,)), D((2 * nc,)), D((2 * nc,))],
-        compiler_params=pltpu.CompilerParams(collective_id=cid, has_side_effects=True),
-        name="front",
-    )(x, wp, tl)
-
-
-def tail_kernel(nf, zs, x_ref, g_ref, tl_ref, o_ref, go_ref, to_ref, t, r0, ral, rar, fin, gt, ga, gb, lsem, s0, q0, szr, szl, rzr, rzl, sf, ts, tr, gl, sg, rg, sa, ra):
+        lambda *refs: attn_kernel(nf, zs, hp, scale, refs),
+        out_shape=[s for s, _ in outs],
+        in_specs=[VM] * 9,
+        out_specs=[b for _, b in outs],
+        scratch_shapes=scratch,
+        compiler_params=pltpu.CompilerParams(collective_id=cid, has_side_effects=True, vmem_limit_bytes=60 * 2**20),
+        name="attention",
+    )(x, wp, tl, wo, tb, cosine, sine, pos[:, None], pos[None, :])
+
+
+def tail_kernel(nf, zs, x_ref, g_ref, tl_ref, o_ref, go_ref, to_ref, t, r0, ral, rar, fin, gt, ga, gb, lsem, s0, q0, szr, szl, rzr, rzl, sf, gl, sg, rg, sa, ra, *tile_b):
     f, c, z, k = place_of()
     nc = 2 * zs
     half = o_ref.shape[1] // 2
@@ -777,7 +1195,7 @@
             cp = pltpu.make_async_copy(g_ref.at[col, pl.ds(p * hc, hc)], gt.at[p, i], gl.at[2 * p + i])
             cp.start()
             gcopies.append(cp)
-    greet_all(f, c, nf, nc)
+    greet_cross(f, c, nf, nc)
     w = Wire()
     for p, (fa, fb, fc) in enumerate(parts):
         for i, col in enumerate((fc, fa)):
@@ -789,7 +1207,8 @@
         cp = pltpu.make_async_copy(src(zz, k), t.at[zz], lsem.at[zi])
         cp.start()
         locals_.append(cp)
-    deal_tiles(tl_ref, to_ref, ts, tr, f, c, nf, nc)
+    small_steps = tile_steps(w, nf, nc, tl_ref, to_ref, *tile_b)
+    advance(small_steps)
 
     def complete(zi):
         zz = zord[zi]
@@ -816,6 +1235,7 @@
 
         w.send(t.at[zz], ral.at[zz], szr.at[zz], rzr.at[zz], (f, c + 2), right)
         w.send(t.at[zz], rar.at[zz], szl.at[zz], rzl.at[zz], (f, c - 2), jnp.logical_not(right))
+        advance(small_steps)
         if zi == 0:
             for p, (fa, fb, fc) in enumerate(parts):
                 for i in (0, 1):
@@ -856,7 +1276,8 @@
         got(go_ref.at[cc], sa.at[cc], ra.at[cc], (f, c), c != cc)
     got(fin, sf.at[0], sf.at[1], sib)
     o_ref[:, pl.ds(pl.multiple_of((1 - k) * half, 128), half)] = fin[...]
-    await_tiles(tl_ref, to_ref, ts, tr, f, c, nf, nc)
+    while advance(small_steps):
+        pass
     w.drain()
 
 
@@ -873,46 +1294,15 @@
         out_shape=(
             jax.ShapeDtypeStruct((rows, width), x.dtype),
             jax.ShapeDtypeStruct((nc,) + gs, g.dtype),
-            jax.ShapeDtypeStruct(tl.shape, tl.dtype),
+            jax.ShapeDtypeStruct((nf * nc,) + tl.shape[2:], tl.dtype),
         ),
         in_specs=[ANY, ANY, VM],
         out_specs=(VM, VM, VM),
         scratch_shapes=[V(zs), V(zs), V(zs), V(zs), pltpu.VMEM((rows, half), x.dtype), G(2, 2), G(2, 2), G(2),
-            D((zs,)), D((zs,)), D((zs,)), D((zs,)), D((zs,)), D((zs,)), D((zs,)), D((2,)), D(()), D(()), D((4,)), D((6,)), D((6,)), D((nc,)), D((nc,))],
+            D((zs,)), D((zs,)), D((zs,)), D((zs,)), D((zs,)), D((zs,)), D((zs,)), D((2,)), D((4,)), D((6,)), D((6,)), D((nc,)), D((nc,))] + tile_bufs(nf, nc, tl.shape[2:]),
         compiler_params=pltpu.CompilerParams(collective_id=cid, has_side_effects=True, vmem_limit_bytes=60 * 2**20),
         name="tail",
     )(x, g, tl)
-
-
-def attend_kernel(scale, qb, q_ref, k_ref, v_ref, pr_ref, pc_ref, o_ref, l_ref):
-    rows = q_ref.shape[0]
-    keys = k_ref[...]
-    values = v_ref[...]
-    for i in range(rows // qb):
-        at = pl.ds(i * qb, qb)
-        s = lax.dot_general(q_ref[at, :], keys, (((1,), (1,)), ((), ())), preferred_element_type=jnp.float32) * scale
-        s = jnp.where(pc_ref[...] <= pr_ref[at, :], s, -jnp.inf)
-        top = jnp.max(s, axis=-1, keepdims=True)
-        e = jnp.exp(s - top)
-        total = jnp.sum(e, axis=-1, keepdims=True)
-        p = (e * (1.0 / total)).astype(jnp.bfloat16)
-        o_ref[at, :] = jnp.dot(p, values, preferred_element_type=jnp.float32).astype(jnp.bfloat16)
-        l_ref[at, :] = jnp.broadcast_to(top + jnp.log(total), (qb, l_ref.shape[1]))
-
-
-def attend(q, keys, values, pos, scale):
-    rows, width = q.shape
-    hd = keys.shape[1]
-    col = pl.BlockSpec((rows, hd), lambda h: (0, h))
-    full = pl.BlockSpec((rows, hd), lambda h: (0, 0))
-    return pl.pallas_call(
-        functools.partial(attend_kernel, scale, 256),
-        grid=(width // hd,),
-        out_shape=(jax.ShapeDtypeStruct((rows, width), jnp.bfloat16), jax.ShapeDtypeStruct((rows, width), jnp.float32)),
-        in_specs=[col, full, full, pl.BlockSpec((rows, 1), lambda h: (0, 0)), pl.BlockSpec((1, rows), lambda h: (0, 0))],
-        out_specs=(col, col),
-        name="attend",
-    )(q, keys, values, pos[:, None], pos[None, :])
 
 
 def attend_grad_kernel(scale, qb, q_ref, k_ref, v_ref, c_ref, g_ref, l_ref, pr_ref, pc_ref, gq_ref, gk_ref, gv_ref):
@@ -925,12 +1315,13 @@
         gk_ref[...] = jnp.zeros_like(gk_ref)
         gv_ref[...] = jnp.zeros_like(gv_ref)
 
+    lane = lax.broadcasted_iota(jnp.int32, (1, l_ref.shape[1]), 1)
     for i in range(rows // qb):
         at = pl.ds(i * qb, qb)
         q = q_ref[at, :]
         g = g_ref[at, :]
         s = lax.dot_general(q, keys, (((1,), (1,)), ((), ())), preferred_element_type=jnp.float32) * scale
-        p = jnp.where(pc_ref[...] <= pr_ref[at, :], jnp.exp(s - l_ref[at, 0:1]), 0.0)
+        p = jnp.where(pc_ref[...] <= pr_ref[at, :], jnp.exp(s - jnp.sum(jnp.where(lane == pl.program_id(0), l_ref[at, :], 0.0), axis=-1, keepdims=True)), 0.0)
         gv_ref[...] += lax.dot_general(p.astype(jnp.bfloat16), g, (((0,), (0,)), ((), ())), preferred_element_type=jnp.float32)
         gp = lax.dot_general(g, values, (((1,), (1,)), ((), ())), preferred_element_type=jnp.float32)
         delta = jnp.sum(g.astype(jnp.float32) * c_ref[at, :].astype(jnp.float32), axis=-1, keepdims=True)
@@ -948,7 +1339,7 @@
         functools.partial(attend_grad_kernel, scale, 256),
         grid=(width // hd,),
         out_shape=(jax.ShapeDtypeStruct((rows, width), jnp.float32), jax.ShapeDtypeStruct((rows, hd), jnp.float32), jax.ShapeDtypeStruct((rows, hd), jnp.float32)),
-        in_specs=[col, full, full, col, col, col, pl.BlockSpec((rows, 1), lambda h: (0, 0)), pl.BlockSpec((1, rows), lambda h: (0, 0))],
+        in_specs=[col, full, full, col, col, full, pl.BlockSpec((rows, 1), lambda h: (0, 0)), pl.BlockSpec((1, rows), lambda h: (0, 0))],
         out_specs=(col, full, full),
         name="attend_grad",
     )(q, keys, values, ctx, grad, lse, pos[:, None], pos[None, :])
@@ -993,53 +1384,38 @@
     ids, weights = expert_ids[0], route_weight[0].astype(f32)
     named = ids[None, :, :] == jnp.arange(n, dtype=jnp.int32)[:, None, None]
     to_expert = jnp.sum(jnp.where(named, weights[None], 0.0), axis=-1)
-    gains = jnp.concatenate([gain_attn, gain_moe]).astype(f32)
-    gains = jnp.pad(gains, (0, rows - gains.shape[0]))
-    qk_row = jnp.pad(qk_gain.reshape(-1).astype(f32), (0, rows - qk_gain.size))
-    tiles = jnp.concatenate(
-        [to_expert[:, None], jnp.broadcast_to(jnp.stack([gains, qk_row]), (n, 2, rows)), jnp.zeros((n, 5, rows), f32)], axis=1
-    )
+    lane = jnp.arange(rows)
+    gs = gain_attn.shape[0]
+    me = f * nc + c
+    spots = lane // gs == me % (rows // gs)
+    gain_row = lambda g: jnp.where(spots, jnp.tile(g.astype(f32), rows // gs), 0.0)
+    qs = qk_gain.shape[1]
+    qk_row = lambda g: jnp.where(lane // qs == me, jnp.tile(g.astype(f32), rows // qs), 0.0)
+    small = jnp.stack([gain_row(gain_attn), qk_row(qk_gain[0]), qk_row(qk_gain[1]), gain_row(gain_moe)])
+    tiles = jnp.concatenate([to_expert[:, None], jnp.broadcast_to(small, (n,) + small.shape), jnp.zeros((n, 3, rows), f32)], axis=1)
+    by_place = lambda t: t.reshape((nf, nc) + t.shape[1:]).swapaxes(0, 1)
     per = nc // kv_heads
     wq_p = w_query.reshape(shard, nc, hp * hd).transpose(1, 0, 2)
     wk_p = jnp.repeat(w_key.reshape(shard, kv_heads, hd).transpose(1, 0, 2), per, axis=0)
     wv_p = jnp.repeat(w_value.reshape(shard, kv_heads, hd).transpose(1, 0, 2), per, axis=0)
     packed = jnp.concatenate([wq_p, wk_p, wv_p], axis=2)
-    x_seq, w_all, dealt = front(x_own, packed, tiles, nf, zs, 0)
-
+    top_own = cotangent[0]
+    pos = seq_positions(pair_order, BLOCK)
+    cosine, sine = rope_tables(pos, hd)
+    (x_seq, normed_in, w_all, dealt, wo_all, top_all, q_pre, k_pre, query_rot, key_rot, values, context, lse, hidden_res, tokens) = attention(
+        x_own, packed, by_place(tiles), w_out, top_own.astype(bf16), cosine, sine, pos, nf, zs, hp, scale, 0
+    )
+    lin = lambda ff, cc: ff * nc + cc
+    hops = [(h, lin(h % hp, h // hp)) for h in range(n)]
     qw = hp * hd
     w_cat = w_all.reshape(n * shard, qw + 2 * hd)
-    gs = gain_attn.shape[0]
-    g_attn = dealt[:, 1, :gs].reshape(-1)
-    g_moe = dealt[:, 1, gs : 2 * gs].reshape(-1)
-    g_qk = dealt[:, 2, : qk_gain.size].reshape(n, 2, -1).transpose(1, 0, 2).reshape(2, hd)
+    wo_mine = wo_all.reshape(qw, width)
+    full_row = lambda r: dealt[:, r].reshape(-1, rows // gs, rows).sum(axis=1).reshape(-1)
+    g_attn, g_moe = full_row(1), full_row(4)
+    g_qk = dealt[:, 2:4].sum(axis=0)
     route_w = dealt[:, 0, :]
-
-    top_own = cotangent[0]
-    top_b = top_own.astype(bf16)
-    wo_own, top_b_sent, x_seq = lax.optimization_barrier((w_out, top_b, x_seq))
-    lin = lambda ff, cc: ff * nc + cc
-    hops = [(h, lin(h % hp, h // hp)) for h in range(n)]
-    wo_mine = lax.all_gather(lax.ppermute(wo_own, ("fsdp", "cp"), hops), "fsdp", axis=0, tiled=True)
-    top_all = lax.all_gather(top_b_sent, ("fsdp", "cp"), axis=0, tiled=True)
-
-    x32 = x_seq.reshape(span, width).astype(f32)
-    inv_in = lax.rsqrt(jnp.mean(x32 * x32, axis=-1, keepdims=True) + EPSILON)
-    normed_in = (x32 * inv_in * g_attn).astype(bf16)
-    pre = jnp.dot(normed_in, w_cat, preferred_element_type=f32)
-    q_pre = pre[:, :qw].reshape(span, hp, hd)
-    k_pre = pre[:, qw : qw + hd].reshape(span, 1, hd)
-    values = pre[:, qw + hd :].astype(bf16)
-    pos = seq_positions(pair_order, BLOCK)
-    cosine, sine = rope_tables(pos, hd)
-    query_rot = head_post(q_pre, g_qk[0], cosine, sine).astype(bf16).reshape(span, qw)
-    key_rot = head_post(k_pre, g_qk[1], cosine, sine).astype(bf16).reshape(span, hd)
-    context, lse = attend(query_rot, key_rot, values, pos, scale)
-    partial = jnp.dot(context, wo_mine, preferred_element_type=f32).astype(bf16)
-    attn_out = scatter(partial.reshape(nc, rows, width), zs, False, 1)
-    hidden_res = resid + attn_out.astype(f32)
-    normed_mid = rms_scale(hidden_res, g_moe).astype(bf16)
-
-    tokens = gather(normed_mid, zs, True, 2, nf)
+    q_pre = q_pre.reshape(span, hp, hd)
+    k_pre = k_pre.reshape(span, 1, hd)
     hit = route_w > 0.0
     below = (jnp.arange(rows)[:, None] < jnp.arange(rows)[None, :]).astype(f32)
     rank = jnp.dot(hit.astype(f32), below, preferred_element_type=f32).astype(jnp.int32)
@@ -1092,6 +1468,8 @@
     _, key_back = jax.vjp(lambda pre, gain: head_post(pre, gain, cosine, sine), k_pre, g_qk[1])
     grad_k_pre, grad_k_gain = key_back(grad_keys.reshape(span, 1, hd))
     grad_q_b = grad_q_pre.reshape(span, qw).astype(bf16)
+    x32 = x_seq.reshape(span, width).astype(f32)
+    inv_in = lax.rsqrt(jnp.mean(x32 * x32, axis=-1, keepdims=True) + EPSILON)
     first = k == 0
     grad_kv_b = jnp.where(first, grad_k_pre.reshape(span, hd), grad_values).astype(bf16)
     grad_cat = jnp.concatenate([grad_q_b, grad_kv_b], axis=1)
@@ -1107,7 +1485,7 @@
     wide = lambda v: jnp.pad(v, ((0, 0), (0, rows - v.shape[1])))
     sums = jnp.concatenate([wide(line0)[:, None], wide(qk_parts)[:, None], jnp.zeros((n, 6, rows), f32)], axis=1)
     grad_in, grads, summed = tail(
-        grad_norm.astype(bf16).reshape(nc, rows, width), grad_w.reshape(nf, nc, shard, qw + hd), sums, nf, zs, 5
+        grad_norm.astype(bf16).reshape(nc, rows, width), grad_w.reshape(nf, nc, shard, qw + hd), by_place(sums), nf, zs, 5
     )
     total = jnp.sum(summed, axis=0)
     own_attn_gain = total[0, :gs]

time: 899 us -> 817 us (0.909)
  Pallas kernels: 544 us -> 508 us
  other arithmetic: 84.8 us -> 67.1 us
  matrix products: 163 us -> 147 us
  local copies, waits for them, and re-layouts: 36.3 us -> 25.5 us
    pallas_call x2 -> x1, Pallas kernels: 87.4 us -> 256 us  [attention(): pl.pallas_call(lambda *refs: attn_kernel(nf, zs, hp, scale, refs), out_sh...]
    pallas_call x2 -> x1, Pallas kernels: 196 us -> 92.2 us  [scatter(): pl.pallas_call(functools.partial(rs_kernel, zs, planes), out_shape=jax.Sh...]
    pallas_call x2 -> x1, Pallas kernels: 144 us -> 45.8 us  [gather(): pl.pallas_call(functools.partial(ag_kernel, zs, planes), out_shape=jax.Sh...]
    dot_general x2 -> x0, matrix products: 9.68 us -> none  [the longest x1 6.27 us: head_body(): partial = jnp.dot(context, wo_mine, preferred_element_type=f32).astype(bf16)]
  transfers between devices with their start and end apart: 7 -> 4, of which waited for: 2 -> 1; matrix products, arithmetic and copies ran while one was open for 23% -> 15% of each run, Pallas kernels for 37% -> 14%
where the time goes in v2:
time: 817 us; the launch traced here: 808 us
  Pallas kernels  508 us (62%)
  matrix products  147 us (18%)
  other arithmetic  67.1 us (8%)
  waiting for transfers between devices  39.1 us (5%)
  local copies, waits for them, and re-layouts  25.5 us (3%)
  between operations  15.1 us (2%)
    pallas_call x1, Pallas kernels, attention(): pl.pallas_call(lambda *refs: attn_kernel(nf, zs, hp, scale, refs), out_sh...  256 us
    pallas_call x1, Pallas kernels, tail(): pl.pallas_call(functools.partial(tail_kernel, nf, zs), out_shape=(jax.Sha...  97.6 us
    pallas_call x1, Pallas kernels, scatter(): pl.pallas_call(functools.partial(rs_kernel, zs, planes), out_shape=jax.Sh...  92.2 us
    pallas_call x1, Pallas kernels, gather(): pl.pallas_call(functools.partial(ag_kernel, zs, planes), out_shape=jax.Sh...  45.8 us
    dot_general x5, matrix products, contract_cols(): lax.dot_general(left, right, (((1,), (1,)), ((), ())), preferred_element_...  44.3 us
    reduce_scatter x1, waiting for transfers between devices, head_body(): lax.psum_scatter(back(mixing, expert_out).reshape(n * rows, width), ('fsd...  39.1 us
    dot_general x5, matrix products, contract_rows(): lax.dot_general(left, right, (((0,), (0,)), ((), ())), preferred_element_...  37.8 us
    dot_general x2, matrix products, head_body(): jnp.einsum('srt,srd->std', table, rws.reshape(n, capacity, width), prefer...  26.3 us
  transfers between devices with their start and end apart: 4, of which 1 were waited for; matrix products, arithmetic and copies ran while one was open for 15% of the time, Pallas kernels for 14%

profile of v2, /device:TPU:0, one launch (start us, length us, event | category | flops | bytes accessed | tf_op | source)
XLA Modules:
  0.0 807.8 jit_solution(4115126980084400968)
XLA Ops:
  9.2 1.9 copy.130
  15.0 2.1 bitcast_convert_fusion.refs_4_
  17.7 4.7 select_reduce_fusion
  24.1 2.9 fusion.50
  28.0 1.9 fusion.41.refs_7_.pr_ref
  30.7 2.0 pad_maximum_fusion.4.refs_1_
  33.5 255.5 %attention.1 = (bf16[8,128,2048]{2,1,0:T(8,128)(2,1)}, bf16[1024,2048]{1,0:T(8,128)(2,1)}, bf16[32,64,768]{2,1,0:T(8,128)(2,1)}, f32[32,8,128]{2,1,0:T(8,128)}, ...) custom-call(bf16[128,2048]{1,0:T(8,128)(2,1)} %bitcast.209, ...), custom_call_target="tpu_custom_call" | custom-call | tf_op jit(solution)/shard_map/attention/pallas_call | solution.py:1158
  291.2 8.2 %convolution_convert_fusion.4 = bf16[32,48,2048]{2,1,0:T(8,128)(2,1)S(1)} fusion(bf16[32,128,2048]{2,1,0:T(8,128)(2,1)} %get-tuple-element.38, s32[32,128]{1,0:T(8,128)S(1)} %convolution_convert_fusion.8, pred[32,128]{1,0:T(8,128)(4,1)S(1)} %bitcast.234), kind=kOutput, calls=%fused_computation.14 | convolution fusion | flops 808845312 | bytes 23089152 | tf_op jit(solution)/shard_map/srt,std->srd/dot_general | solution.py:1426
  299.5 6.6 fusion.11
  306.1 6.6 fusion.7
  312.7 8.1 %convolution_convert_fusion.3 = bf16[32,48,2048]{2,1,0:T(8,128)(2,1)S(1)} fusion(bf16[32,128,2048]{2,1,0:T(8,128)(2,1)} %get-tuple-element.39, f32[32,128]{1,0:T(8,128)S(1)} %bitcast.230, s32[32,128]{1,0:T(8,128)S(1)} %convolution_convert_fusion.8, pred[32,128]{1,0:T(8,128)(4,1)S(1)} %bitcast.235), kind=kOutput, calls=%fused_computation.13 | convolution fusion | flops 809041920 | bytes 23105536 | tf_op jit(solution)/shard_map/srt,std->srd/dot_general | solution.py:1426
  320.8 13.4 %multiply_convert_fusion = (bf16[1536,768]{1,0:T(8,128)(2,1)}, bf16[1536,768]{1,0:T(8,128)(2,1)}, bf16[1536,768]{1,0:T(8,128)(2,1)}) fusion(f32[1536,768]{1,0:T(8,128)} %fusion.11, f32[1536,768]{1,0:T(8,128)} %fusion.7, bf16[1536,2048]{1,0:T(8,128)(2,1)S(1)} %bitcast.203, bf16[1,768,2048]{2,1,0:T(8,128)(2,1)S(1)} %copy-done), kind=kOutput, calls=%fused_computation.8 | convolution fusion | flops 4849532928 | bytes 25952256 | tf_op jit(solution)/shard_map/dot_general | solution.py:99
  334.3 6.8 fusion.9
  341.1 9.2 %add_convert_fusion = bf16[1536,2048]{1,0:T(8,128)(2,1)} fusion(f32[1536,2048]{1,0:T(8,128)S(1)} %fusion.9, bf16[1536,768]{1,0:T(8,128)(2,1)} %get-tuple-element.72, bf16[1,2048,768]{2,1,0:T(8,128)(2,1)S(1)} %copy-done.17), kind=kOutput, calls=%fused_computation.2 | convolution fusion | flops 4838129664 | bytes 24379392 | tf_op jit(solution)/shard_map/dot_general | solution.py:99
  350.4 13.0 %convolution_convert_fusion.1.x_ref = bf16[32,128,2048]{2,1,0:T(8,128)(2,1)} fusion(bf16[32,48,2048]{2,1,0:T(8,128)(2,1)} %bitcast.208, s32[32,128]{1,0:T(8,128)S(1)} %convolution_convert_fusion.8, pred[32,128]{1,0:T(8,128)(4,1)S(1)} %bitcast.236), kind=kOutput, calls=%fused_computation.1 | convolution fusion | flops 814088192 | bytes 23089152 | tf_op jit(solution)/shard_map/srt,srd->std/dot_general | solution.py:1427
  363.4 92.2 %scatter_all.1 = bf16[128,2048]{1,0:T(8,128)(2,1)} custom-call(bf16[32,128,2048]{2,1,0:T(8,128)(2,1)} %convolution_convert_fusion.1.x_ref), custom_call_target="tpu_custom_call" | custom-call | tf_op jit(solution)/shard_map/scatter_all/pallas_call | solution.py:605
  457.0 1.7 multiply_reduce_fusion.4
  458.7 2.8 fusion.92.x_ref
  461.5 45.8 %gather_seq.1 = bf16[8,128,2048]{2,1,0:T(8,128)(2,1)} custom-call(bf16[128,2048]{1,0:T(8,128)(2,1)} %fusion.92.x_ref), custom_call_target="tpu_custom_call" | custom-call | tf_op jit(solution)/shard_map/gather_seq/pallas_call | solution.py:464
  507.4 6.2 convolution_convert_fusion.6
  513.6 9.0 %convolution_convert_fusion.2 = bf16[1536,2048]{1,0:T(8,128)(2,1)} fusion(bf16[1536,768]{1,0:T(8,128)(2,1)} %get-tuple-element.40, bf16[1,768,2048]{2,1,0:T(8,128)(2,1)S(1)} %copy-done), kind=kOutput, calls=%fused_computation.7 | convolution fusion | flops 4834983936 | bytes 11796480 | tf_op jit(solution)/shard_map/dot_general | solution.py:1448
  522.6 13.2 %convolution_convert_fusion = bf16[32,128,2048]{2,1,0:T(8,128)(2,1)} fusion(bf16[32,48,2048]{2,1,0:T(8,128)(2,1)} %bitcast.207, f32[32,128]{1,0:T(8,128)S(1)} %bitcast.231, s32[32,128]{1,0:T(8,128)S(1)} %convolution_convert_fusion.8, pred[32,128]{1,0:T(8,128)(4,1)S(1)} %bitcast.237), kind=kOutput, calls=%fused_computation | convolution fusion | flops 814284800 | bytes 23105536 | tf_op jit(solution)/shard_map/srt,srd->std/dot_general | solution.py:1427
  535.9 1.6 copy-done.18
  537.4 5.9 convolution_convert_fusion.7.g_ref
  543.3 16.9 %attend_grad.1 = (f32[1024,512]{1,0:T(8,128)}, f32[1024,128]{1,0:T(8,128)}, f32[1024,128]{1,0:T(8,128)}) custom-call(bf16[1024,512]{1,0:T(8,128)(2,1)} %get-tuple-element.41.q_ref, bf16[1024,128]{1,0:T(8,128)(2,1)} %get-tuple-element.42.k_ref, bf16[1024,128]{1,0:T(8,128)(2,1)} %get-tuple-element.43.v_ref, bf16[1024,512]{1,0:T(8,128)(2,1)} %get-tuple-element.44.c_ref, ...), custom_call_target="tpu_custom_call" | custom-call | tf_op jit(solution)/shard_map/attend_grad/pallas_call | solution.py:1338
  560.2 2.2 pad_maximum_fusion.1
  562.8 1.5 slice.91
  564.3 2.0 reshape.784
  567.9 2.9 reshape.783
  571.8 2.2 broadcast_multiply_fusion
  574.0 1.5 fusion.93
  575.7 5.9 multiply_reduce_fusion.1
  583.8 6.0 fusion.17
  591.6 3.3 multiply_reduce_fusion
  594.9 2.1 slice_select_fusion
  597.0 10.1 %convolution_bitcast_fusion.2 = f32[1,2048,768]{2,1,0:T(8,128)} fusion(bf16[1536,2048]{1,0:T(8,128)(2,1)} %bitcast.199, bf16[1536,768]{1,0:T(8,128)(2,1)S(1)} %copy-done.20), kind=kOutput, calls=%fused_computation.17 | convolution fusion | flops 4831838208 | bytes 14942208 | tf_op jit(solution)/shard_map/dot_general | solution.py:93
  607.2 7.3 convolution_bitcast_fusion.1
  614.5 7.0 convolution_bitcast_fusion
  621.5 1.4 fusion.91
  622.9 1.9 sine_multiply_fusion
  625.0 2.5 fusion.46
  628.2 8.9 %fusion.1 = (f32[2048]{0:T(1024)S(1)}, bf16[1024,2048]{1,0:T(8,128)(2,1)}) fusion(f32[1024]{0:T(1024)S(1)} %rsqrt_bitcast_fusion, bf16[8,128,2048]{2,1,0:T(8,128)(2,1)} %get-tuple-element.54, bf16[2048,128]{1,0:T(8,128)(2,1)} %slice_select_fusion, bf16[2048,512]{1,0:T(8,128)(2,1)} %slice.91, bf16[1024,128]{1,0:T(8,128)(2,1)S(1)} %fusion.44, ...), kind=kOutput, calls=%fused_computation.5 | convolution fusion | flops 2702702592 | bytes 12333056 | tf_op jit(solution)/shard_map/dot_general | solution.py:99
  638.0 7.3 convolution_convert_fusion.5
  645.2 97.6 %tail.1 = (bf16[128,2048]{1,0:T(8,128)(2,1)}, bf16[8,64,640]{2,1,0:T(8,128)(2,1)}, f32[32,8,128]{2,1,0:T(8,128)}) custom-call(bf16[8,128,2048]{2,1,0:T(8,128)(2,1)} %bitcast.213, bf16[4,8,64,640]{3,2,1,0:T(8,128)(2,1)} %bitcast.216, f32[8,4,8,128]{3,2,1,0:T(8,128)} %maximum_bitcast_fusion.1.tl_ref), custom_call_target="tpu_custom_call" | custom-call | tf_op jit(solution)/shard_map/tail/pallas_call | solution.py:1292
  748.8 5.4 collective-permute-start.1
  755.4 2.3 convert_element_type.186
  757.7 39.1 %reduce-scatter.3.cloned.1.call-done = bf16[128,2048]{1,0:T(8,128)(2,1)} async-done(((bf16[4096,2048]{1,0:T(8,128)(2,1)}), bf16[128,2048]{1,0:T(8,128)(2,1)}) %reduce-scatter.3.cloned.1.call-update) | async-done | bytes 524304 | tf_op jit(solution)/shard_map/reduce_scatter | solution.py:1449
  796.8 3.8 fusion.22
  (146 shorter events, 30.4 us)
Async XLA Ops:
  7.2 313.7 %copy-start = (bf16[1,768,2048]{2,1,0:T(8,128)(2,1)S(1)}, bf16[1,768,2048]{2,1,0:T(8,128)(2,1)}, u32[]{:S(2)}) copy-start(bf16[1,768,2048]{2,1,0:T(8,128)(2,1)} %param.26) | copy-start | bytes 9437188
  7.2 9.9 %copy-start.15 = (s32[8]{0:T(128)S(1)}, s32[8]{0:T(128)}, u32[]{:S(2)}) copy-start(s32[8]{0:T(128)} %param.29) | copy-start | bytes 100
  7.2 741.6 %reduce-scatter.5.cloned.1.call-start = ((), (), s32[]{:S(2)}) async-start(), calls=%async_computation.3 | async-start | bytes 2621440 | tf_op jit(solution)/shard_map/reduce_scatter | solution.py:1458
  291.2 8.3 %copy-start.16 = (bf16[1,2048,768]{2,1,0:T(8,128)(2,1)S(1)}, bf16[1,2048,768]{2,1,0:T(8,128)(2,1)}, u32[]{:S(2)}) copy-start(bf16[1,2048,768]{2,1,0:T(8,128)(2,1)} %param.24) | copy-start | bytes 9437188
  299.4 6.7 copy-start.3
  299.4 6.7 copy-start.17
  320.8 13.5 %copy-start.4 = (bf16[32,48,2048]{2,1,0:T(8,128)(2,1)}, bf16[32,48,2048]{2,1,0:T(8,128)(2,1)S(1)}, u32[]{:S(2)}) copy-start(bf16[32,48,2048]{2,1,0:T(8,128)(2,1)S(1)} %convolution_convert_fusion.3) | copy-start | bytes 18874372
  513.6 283.2 %reduce-scatter.3.cloned.1.call-start = ((), (), s32[]{:S(2)}) async-start(), calls=%async_computation.2 | async-start | bytes 17301504 | tf_op jit(solution)/shard_map/reduce_scatter | solution.py:1449
  535.9 1.6 copy-start.18
  543.3 19.5 %copy-start.10 = (bf16[32,64,768]{2,1,0:T(8,128)(2,1)S(1)}, bf16[32,64,768]{2,1,0:T(8,128)(2,1)}, u32[]{:S(2)}) copy-start(bf16[32,64,768]{2,1,0:T(8,128)(2,1)} %get-tuple-element.52) | copy-start | bytes 9437188
  562.4 59.0 %collective-permute-start = (f32[2,1024,128]{2,1,0:T(8,128)}, f32[2,1024,128]{2,1,0:T(8,128)}, u32[]{:S(2)}, u32[]{:S(2)}) collective-permute-start(f32[2,1024,128]{2,1,0:T(8,128)} %pad_maximum_fusion.1), channel_id=1, source_target_pairs={{0,1},{1,0},{2,3},{3,2},{4,5},{5,4},{6,7},{7,6},{8,9},{9,8},{10,11... | collective-permute-start | bytes 3145736 | tf_op jit(solution)/shard_map/ppermute | solution.py:1464
  567.5 4.3 copy-start.6
  573.9 1.6 copy-start.2
  574.0 1.7 copy-start.5
  583.8 7.6 copy-start.9
  591.4 5.6 copy-start.20
  591.6 15.5 %slice-start = ((s8[6291456]{0:T(1024)(128)(4,1)}), s8[4194304]{0:T(1024)(128)(4,1)S(1)}, s32[]{:S(2)}) async-start(s8[6291456]{0:T(1024)(128)(4,1)} %bitcast.200), calls=%async_computation.4 | async-start | bytes 8388608
  597.0 10.1 %slice-start.1 = ((s8[6291456]{0:T(1024)(128)(4,1)}), s8[2097152]{0:T(1024)(128)(4,1)S(1)}, s32[]{:S(2)}) async-start(s8[6291456]{0:T(1024)(128)(4,1)} %bitcast.200), calls=%async_computation.5 | async-start | bytes 4194304
  597.0 10.1 %copy-start.21 = (bf16[1536,768]{1,0:T(8,128)(2,1)S(1)}, bf16[1536,768]{1,0:T(8,128)(2,1)}, u32[]{:S(2)}) copy-start(bf16[1536,768]{1,0:T(8,128)(2,1)} %get-tuple-element.72) | copy-start | bytes 7077892
  597.0 17.4 %slice-start.2 = ((s8[6291456]{0:T(1024)(128)(4,1)}), s8[4194304]{0:T(1024)(128)(4,1)S(1)}, s32[]{:S(2)}) async-start(s8[6291456]{0:T(1024)(128)(4,1)} %bitcast.204), calls=%async_computation.6 | async-start | bytes 8388608
  607.1 7.3 slice-start.3
  607.2 7.3 copy-start.19
  614.4 7.0 copy-start.11
  614.5 7.0 copy-start.12
  621.5 1.4 copy-start.8
  628.2 9.8 %copy-start.14 = (bf16[128,8,4,128]{3,1,2,0:T(8,128)(2,1)S(1)}, bf16[128,8,4,128]{3,1,2,0:T(8,128)(2,1)}, u32[]{:S(2)}) copy-start(bf16[128,8,4,128]{3,1,2,0:T(8,128)(2,1)} %copy.129) | copy-start | bytes 3145732
  742.9 5.6 copy-start.7
  742.9 5.6 copy-start.13
  748.8 6.6 collective-permute-start.1
  755.4 45.1 %copy-start.1 = (bf16[1,768,2048]{2,1,0:T(8,128)(2,1)S(1)}, bf16[1,768,2048]{2,1,0:T(8,128)(2,1)}, u32[]{:S(2)}) copy-start(bf16[1,768,2048]{2,1,0:T(8,128)(2,1)} %param.26) | copy-start | bytes 9437188
Sparse Core Ops, SparseCore 0:
  513.7 33.7 reduce-scatter.4
  549.8 246.9 reduce-scatter.2

commit v3 on v2

--- a/solution.py
+++ b/solution.py
@@ -1166,183 +1166,693 @@
     )(x, wp, tl, wo, tb, cosine, sine, pos[:, None], pos[None, :])
 
 
-def tail_kernel(nf, zs, x_ref, g_ref, tl_ref, o_ref, go_ref, to_ref, t, r0, ral, rar, fin, gt, ga, gb, lsem, s0, q0, szr, szl, rzr, rzl, sf, gl, sg, rg, sa, ra, *tile_b):
+def sum_block(dst, srcs, rows=32):
+    n, r, wd = dst.shape
+
+    def step(i, _):
+        a = pl.ds(pl.multiple_of(i % (r // rows) * rows, rows), rows)
+        j = i // (r // rows)
+        total = srcs[0][j, a, :].astype(jnp.float32)
+        for s in srcs[1:]:
+            total = total + s[j, a, :].astype(jnp.float32)
+        dst[j, a, :] = total.astype(dst.dtype)
+        return 0
+
+    lax.fori_loop(0, n * (r // rows), step, 0)
+
+
+def spill_sum_steps(w, zs, x_ref, o_ref, r0, r1, r2, ral, rar, stage, out, fin, ls, s0, q0, s1, q1, s2, q2, szr, szl, rzr, rzl, sf):
     f, c, z, k = place_of()
-    nc = 2 * zs
     half = o_ref.shape[1] // 2
-    sib_c = c + 1 - 2 * k
-    sib = (f, sib_c)
-    low = z < zs // 2
-    zord = []
-    for i in range(zs - 1):
-        far_low = jnp.where(i < zs - 1 - z, zs - 1 - i, zs - 2 - i)
-        far_high = jnp.where(i < z, i, i + 1)
-        zord.append(jnp.where(low, far_low, far_high))
-    zord.append(z)
-
-    def src(zz, kk):
-        return x_ref.at[pl.ds(2 * zz, 2), :, pl.ds(pl.multiple_of(kk * half, 128), half)]
-
+    sib = (f, c + 1 - 2 * k)
+    b1 = 2 - k
+    b2 = 1 + k
+    f1 = flip(f, b1)
+    f2 = flip(f, b2)
+    f3 = flip(f1, b2)
+    cs = 2 * zs
+    cols = [f3, f1, f2, f]
+    order = far_first(z, zs)
+    held = [None] * out.shape[0]
+    count = [0]
+
+    def src(col, zz, kk):
+        return x_ref.at[pl.ds(col * cs + 2 * zz, 2), :, pl.ds(pl.multiple_of(kk * half, 128), half)]
+
+    for ci in range(4):
+        for zz in order:
+            slot = {0: 0, 1: 2, 2: 1, 3: 3}[ci] * zs + zz
+            w.send(src(cols[ci], zz, 1 - k), r0.at[slot], s0.at[slot], q0.at[slot], sib)
+    yield
+
+    def load(i, ref, when=None):
+        copy = pltpu.make_async_copy(ref, stage.at[i], ls.at[i])
+        if when is None:
+            copy.start()
+        else:
+            pl.when(when)(copy.start)
+        return copy
+
+    def slot_for():
+        i = count[0] % len(held)
+        count[0] += 1
+        if held[i] is not None:
+            w.settle(held[i])
+        return i
+
+    def base(ci, zz):
+        got(r0.at[ci * zs + zz], s0.at[ci * zs + zz], q0.at[ci * zs + zz], sib)
+        loads = [load(0, src(cols[ci], zz, k)), load(1, r0.at[ci * zs + zz])]
+        if ci >= 2:
+            m = (ci - 2) * zs + zz
+            got(r1.at[m], s1.at[m], q1.at[m], (f1, c))
+            loads.append(load(2, r1.at[m]))
+        if ci == 3:
+            got(r2.at[zz], s2.at[zz], q2.at[zz], (f2, c))
+            loads.append(load(3, r2.at[zz]))
+        return loads
+
+    def total(loads):
+        i = slot_for()
+        for copy in loads:
+            copy.wait()
+        sum_block(out.at[i], [stage.at[j] for j in range(len(loads))])
+        return i
+
+    for ci in (0, 1, 2):
+        for zz in order:
+            loads = base(ci, zz)
+            yield
+            i = total(loads)
+            if ci < 2:
+                m = ci * zs + zz
+                held[i] = [w.send(out.at[i], r1.at[m], s1.at[m], q1.at[m], (f1, c))]
+            else:
+                held[i] = [w.send(out.at[i], r2.at[zz], s2.at[zz], q2.at[zz], (f2, c))]
+            yield
+    for zz in order[:-1]:
+        loads = base(3, zz)
+        right = zz > z
+        from_left = jnp.logical_and(right, z > 0)
+        from_right = jnp.logical_and(jnp.logical_not(right), z < zs - 1)
+        got(ral.at[zz], szr.at[zz], rzr.at[zz], (f, c), from_left)
+        got(rar.at[zz], szl.at[zz], rzl.at[zz], (f, c), from_right)
+        more = [load(4, ral.at[zz], from_left), load(4, rar.at[zz], from_right)]
+        yield
+        i = total(loads)
+        for copy, when in zip(more, (from_left, from_right)):
+            pl.when(when)(copy.wait)
+
+            @pl.when(when)
+            def _(i=i):
+                add_into(out.at[i], stage.at[4])
+
+        held[i] = [
+            w.send(out.at[i], ral.at[zz], szr.at[zz], rzr.at[zz], (f, c + 2), right),
+            w.send(out.at[i], rar.at[zz], szl.at[zz], rzl.at[zz], (f, c - 2), jnp.logical_not(right)),
+        ]
+        yield
+    loads = base(3, z)
+    got(ral.at[z], szr.at[z], rzr.at[z], (f, c), z > 0)
+    more = load(4, ral.at[z], z > 0)
+    yield
+    i = total(loads)
+    pl.when(z > 0)(more.wait)
+
+    @pl.when(z > 0)
+    def _():
+        add_into(out.at[i], stage.at[4])
+
+    got(rar.at[z], szl.at[z], rzl.at[z], (f, c), z < zs - 1)
+    more = load(4, rar.at[z], z < zs - 1)
+    pl.when(z < zs - 1)(more.wait)
+
+    @pl.when(z < zs - 1)
+    def _():
+        add_into(out.at[i], stage.at[4])
+
+    w.send(out.at[i, 1 - k], fin, sf.at[0], sf.at[1], sib)
+    o_ref[:, pl.ds(pl.multiple_of(k * half, 128), half)] = out[i, k]
+    yield
+    got(fin, sf.at[0], sf.at[1], sib)
+    o_ref[:, pl.ds(pl.multiple_of((1 - k) * half, 128), half)] = fin[...]
+    yield
+
+
+def head_sum_steps(w, nf, nc, hp, g, o_ref, ga, gb, loc, sg, rg, so, ro):
+    f, c, z, k = place_of()
+    hr = g.shape[1] // 2
+    parts = []
+    for p in (0, 1):
+        mm = (lambda d: flip(d, 2)) if p else (lambda d: d)
+        fa = flip(f, 1 + p)
+        fb = flip(f, 2 - p)
+        parts.append((p, pl.ds(p * hr, hr), mm, fa, fb, flip(fa, 2 - p)))
+    for p, at, mm, fa, fb, fc in parts:
+        for i, d in enumerate((fc, fa)):
+            w.send(g.at[mm(d), at], ga.at[p, i], sg.at[p, i], rg.at[p, i], (fa, c))
+    yield
+    for p, at, mm, fa, fb, fc in parts:
+        for i, d in enumerate((fb, f)):
+            got(ga.at[p, i], sg.at[p, i], rg.at[p, i], (fa, c))
+            add_into(g.at[pl.ds(mm(d), 1), at], ga.at[p, pl.ds(i, 1)])
+            if i == 0:
+                w.send(g.at[mm(fb), at], gb.at[p], sg.at[p, 2], rg.at[p, 2], (fb, c))
+    yield
+    for p, at, mm, fa, fb, fc in parts:
+        got(gb.at[p], sg.at[p, 2], rg.at[p, 2], (fb, c))
+        add_into(g.at[pl.ds(mm(f), 1), at], gb.at[pl.ds(p, 1)])
+        head = hp * c + mm(f)
+        df, dc = head // nc, head % nc
+        stay = jnp.logical_and(df == f, dc == c)
+        w.send(g.at[mm(f), at], o_ref.at[at], so.at[p], ro.at[p], (df, dc), jnp.logical_not(stay))
+        keep = pltpu.make_async_copy(g.at[mm(f), at], o_ref.at[at], loc.at[p])
+        pl.when(stay)(keep.start)
+        pl.when(stay)(keep.wait)
+    yield
+    for p, at, mm, fa, fb, fc in parts:
+        head = f * nc + c
+        here = jnp.logical_and(head // hp == c, mm(head % hp) == f)
+        got(o_ref.at[at], so.at[p], ro.at[p], (f, c), jnp.logical_not(here))
+    yield
+
+
+def weight_sum_steps(w, nf, nc, g, o_ref, ga, gb, sg, rg, sa, ra):
+    f, c, z, k = place_of()
     hc = nc // 2
     parts = []
     for p in (0, 1):
         fa = flip(f, 1 + p)
         fb = flip(f, 2 - p)
-        parts.append((fa, fb, flip(fa, 2 - p)))
-    gcopies = []
-    for p, (fa, fb, fc) in enumerate(parts):
+        parts.append((p, pl.ds(p * hc, hc), fa, fb, flip(fa, 2 - p)))
+    for p, at, fa, fb, fc in parts:
+        for i, col in enumerate((fc, fa)):
+            w.send(g.at[col, at], ga.at[p, i], sg.at[2 * p + i], rg.at[2 * p + i], (fa, c))
+    yield
+    for p, at, fa, fb, fc in parts:
         for i, col in enumerate((fb, f)):
-            cp = pltpu.make_async_copy(g_ref.at[col, pl.ds(p * hc, hc)], gt.at[p, i], gl.at[2 * p + i])
-            cp.start()
-            gcopies.append(cp)
-    greet_cross(f, c, nf, nc)
+            got(ga.at[p, i], sg.at[2 * p + i], rg.at[2 * p + i], (fa, c))
+            add_into(g.at[col, at], ga.at[p, i])
+            if i == 0:
+                w.send(g.at[fb, at], gb.at[p], sg.at[4 + p], rg.at[4 + p], (fb, c))
+    yield
+    for p, at, fa, fb, fc in parts:
+        got(gb.at[p], sg.at[4 + p], rg.at[4 + p], (fb, c))
+        add_into(g.at[f, at], gb.at[p])
+    for i in range(1, nc):
+        cc = (c + i) % nc
+        w.send(g.at[f, cc], o_ref.at[c], sa.at[cc], ra.at[c], (f, cc))
+    o_ref[c] = g[f, c]
+    yield
+    for i in range(1, nc):
+        cc = (c + i) % nc
+        got(o_ref.at[cc], sa.at[cc], ra.at[cc], (f, c))
+    yield
+
+
+def grad_kernel(nf, zs, hp, scale, refs):
+    (res_ref, nm_ref, w_ref, wo_ref, qp_ref, kp_ref, qr_ref, kr_ref, v_ref, ctx_ref, lse_ref, cos_ref, sin_ref, pr_ref, pc_ref,
+     gqk_ref, gat_ref, moe_ref, mix_ref,
+     out_ref, go_ref, gwo_ref, to_ref, mixed_ref, h0, h1, h2, hl, hr,
+     res, gkv, gkv2, gcat, gw, gwo, tl, gqk, gat, loc, sl, szr, szl, rz, ssib, rsib, sk) = refs[:46]
+    rest = list(refs[46:])
+
+    def take(n):
+        part = rest[:n]
+        del rest[:n]
+        return part
+
+    tile_b = take(5)
+    sum_bufs = take(13)
+    spill_bufs = take(15)
+    head_b = take(7)
+    weight_b = take(6)
+    f, c, z, k = place_of()
+    nc = 2 * zs
+    rows, width = res_ref.shape
+    half = width // 2
+    hd = kr_ref.shape[1]
+    qw = hp * hd
+    span = nc * rows
+    f32, bf16 = jnp.float32, jnp.bfloat16
+    sib_c = c + 1 - 2 * k
+    sib = (f, sib_c)
+    first = k == 0
+
+    def chunk(zz, kk):
+        return res.at[pl.ds(2 * zz, 2), :, pl.ds(pl.multiple_of(kk * half, 128), half)]
+
+    own = pltpu.make_async_copy(res_ref, res.at[c], loc)
+    own.start()
+    with jax.named_scope("greet"):
+        greet_cross(f, c, nf, nc)
     w = Wire()
-    for p, (fa, fb, fc) in enumerate(parts):
-        for i, col in enumerate((fc, fa)):
-            w.send(g_ref.at[col, pl.ds(p * hc, hc)], ga.at[p, i], sg.at[2 * p + i], rg.at[2 * p + i], (fa, c))
-    locals_ = []
-    for zi in range(zs):
-        zz = zord[zi]
-        w.send(src(zz, 1 - k), r0.at[zz], s0.at[zz], q0.at[zz], sib)
-        cp = pltpu.make_async_copy(src(zz, k), t.at[zz], lsem.at[zi])
-        cp.start()
-        locals_.append(cp)
-    small_steps = tile_steps(w, nf, nc, tl_ref, to_ref, *tile_b)
-    advance(small_steps)
-
-    def complete(zi):
-        zz = zord[zi]
-        locals_[zi].wait()
-        got(r0.at[zz], s0.at[zz], q0.at[zz], sib)
-        add_into(t.at[zz], r0.at[zz])
-
-    for zi in range(zs - 1):
-        zz = zord[zi]
-        complete(zi)
+    w.send(res_ref, res.at[c], sl.at[0], sl.at[1], sib)
+    mix_steps = spill_sum_steps(w, zs, mix_ref, mixed_ref, h0, h1, h2, hl, hr, *spill_bufs)
+    own.wait()
+    got(res.at[sib_c], sl.at[0], sl.at[1], sib)
+    w.send(chunk(z, k), chunk(z, k), szr.at[z], rz.at[z], (f, c + 2), z < zs - 1)
+    w.send(chunk(z, k), chunk(z, k), szl.at[z], rz.at[z], (f, c - 2), z > 0)
+    advance(mix_steps, "mix")
+    gkv[...] = jnp.zeros_like(gkv)
+    gqk[...] = jnp.zeros_like(gqk)
+    gat[...] = jnp.zeros_like(gat)
+    gq, gk = gqk_ref[0:1, :], gqk_ref[1:2, :]
+    low_half = lax.broadcasted_iota(jnp.int32, (1, hd), 1) < hd // 2
+    lane = lax.broadcasted_iota(jnp.int32, (1, hd), 1)
+
+    def turned_back(t, g, grad, at):
+        u = grad * sin_ref[at, :]
+        other = pltpu.roll(u, hd // 2, 1)
+        gy = grad * cos_ref[at, :] + jnp.where(low_half, other, -other)
+        r = lax.rsqrt(jnp.mean(t * t, axis=-1, keepdims=True) + EPSILON)
+        n = t * r
+        gn = gy * g
+        back = r * (gn - n * jnp.mean(gn * n, axis=-1, keepdims=True))
+        return back, jnp.sum(gy * n, axis=0, keepdims=True)
+
+    def process(zz):
+        at = pl.ds(pl.multiple_of(2 * zz * rows, 2 * rows), 2 * rows)
+        rr = res[pl.ds(2 * zz, 2)].reshape(2 * rows, width)
+
+        def head(h, _):
+            hc = pl.ds(pl.multiple_of(h * hd, hd), hd)
+            g = lax.dot_general(rr, wo_ref[h], (((1,), (1,)), ((), ())), preferred_element_type=f32).astype(bf16)
+            q = qr_ref[at, hc]
+            s = lax.dot_general(q, kr_ref[...], (((1,), (1,)), ((), ())), preferred_element_type=f32) * scale
+            lse = jnp.sum(jnp.where(lane == h, lse_ref[at, :], 0.0), axis=-1, keepdims=True)
+            p = jnp.where(pc_ref[...] <= pr_ref[at, :], jnp.exp(s - lse), 0.0)
+            gkv[1] += lax.dot_general(p.astype(bf16), g, (((0,), (0,)), ((), ())), preferred_element_type=f32)
+            gp = lax.dot_general(g, v_ref[...], (((1,), (1,)), ((), ())), preferred_element_type=f32)
+            delta = jnp.sum(g.astype(f32) * ctx_ref[at, hc].astype(f32), axis=-1, keepdims=True)
+            ds = (p * (gp - delta)).astype(bf16)
+            gkv[0] += lax.dot_general(ds, q, (((0,), (0,)), ((), ())), preferred_element_type=f32) * scale
+            gr = jnp.dot(ds, kr_ref[...], preferred_element_type=f32) * scale
+            back, gain = turned_back(qp_ref[at, hc], gq, gr, at)
+            gcat[at, hc] = back.astype(bf16)
+            gqk[0:1, :] += gain
+            return 0
+
+        with jax.named_scope("process"):
+            lax.fori_loop(0, hp, head, 0)
+
+    def mix(count):
+        for _ in range(count):
+            advance(mix_steps, "mix")
+
+    near = far_first(z, zs)[::-1]
+    mix(2 * zs)
+    process(near[0])
+    for h in range(1, zs):
+        sides = (
+            (z - h, z - h >= 0, z < zs - 1, 2, szr),
+            (z + h, z + h < zs, z > 0, -2, szl),
+        )
+        with jax.named_scope("hop"):
+            for zz, when, on, dz, sem in sides:
+                got(chunk(zz, k), sem.at[zz], rz.at[zz], (f, c), when)
+                w.send(chunk(zz, k), chunk(zz, k), sem.at[zz], rz.at[zz], (f, c + dz), jnp.logical_and(when, on))
+                w.send(chunk(zz, k), chunk(zz, k), ssib.at[zz], rsib.at[zz], sib, when)
+        mix(zs - 1)
+        with jax.named_scope("rest"):
+            for zz, when, *_ in sides:
+                got(chunk(zz, 1 - k), ssib.at[zz], rsib.at[zz], sib, when)
+        process(near[h])
+    w.send(gkv, gkv2, sk.at[0], sk.at[1], sib)
+    mix(2)
+
+    with jax.named_scope("gwo"):
+        def gwo_block(j, _):
+            cols = pl.ds(pl.multiple_of(j * 256, 256), 256)
+            r = res[:, :, cols].reshape(span, 256)
+            o = lax.dot_general(ctx_ref[...], r, (((0,), (0,)), ((), ())), preferred_element_type=f32).astype(bf16)
+            gwo[:, :, cols] = o.reshape(hp, hd, 256)
+            return 0
+
+        lax.fori_loop(0, width // 256, gwo_block, 0)
+    head_steps = head_sum_steps(w, nf, nc, hp, gwo, gwo_ref, *head_b)
+    advance(head_steps, "heads")
+    mix(2)
+    with jax.named_scope("kv"):
+        got(gkv2, sk.at[0], sk.at[1], sib)
+
+        def keys(i, _):
+            at = pl.ds(pl.multiple_of(i * 2 * rows, 2 * rows), 2 * rows)
+            back, gain = turned_back(kp_ref[at, :], gk, gkv[0, at, :] + gkv2[0, at, :], at)
+            gv = gkv[1, at, :] + gkv2[1, at, :]
+            gcat[at, pl.ds(qw, hd)] = jnp.where(first, back, gv).astype(bf16)
+            gqk[1:2, :] += jnp.where(first, gain, 0.0)
+            return 0
+
+        lax.fori_loop(0, zs, keys, 0)
+    t, u = sum_bufs[0], sum_bufs[1]
+
+    def make(zz):
+        at = pl.ds(pl.multiple_of(2 * zz * rows, 2 * rows), 2 * rows)
+        a = gcat[at, 0:qw]
+        b = gcat[at, qw : qw + hd]
+        for dst, kk in ((u, 1 - k), (t, k)):
+            def block(j, _, dst=dst, kk=kk):
+                slabs = pl.ds(kk * (half // 64) + j * 8, 8)
+                wq = w_ref[slabs, :, 0:qw].reshape(512, qw)
+                wk = w_ref[slabs, :, pl.ds(pl.multiple_of(qw + k * hd, hd), hd)].reshape(512, hd)
+                o = lax.dot_general(a, wq, (((1,), (1,)), ((), ())), preferred_element_type=f32)
+                o = o + lax.dot_general(b, wk, (((1,), (1,)), ((), ())), preferred_element_type=f32)
+                cols = pl.ds(pl.multiple_of(kk * half + j * 512, 512), 512)
+                gat[:, cols] += jnp.sum(o * nm_ref[at, cols].astype(f32), axis=0, keepdims=True)
+                dst[zz, :, :, pl.ds(pl.multiple_of(j * 512, 512), 512)] = o.astype(bf16).reshape(2, rows, 512)
+                return 0
+
+            lax.fori_loop(0, half // 512, block, 0)
+
+    sum_steps = line_sum_steps(w, zs, make, out_ref, *sum_bufs)
+    for _ in range(2):
+        advance(sum_steps, "sum")
+    advance(head_steps, "heads")
+    with jax.named_scope("gw"):
+        def gw_block(j, _):
+            cols = pl.ds(pl.multiple_of(j * 256, 256), 256)
+            o = lax.dot_general(nm_ref[:, cols], gcat[...], (((0,), (0,)), ((), ())), preferred_element_type=f32).astype(bf16)
+            gw[j // 2, pl.ds(j % 2 * 4, 4)] = o.reshape(4, 64, qw + hd)
+            return 0
+
+        lax.fori_loop(0, width // 256, gw_block, 0)
+    weight_steps = weight_sum_steps(w, nf, nc, gw, go_ref, *weight_b)
+    advance(weight_steps, "weights")
+    for turn in "mmmssmmsmmwsmsmwhs":
+        if turn == "s":
+            advance(sum_steps, "sum")
+        elif turn == "w":
+            advance(weight_steps, "weights")
+        elif turn == "h":
+            advance(head_steps, "heads")
+        else:
+            mix(1)
+    for cc in range(nc):
+        for ff in range(nf):
+            lanes = pl.ds(128 * ((ff * nc + cc) // 2), 128)
+            tl[cc, ff, 0:1, :] = gat[:, lanes] / gat_ref[:, lanes]
+            tl[cc, ff, 1:2, :] = moe_ref[:, lanes]
+            tl[cc, ff, 2:4, :] = gqk[...]
+            tl[cc, ff, 4:8, :] = jnp.zeros((4, hd), f32)
+    small_steps = tile_steps(w, nf, nc, tl, to_ref, *tile_b)
+    advance(small_steps, "tiles")
+    for name, steps in (("sum", sum_steps), ("heads", head_steps), ("mix", mix_steps), ("weights", weight_steps), ("tiles", small_steps)):
+        while advance(steps, name):
+            pass
+    w.drain()
+
+
+def gradients(res, nm, wcat, wo, qp, kp, qr, kr, v, ctx, lse, cosine, sine, pos, gqk, gat, moe, mix, nf, zs, hp, scale, cid):
+    rows, width = res.shape
+    nc = 2 * zs
+    span = nc * rows
+    hd = cosine.shape[1]
+    bf16, f32 = jnp.bfloat16, jnp.float32
+    D = pltpu.SemaphoreType.DMA
+    S = jax.ShapeDtypeStruct
+    half = width // 2
+    cols = hp * hd + hd
+    shard = wcat.shape[1]
+    spill = lambda n: (S((n, 2, rows, half), bf16), ANY)
+    outs = [
+        (S((rows, width), bf16), VM),
+        (S((nc, shard, cols), bf16), VM),
+        (S((hd, width), bf16), VM),
+        (S((nf * nc, 8, hd), f32), VM),
+        (S((rows, width), bf16), VM),
+        spill(4 * zs), spill(2 * zs), spill(zs), spill(zs), spill(zs),
+    ]
+    V = pltpu.VMEM
+    chunk = (2, rows, half)
+    scratch = [V((nc, rows, width), bf16), V((2, span, hd), f32), V((2, span, hd), f32), V((span, cols), bf16),
+               V((nf, nc, shard, cols), bf16), V((hp, hd, width), bf16), V((nc, nf, 8, hd), f32), V((2, hd), f32), V((1, width), f32),
+               D(()), D((2,)), D((zs,)), D((zs,)), D((zs,)), D((zs,)), D((zs,)), D((2,))]
+    scratch += tile_bufs(nf, nc, (8, hd)) + line_sum_bufs(zs, rows, half, bf16)
+    scratch += [V((5,) + chunk, bf16), V((3,) + chunk, bf16), V((rows, half), bf16), D((5,)), D((4 * zs,)), D((4 * zs,)), D((2 * zs,)), D((2 * zs,)),
+                D((zs,)), D((zs,)), D((zs,)), D((zs,)), D((zs,)), D((zs,)), D((2,))]
+    scratch += [V((2, 2, hd // 2, width), bf16), V((2, hd // 2, width), bf16), D((2,)), D((2, 3)), D((2, 3)), D((2,)), D((2,))]
+    scratch += [V((2, 2, nc // 2, shard, cols), bf16), V((2, nc // 2, shard, cols), bf16), D((6,)), D((6,)), D((nc,)), D((nc,))]
+    return pl.pallas_call(
+        lambda *refs: grad_kernel(nf, zs, hp, scale, refs),
+        out_shape=[s for s, _ in outs],
+        in_specs=[VM] * 18 + [ANY],
+        out_specs=[b for _, b in outs],
+        scratch_shapes=scratch,
+        compiler_params=pltpu.CompilerParams(collective_id=cid, has_side_effects=True, vmem_limit_bytes=62 * 2**20),
+        name="gradients",
+    )(res, nm, wcat, wo, qp, kp, qr, kr, v, ctx, lse, cosine, sine, pos[:, None], pos[None, :], gqk, gat, moe, mix)
+
+
+def expert_kernel(nf, zs, refs):
+    (tok, top, place, mixing, wg, wu, wd,
+     out_ref, shares, arr, garr, hid, ggp, gup,
+     tb, cb, a, g, rows_b, t, u, r0, r1, r2, ral, rar, fin, sh,
+     lt, lc, la, lg, ls, s0, q0, s1, q1, s2, q2, szr, szl, rzr, rzl, sf) = refs
+    f, c, z, k = place_of()
+    nc = 2 * zs
+    rows, width = tb.shape[2:]
+    half = width // 2
+    cap = place.shape[1]
+    per = zs * cap
+    f32, bf16 = jnp.float32, jnp.bfloat16
+    sib = (f, c + 1 - 2 * k)
+    f1 = flip(f, 2 - k)
+    f2 = flip(f, 1 + k)
+    cols = [flip(flip(f, 1), 2), flip(f, 1), flip(f, 2), f]
+    order = far_first(z, zs)
+    with jax.named_scope("greet"):
+        greet(f, c, z, zs, True)
+    w = Wire()
+
+    def fetch(col, s, slot):
+        two = pl.ds(col * nc + 2 * s, 2)
+        return (
+            pltpu.make_async_copy(tok.at[two], tb.at[slot], lt.at[slot]),
+            pltpu.make_async_copy(top.at[two], cb.at[slot], lc.at[slot]),
+        )
+
+    def compute(li):
+        col = cols[li]
+        base = pl.multiple_of(col * per, 16)
+        for copy in fetch(col, 0, 0):
+            copy.start()
+        if li:
+            for copy in keep:
+                copy.wait()
+
+        def pick(s, _):
+            slot = s % 2
+
+            @pl.when(s < zs - 1)
+            def _():
+                for copy in fetch(col, s + 1, 1 - slot):
+                    copy.start()
+
+            for copy in fetch(col, s, slot):
+                copy.wait()
+            at = pl.ds(pl.multiple_of(s * cap, 16), cap)
+            a[at, :] = jnp.dot(place[col * zs + s], tb[slot].reshape(2 * rows, width), preferred_element_type=f32).astype(bf16)
+            g[at, :] = jnp.dot(mixing[col * zs + s], cb[slot].reshape(2 * rows, width), preferred_element_type=f32).astype(bf16)
+            return 0
+
+        with jax.named_scope("pick"):
+            lax.fori_loop(0, zs, pick, 0)
+        mine = pl.ds(base, per)
+        keep[:] = [pltpu.make_async_copy(a, arr.at[mine], la), pltpu.make_async_copy(g, garr.at[mine], lg)]
+        for copy in keep:
+            copy.start()
+
+        def hidden(j, _):
+            cc = pl.ds(pl.multiple_of(j * 256, 256), 256)
+            gate = jnp.dot(a[...], wg[:, cc], preferred_element_type=f32)
+            up = jnp.dot(a[...], wu[:, cc], preferred_element_type=f32)
+            back = lax.dot_general(g[...], wd[cc, :], (((1,), (1,)), ((), ())), preferred_element_type=f32)
+            sig = jax.nn.sigmoid(gate)
+            act = gate * sig
+            hid[mine, cc] = (act * up).astype(bf16)
+            ggp[mine, cc] = (back * up * sig * (1.0 + gate * (1.0 - sig))).astype(bf16)
+            gup[mine, cc] = (back * act).astype(bf16)
+            return 0
+
+        with jax.named_scope("hidden"):
+            lax.fori_loop(0, wg.shape[1] // 256, hidden, 0)
+
+        def rows_of(j, _):
+            cc = pl.ds(pl.multiple_of(j * 256, 256), 256)
+            o = lax.dot_general(ggp[mine, :], wg[cc, :], (((1,), (1,)), ((), ())), preferred_element_type=f32)
+            o = o + lax.dot_general(gup[mine, :], wu[cc, :], (((1,), (1,)), ((), ())), preferred_element_type=f32)
+            rows_b[:, cc] = o.astype(bf16)
+            return 0
+
+        with jax.named_scope("rows"):
+            lax.fori_loop(0, width // 256, rows_of, 0)
+
+        def spread(s, _):
+            at = pl.ds(pl.multiple_of(s * cap, 16), cap)
+            p = place[col * zs + s]
+            for dst, kk in ((u.at[li % 2], 1 - k), (t.at[pl.ds(li * zs, zs)], k)):
+                r = rows_b[at, pl.ds(pl.multiple_of(kk * half, 128), half)]
+                o = lax.dot_general(p, r, (((0,), (0,)), ((), ())), preferred_element_type=f32)
+                dst[s] = o.astype(bf16).reshape(2, rows, half)
+            return 0
+
+        if li >= 2:
+            w.settle(passed[li - 2])
+        with jax.named_scope("spread"):
+            lax.fori_loop(0, zs, spread, 0)
+        passed.append(
+            [w.send(u.at[li % 2, zz], r0.at[li * zs + zz], s0.at[li * zs + zz], q0.at[li * zs + zz], sib) for zz in order]
+        )
+
+    def pair(li, zz):
+        m = li * zs + zz
+        got(r0.at[m], s0.at[m], q0.at[m], sib)
+        add_into(t.at[m], r0.at[m])
+
+    def second(li, zz, when):
+        got(r1.at[zz], s1.at[zz], q1.at[zz], (f1, c), when)
+
+        @pl.when(when)
+        def _():
+            add_into(t.at[li * zs + zz], r1.at[zz])
+
+        w.send(t.at[li * zs + zz], r2.at[zz], s2.at[zz], q2.at[zz], (f2, c), when)
+
+    keep, passed = [], []
+    compute(0)
+    for zz in order:
+        pair(0, zz)
+        w.send(t.at[zz], r1.at[zz], s1.at[zz], q1.at[zz], (f1, c))
+    for li in (1, 2):
+        compute(li)
+        is_first = k == 2 - li
+        for zz in order:
+            pair(li, zz)
+            w.send(t.at[li * zs + zz], r1.at[zs + zz], s1.at[zs + zz], q1.at[zs + zz], (f1, c), is_first)
+        for zz in order:
+            second(li, zz, jnp.logical_not(is_first))
+    compute(3)
+    for copy in keep:
+        copy.wait()
+
+    def give(i, _):
+        at = pl.ds(pl.multiple_of(i * per, 16), per)
+
+        def out_of(j, _):
+            cc = pl.ds(pl.multiple_of(j * 256, 256), 256)
+            rows_b[:, cc] = jnp.dot(hid[at, :], wd[:, cc], preferred_element_type=f32).astype(bf16)
+            return 0
+
+        lax.fori_loop(0, width // 256, out_of, 0)
+
+        def one(s, _):
+            slot = s % 2
+            there = lambda ss: pltpu.make_async_copy(sh.at[slot], shares.at[pl.ds(i * nc + 2 * ss, 2)], ls.at[slot])
+
+            @pl.when(s > 1)
+            def _():
+                there(s - 2).wait()
+
+            e = rows_b[pl.ds(pl.multiple_of(s * cap, 16), cap), :]
+            o = lax.dot_general(mixing[i * zs + s], e, (((0,), (0,)), ((), ())), preferred_element_type=f32)
+            sh[slot] = o.astype(bf16).reshape(2, rows, width)
+            there(s).start()
+            return 0
+
+        lax.fori_loop(0, zs, one, 0)
+        for s in (zs - 2, zs - 1):
+            pltpu.make_async_copy(sh.at[s % 2], shares.at[pl.ds(i * nc + 2 * s, 2)], ls.at[s % 2]).wait()
+        return 0
+
+    base = 3 * zs
+
+    def complete(zz):
+        pair(3, zz)
+        got(r1.at[zs + zz], s1.at[zs + zz], q1.at[zs + zz], (f1, c))
+        add_into(t.at[base + zz], r1.at[zs + zz])
+        got(r2.at[zz], s2.at[zz], q2.at[zz], (f2, c))
+        add_into(t.at[base + zz], r2.at[zz])
+
+    for i, zz in enumerate(order[:-1]):
+        with jax.named_scope("complete"):
+            complete(zz)
         right = zz > z
         from_left = jnp.logical_and(right, z > 0)
         from_right = jnp.logical_and(jnp.logical_not(right), z < zs - 1)
-        got(ral.at[zz], szr.at[zz], rzr.at[zz], (f, c), from_left)
-        got(rar.at[zz], szl.at[zz], rzl.at[zz], (f, c), from_right)
+        with jax.named_scope("line"):
+            got(ral.at[zz], szr.at[zz], rzr.at[zz], (f, c), from_left)
+            got(rar.at[zz], szl.at[zz], rzl.at[zz], (f, c), from_right)
 
         @pl.when(from_left)
         def _():
-            add_into(t.at[zz], ral.at[zz])
+            add_into(t.at[base + zz], ral.at[zz])
 
         @pl.when(from_right)
         def _():
-            add_into(t.at[zz], rar.at[zz])
-
-        w.send(t.at[zz], ral.at[zz], szr.at[zz], rzr.at[zz], (f, c + 2), right)
-        w.send(t.at[zz], rar.at[zz], szl.at[zz], rzl.at[zz], (f, c - 2), jnp.logical_not(right))
-        advance(small_steps)
-        if zi == 0:
-            for p, (fa, fb, fc) in enumerate(parts):
-                for i in (0, 1):
-                    gcopies[2 * p + i].wait()
-                    got(ga.at[p, i], sg.at[2 * p + i], rg.at[2 * p + i], (fa, c))
-                    add_into(gt.at[p, i], ga.at[p, i])
-                    if i == 0:
-                        w.send(gt.at[p, 0], gb.at[p], sg.at[4 + p], rg.at[4 + p], (fb, c))
-        if zi == 1:
-            for p, (fa, fb, fc) in enumerate(parts):
-                got(gb.at[p], sg.at[4 + p], rg.at[4 + p], (fb, c))
-                add_into(gt.at[p, 1], gb.at[p])
-            for cc in range(nc):
-                w.send(gt.at[cc // hc, 1, cc % hc], go_ref.at[c], sa.at[cc], ra.at[c], (f, cc), c != cc)
-
-            def keep(cc):
-                @pl.when(c == cc)
-                def _():
-                    go_ref[cc] = gt[cc // hc, 1, cc % hc]
-
-            for cc in range(nc):
-                keep(cc)
-    complete(zs - 1)
-    got(ral.at[z], szr.at[z], rzr.at[z], (f, c), z > 0)
-    got(rar.at[z], szl.at[z], rzl.at[z], (f, c), z < zs - 1)
+            add_into(t.at[base + zz], rar.at[zz])
+
+        w.send(t.at[base + zz], ral.at[zz], szr.at[zz], rzr.at[zz], (f, c + 2), right)
+        w.send(t.at[base + zz], rar.at[zz], szl.at[zz], rzl.at[zz], (f, c - 2), jnp.logical_not(right))
+        with jax.named_scope("give"):
+            give(i, 0)
+    with jax.named_scope("complete"):
+        complete(z)
+    with jax.named_scope("give"):
+        for i in range(zs - 1, nf):
+            give(i, 0)
+    with jax.named_scope("line"):
+        got(ral.at[z], szr.at[z], rzr.at[z], (f, c), z > 0)
+        got(rar.at[z], szl.at[z], rzl.at[z], (f, c), z < zs - 1)
 
     @pl.when(z > 0)
     def _():
-        add_into(t.at[z], ral.at[z])
+        add_into(t.at[base + z], ral.at[z])
 
     @pl.when(z < zs - 1)
     def _():
-        add_into(t.at[z], rar.at[z])
-
-    w.send(t.at[z, 1 - k], fin, sf.at[0], sf.at[1], sib)
-    o_ref[:, pl.ds(pl.multiple_of(k * half, 128), half)] = t[z, k]
-    for cc in range(nc):
-        got(go_ref.at[cc], sa.at[cc], ra.at[cc], (f, c), c != cc)
+        add_into(t.at[base + z], rar.at[z])
+
+    w.send(t.at[base + z, 1 - k], fin, sf.at[0], sf.at[1], sib)
+    out_ref[:, pl.ds(pl.multiple_of(k * half, 128), half)] = t[base + z, k]
     got(fin, sf.at[0], sf.at[1], sib)
-    o_ref[:, pl.ds(pl.multiple_of((1 - k) * half, 128), half)] = fin[...]
-    while advance(small_steps):
-        pass
+    out_ref[:, pl.ds(pl.multiple_of((1 - k) * half, 128), half)] = fin[...]
     w.drain()
 
 
-def tail(x, g, tl, nf, zs, cid):
-    n, rows, width = x.shape
-    nc = 2 * zs
+def experts_of(tokens, top, place, mixing, wg, wu, wd, nf, zs, cid):
+    n, rows, width = tokens.shape
+    slots = place.shape[0] * place.shape[1]
+    per = slots // nf
+    ff = wg.shape[1]
+    half = width // 2
+    bf16 = jnp.bfloat16
+    S = jax.ShapeDtypeStruct
     D = pltpu.SemaphoreType.DMA
-    half = width // 2
-    V = lambda m: pltpu.VMEM((m, 2, rows, half), x.dtype)
-    gs = g.shape[2:]
-    G = lambda *lead: pltpu.VMEM(lead + (nc // 2,) + gs, g.dtype)
+    V = lambda *s: pltpu.VMEM(s, bf16)
+    C = lambda *m: pltpu.VMEM(m + (2, rows, half), bf16)
+    outs = [
+        (S((rows, width), bf16), VM),
+        (S((n, rows, width), bf16), ANY),
+        (S((slots, width), bf16), ANY),
+        (S((slots, width), bf16), ANY),
+        (S((slots, ff), bf16), VM),
+        (S((slots, ff), bf16), VM),
+        (S((slots, ff), bf16), VM),
+    ]
+    scratch = [V(2, 2, rows, width), V(2, 2, rows, width), V(per, width), V(per, width), V(per, width),
+               C(nf * zs), C(2, zs), C(nf * zs), C(2 * zs), C(zs), C(zs), C(zs), V(rows, half), V(2, 2, rows, width),
+               D((2,)), D((2,)), D(()), D(()), D((2,)), D((nf * zs,)), D((nf * zs,)), D((2 * zs,)), D((2 * zs,)), D((zs,)), D((zs,)),
+               D((zs,)), D((zs,)), D((zs,)), D((zs,)), D((2,))]
     return pl.pallas_call(
-        functools.partial(tail_kernel, nf, zs),
-        out_shape=(
-            jax.ShapeDtypeStruct((rows, width), x.dtype),
-            jax.ShapeDtypeStruct((nc,) + gs, g.dtype),
-            jax.ShapeDtypeStruct((nf * nc,) + tl.shape[2:], tl.dtype),
-        ),
-        in_specs=[ANY, ANY, VM],
-        out_specs=(VM, VM, VM),
-        scratch_shapes=[V(zs), V(zs), V(zs), V(zs), pltpu.VMEM((rows, half), x.dtype), G(2, 2), G(2, 2), G(2),
-            D((zs,)), D((zs,)), D((zs,)), D((zs,)), D((zs,)), D((zs,)), D((zs,)), D((2,)), D((4,)), D((6,)), D((6,)), D((nc,)), D((nc,))] + tile_bufs(nf, nc, tl.shape[2:]),
-        compiler_params=pltpu.CompilerParams(collective_id=cid, has_side_effects=True, vmem_limit_bytes=60 * 2**20),
-        name="tail",
-    )(x, g, tl)
-
-
-def attend_grad_kernel(scale, qb, q_ref, k_ref, v_ref, c_ref, g_ref, l_ref, pr_ref, pc_ref, gq_ref, gk_ref, gv_ref):
-    rows = q_ref.shape[0]
-    keys = k_ref[...]
-    values = v_ref[...]
-
-    @pl.when(pl.program_id(0) == 0)
-    def _():
-        gk_ref[...] = jnp.zeros_like(gk_ref)
-        gv_ref[...] = jnp.zeros_like(gv_ref)
-
-    lane = lax.broadcasted_iota(jnp.int32, (1, l_ref.shape[1]), 1)
-    for i in range(rows // qb):
-        at = pl.ds(i * qb, qb)
-        q = q_ref[at, :]
-        g = g_ref[at, :]
-        s = lax.dot_general(q, keys, (((1,), (1,)), ((), ())), preferred_element_type=jnp.float32) * scale
-        p = jnp.where(pc_ref[...] <= pr_ref[at, :], jnp.exp(s - jnp.sum(jnp.where(lane == pl.program_id(0), l_ref[at, :], 0.0), axis=-1, keepdims=True)), 0.0)
-        gv_ref[...] += lax.dot_general(p.astype(jnp.bfloat16), g, (((0,), (0,)), ((), ())), preferred_element_type=jnp.float32)
-        gp = lax.dot_general(g, values, (((1,), (1,)), ((), ())), preferred_element_type=jnp.float32)
-        delta = jnp.sum(g.astype(jnp.float32) * c_ref[at, :].astype(jnp.float32), axis=-1, keepdims=True)
-        ds = (p * (gp - delta)).astype(jnp.bfloat16)
-        gq_ref[at, :] = jnp.dot(ds, keys, preferred_element_type=jnp.float32) * scale
-        gk_ref[...] += lax.dot_general(ds, q, (((0,), (0,)), ((), ())), preferred_element_type=jnp.float32) * scale
-
-
-def attend_grad(q, keys, values, ctx, grad, lse, pos, scale):
-    rows, width = q.shape
-    hd = keys.shape[1]
-    col = pl.BlockSpec((rows, hd), lambda h: (0, h))
-    full = pl.BlockSpec((rows, hd), lambda h: (0, 0))
-    return pl.pallas_call(
-        functools.partial(attend_grad_kernel, scale, 256),
-        grid=(width // hd,),
-        out_shape=(jax.ShapeDtypeStruct((rows, width), jnp.float32), jax.ShapeDtypeStruct((rows, hd), jnp.float32), jax.ShapeDtypeStruct((rows, hd), jnp.float32)),
-        in_specs=[col, full, full, col, col, full, pl.BlockSpec((rows, 1), lambda h: (0, 0)), pl.BlockSpec((1, rows), lambda h: (0, 0))],
-        out_specs=(col, full, full),
-        name="attend_grad",
-    )(q, keys, values, ctx, grad, lse, pos[:, None], pos[None, :])
+        lambda *refs: expert_kernel(nf, zs, refs),
+        out_shape=[s for s, _ in outs],
+        in_specs=[ANY, ANY] + [VM] * 5,
+        out_specs=[b for _, b in outs],
+        scratch_shapes=scratch,
+        compiler_params=pltpu.CompilerParams(collective_id=cid, has_side_effects=True, vmem_limit_bytes=62 * 2**20),
+        name="experts",
+    )(tokens, top, place, mixing, wg, wu, wd)
 
 
 def head_body(
@@ -1405,17 +1915,11 @@
     (x_seq, normed_in, w_all, dealt, wo_all, top_all, q_pre, k_pre, query_rot, key_rot, values, context, lse, hidden_res, tokens) = attention(
         x_own, packed, by_place(tiles), w_out, top_own.astype(bf16), cosine, sine, pos, nf, zs, hp, scale, 0
     )
-    lin = lambda ff, cc: ff * nc + cc
-    hops = [(h, lin(h % hp, h // hp)) for h in range(n)]
     qw = hp * hd
-    w_cat = w_all.reshape(n * shard, qw + 2 * hd)
-    wo_mine = wo_all.reshape(qw, width)
     full_row = lambda r: dealt[:, r].reshape(-1, rows // gs, rows).sum(axis=1).reshape(-1)
     g_attn, g_moe = full_row(1), full_row(4)
     g_qk = dealt[:, 2:4].sum(axis=0)
     route_w = dealt[:, 0, :]
-    q_pre = q_pre.reshape(span, hp, hd)
-    k_pre = k_pre.reshape(span, 1, hd)
     hit = route_w > 0.0
     below = (jnp.arange(rows)[:, None] < jnp.arange(rows)[None, :]).astype(f32)
     rank = jnp.dot(hit.astype(f32), below, preferred_element_type=f32).astype(jnp.int32)
@@ -1423,74 +1927,37 @@
     place = slot.astype(bf16)
     mixing = jnp.where(slot, route_w[:, None, :], 0.0).astype(bf16)
     gate_w, up_w, down_w = w_gate[0], w_up[0], w_down[0]
-    pick = lambda table, rws: jnp.einsum("srt,std->srd", table, rws, preferred_element_type=f32).astype(bf16).reshape(n * capacity, width)
-    back = lambda table, rws: jnp.einsum("srt,srd->std", table, rws.reshape(n, capacity, width), preferred_element_type=f32).astype(bf16)
-    arrived = pick(place, tokens)
-    gate_pre = jnp.dot(arrived, gate_w, preferred_element_type=f32)
-    up_pre = jnp.dot(arrived, up_w, preferred_element_type=f32)
-    gate_sig = jax.nn.sigmoid(gate_pre)
-    gate_act = gate_pre * gate_sig
-    expert_hidden = (gate_act * up_pre).astype(bf16)
-
-    grad_arrived = pick(mixing, top_all.reshape(n, rows, width))
-    grad_hidden = contract_cols(grad_arrived, down_w)
-    grad_gate_pre = (grad_hidden * up_pre * gate_sig * (1.0 + gate_pre * (1.0 - gate_sig))).astype(bf16)
-    grad_up_pre = (grad_hidden * gate_act).astype(bf16)
-    grad_rows = (contract_cols(grad_gate_pre, gate_w) + contract_cols(grad_up_pre, up_w)).astype(bf16)
-    grad_mid = scatter(back(place, grad_rows), zs, True, 3, nf).astype(f32)
+    def paired(table):
+        two = table.reshape(n // 2, 2, capacity, rows)
+        none = jnp.zeros((n // 2, capacity, rows), bf16)
+        upper = jnp.concatenate([two[:, 0], none], axis=2)
+        lower = jnp.concatenate([none, two[:, 1]], axis=2)
+        return jnp.concatenate([upper, lower], axis=1)
+
+    grad_mid, shares, arrived, grad_arrived, expert_hidden, grad_gate_pre, grad_up_pre = experts_of(
+        tokens, top_all, paired(place), paired(mixing), gate_w, up_w, down_w, nf, zs, 3
+    )
+    grad_mid = grad_mid.astype(f32)
 
     _, mid_back = jax.vjp(rms_scale, hidden_res, g_moe)
     grad_res_mid, grad_moe_gain = mid_back(grad_mid)
     grad_res = top_own + grad_res_mid
-    res_all = gather(grad_res.astype(bf16), zs, False, 4).reshape(span, width)
-
-    hidden_late, arrived_late, grad_arrived_late, _ = lax.optimization_barrier((expert_hidden, arrived, grad_arrived, grad_mid))
-    expert_out = jnp.dot(hidden_late, down_w, preferred_element_type=f32).astype(bf16)
-    mixed = lax.psum_scatter(back(mixing, expert_out).reshape(n * rows, width), ("fsdp", "cp"), scatter_dimension=0, tiled=True)
+
+    grad_down = contract_rows(expert_hidden, grad_arrived)
+    grad_gate = contract_rows(arrived, grad_gate_pre)
+    grad_up = contract_rows(arrived, grad_up_pre)
+
+    grad_in, grads, grad_wo, summed, mixed, *_ = gradients(
+        grad_res.astype(bf16), normed_in, w_all, wo_all, q_pre, k_pre, query_rot, key_rot, values, context, lse, cosine, sine, pos,
+        g_qk, g_attn[None], grad_moe_gain[None], shares, nf, zs, hp, scale, 4
+    )
     block_output = (hidden_res + mixed.astype(f32)).astype(bf16)
-    grad_down = contract_rows(hidden_late, grad_arrived_late)
-    grad_gate = contract_rows(arrived_late, grad_gate_pre)
-    grad_up = contract_rows(arrived_late, grad_up_pre)
-
-    grad_wo_mine = contract_rows(context, res_all)
-    hops_back = [(b, a) for a, b in hops]
-    grad_wo = lax.ppermute(
-        lax.psum_scatter(grad_wo_mine.astype(bf16), "fsdp", scatter_dimension=0, tiled=True), ("fsdp", "cp"), hops_back
-    ).astype(f32)
-    grad_context = contract_cols(res_all, wo_mine).astype(bf16)
-    grad_query, grad_keys, grad_values = attend_grad(query_rot, key_rot, values, context, grad_context, lse, pos, scale)
-    pairs = [(cc, cc + 1 - 2 * (cc % 2)) for cc in range(nc)]
-    both = jnp.stack([grad_keys, grad_values])
-    both = both + lax.ppermute(both, "cp", pairs)
-    grad_keys, grad_values = both[0], both[1]
-    _, query_back = jax.vjp(lambda pre, gain: head_post(pre, gain, cosine, sine), q_pre, g_qk[0])
-    grad_q_pre, grad_q_gain = query_back(grad_query.reshape(span, hp, hd))
-    _, key_back = jax.vjp(lambda pre, gain: head_post(pre, gain, cosine, sine), k_pre, g_qk[1])
-    grad_k_pre, grad_k_gain = key_back(grad_keys.reshape(span, 1, hd))
-    grad_q_b = grad_q_pre.reshape(span, qw).astype(bf16)
-    x32 = x_seq.reshape(span, width).astype(f32)
-    inv_in = lax.rsqrt(jnp.mean(x32 * x32, axis=-1, keepdims=True) + EPSILON)
-    first = k == 0
-    grad_kv_b = jnp.where(first, grad_k_pre.reshape(span, hd), grad_values).astype(bf16)
-    grad_cat = jnp.concatenate([grad_q_b, grad_kv_b], axis=1)
-    w_kv = jnp.where(first, w_cat[:, qw : qw + hd], w_cat[:, qw + hd :])
-    w_back = jnp.concatenate([w_cat[:, :qw], w_kv], axis=1)
-    grad_w = contract_rows(normed_in, grad_cat).astype(bf16)
-    grad_norm = contract_cols(grad_cat, w_back)
-    grad_attn_gain = jnp.sum(grad_norm * (x32 * inv_in), axis=0)
-    grad_k_gain = jnp.where(first, grad_k_gain, 0.0)
-    share = lambda v: v.reshape(n, -1)
-    qk_parts = jnp.stack([grad_q_gain, grad_k_gain]).reshape(2, n, -1).transpose(1, 0, 2).reshape(n, -1)
-    line0 = jnp.concatenate([share(grad_attn_gain), share(grad_moe_gain)], axis=1)
-    wide = lambda v: jnp.pad(v, ((0, 0), (0, rows - v.shape[1])))
-    sums = jnp.concatenate([wide(line0)[:, None], wide(qk_parts)[:, None], jnp.zeros((n, 6, rows), f32)], axis=1)
-    grad_in, grads, summed = tail(
-        grad_norm.astype(bf16).reshape(nc, rows, width), grad_w.reshape(nf, nc, shard, qw + hd), by_place(sums), nf, zs, 5
-    )
     total = jnp.sum(summed, axis=0)
-    own_attn_gain = total[0, :gs]
-    own_moe_gain = total[0, gs : 2 * gs]
-    own_qk = total[1, : qk_gain.size].reshape(2, -1)
+    part = lambda row, size: lax.dynamic_slice_in_dim(row, me * size % rows, size)
+    own_attn_gain = part(total[0], gs)
+    own_moe_gain = part(total[1], gs)
+    own_qk = jnp.stack([part(total[2], qs), part(total[3], qs)])
+    grad_wo = grad_wo.astype(f32)
     grad_wq = grads[:, :, :qw].transpose(1, 0, 2).reshape(shard, heads * hd).astype(f32)
     grad_kv = grads[:, :, qw:].reshape(kv_heads, per, shard, hd)
     grad_wk = grad_kv[:, 0].transpose(1, 0, 2).reshape(shard, kv_heads * hd).astype(f32)

time: 817 us -> 671 us (0.82)
  matrix products: 147 us -> 24.6 us
  Pallas kernels: 508 us -> 598 us
  waiting for transfers between devices: 39.1 us -> 0 us
  other arithmetic: 67.1 us -> 32.8 us
  local copies, waits for them, and re-layouts: 25.5 us -> 10.4 us
  between operations: 15.1 us -> 1.23 us
    dot_general x12 -> x0, matrix products: 109 us -> none  [the longest x5 44.3 us: contract_cols(): lax.dot_general(left, right, (((1,), (1,)), ((), ())), preferred_element_...]
    pallas_call x4 -> x2, Pallas kernels: 252 us -> 332 us  [the longest x1 200 us: gradients(): pl.pallas_call(lambda *refs: grad_kernel(nf, zs, hp, scale, refs), out_sh...]
    reduce_scatter x2 -> x0, waiting for transfers between devices: 39.1 us -> none  [the longest x1 39.1 us: head_body(): lax.psum_scatter(back(mixing, expert_out).reshape(n * rows, width), ('fsd...]
    dot_general x5 -> x3, matrix products: 37.8 us -> 24.4 us  [contract_rows(): lax.dot_general(left, right, (((0,), (0,)), ((), ())), preferred_element_...]
    pallas_call x1, Pallas kernels: 256 us -> 266 us  [attention(): pl.pallas_call(lambda *refs: attn_kernel(nf, zs, hp, scale, refs), out_sh...]
  transfers between devices with their start and end apart: 4 -> 0, of which waited for: 1 -> 0; matrix products, arithmetic and copies ran while one was open for 15% -> 0% of each run, Pallas kernels for 14% -> 0%
where the time goes in v3:
time: 671 us; the launch traced here: 667 us
  Pallas kernels  598 us (89%)
  other arithmetic  32.8 us (5%)
  matrix products  24.6 us (4%)
  local copies, waits for them, and re-layouts  10.4 us (2%)
    pallas_call x1, Pallas kernels, attention(): pl.pallas_call(lambda *refs: attn_kernel(nf, zs, hp, scale, refs), out_sh...  266 us
    pallas_call x1, Pallas kernels, gradients(): pl.pallas_call(lambda *refs: grad_kernel(nf, zs, hp, scale, refs), out_sh...  200 us
    pallas_call x1, Pallas kernels, experts_of(): pl.pallas_call(lambda *refs: expert_kernel(nf, zs, refs), out_shape=[s fo...  132 us
    dot_general x3, matrix products, contract_rows(): lax.dot_general(left, right, (((0,), (0,)), ((), ())), preferred_element_...  24.4 us

profile of v3, /device:TPU:0, one launch (start us, length us, event | category | flops | bytes accessed | tf_op | source)
XLA Modules:
  0.0 667.2 jit_solution(14205519161633152426)
XLA Ops:
  0.8 0.7 tile.46
  1.6 0.7 tile.56
  2.3 0.2 fusion.35
  2.5 0.7 bitcast_convert_fusion.3
  3.2 0.7 bitcast_convert_fusion.1
  3.9 1.6 fusion.63
  5.5 4.7 select_reduce_fusion
  10.2 0.7 fusion.51
  10.9 0.6 fusion.46.refs_8_.refs_14_
  11.5 0.7 select_reduce_fusion.1
  12.4 0.1 tile.55
  12.5 0.7 maximum_bitcast_fusion.refs_2_
  13.3 0.9 reshape.476
  14.2 0.9 reshape.478
  15.1 0.2 broadcast_multiply_fusion
  15.3 0.2 copy.55
  15.5 0.9 fusion.32.refs_7_.refs_13_
  16.4 1.0 pad_maximum_fusion.refs_1_
  17.4 0.9 bitcast_convert_fusion.refs_4_
  18.3 2.9 fusion.36
  21.1 266.1 %attention.1 = (bf16[8,128,2048]{2,1,0:T(8,128)(2,1)}, bf16[1024,2048]{1,0:T(8,128)(2,1)}, bf16[32,64,768]{2,1,0:T(8,128)(2,1)}, f32[32,8,128]{2,1,0:T(8,128)}, ...) custom-call(bf16[128,2048]{1,0:T(8,128)(2,1)} %bitcast.114, ...), custom_call_target="tpu_custom_call" | custom-call | tf_op jit(solution)/shard_map/attention/pallas_call | solution.py:1158
  287.3 1.4 multiply_reduce_fusion
  288.7 1.5 slice_reduce_fusion.refs_15_
  290.2 1.0 fusion.60
  291.1 1.1 fusion.61
  292.2 0.6 reduce_sum.107
  292.9 0.1 convolution_convert_fusion
  293.1 0.2 select_convert_fusion
  293.3 0.2 fusion.18
  293.6 1.0 fusion.13.refs_2_
  294.5 1.0 fusion.14.refs_3_
  295.5 131.6 %experts.1 = (bf16[128,2048]{1,0:T(8,128)(2,1)}, bf16[32,128,2048]{2,1,0:T(8,128)(2,1)}, bf16[1536,2048]{1,0:T(8,128)(2,1)}, bf16[1536,2048]{1,0:T(8,128)(2,1)},...) custom-call(bf16[32,128,2048]{2,1,0:T(8,128)(2,1)} %get-tuple-element.39.refs_0_, ...), custom_call_target="tpu_custom_call" | custom-call | tf_op jit(solution)/shard_map/experts/pallas_call | solution.py:1847
  427.2 2.0 fusion.7
  429.1 2.5 fusion.59.refs_0_
  431.6 200.5 %gradients.1 = (bf16[128,2048]{1,0:T(8,128)(2,1)}, bf16[8,64,640]{2,1,0:T(8,128)(2,1)}, bf16[128,2048]{1,0:T(8,128)(2,1)}, f32[32,8,128]{2,1,0:T(8,128)}, bf16[1...) custom-call(bf16[128,2048]{1,0:T(8,128)(2,1)} %fusion.59.refs_0_, ...), custom_call_target="tpu_custom_call" | custom-call | tf_op jit(solution)/shard_map/gradients/pallas_call | solution.py:1596
  632.2 1.4 fusion.9
  633.6 3.4 fusion.12
  637.0 0.6 fusion.56
  637.6 0.6 fusion.55
  638.3 0.6 pad_maximum_fusion.3
  638.9 0.7 copy.76
  639.6 0.7 copy.77
  640.3 0.1 convert_bitcast_fusion
  640.4 1.1 copy.65
  641.5 1.1 convert_element_type.113
  642.5 10.4 %convolution_bitcast_fusion.2 = f32[1,2048,768]{2,1,0:T(8,128)} fusion(bf16[1536,2048]{1,0:T(8,128)(2,1)} %get-tuple-element.59, bf16[1536,768]{1,0:T(8,128)(2,1)S(1)} %copy-done.10), kind=kOutput, calls=%fused_computation.2 | convolution fusion | flops 4831838208 | bytes 14942208 | tf_op jit(solution)/shard_map/dot_general | solution.py:93
  653.0 7.1 %convolution_bitcast_fusion.1 = f32[1,2048,768]{2,1,0:T(8,128)} fusion(bf16[1536,2048]{1,0:T(8,128)(2,1)S(1)} %bitcast.146, bf16[1536,768]{1,0:T(8,128)(2,1)S(1)} %copy-done.9), kind=kOutput, calls=%fused_computation.1 | convolution fusion | flops 4831838208 | bytes 14942208 | tf_op jit(solution)/shard_map/dot_general | solution.py:93
  660.1 7.0 %convolution_bitcast_fusion = f32[1,768,2048]{2,1,0:T(8,128)} fusion(bf16[1536,768]{1,0:T(8,128)(2,1)S(1)} %copy-done.8, bf16[1536,2048]{1,0:T(8,128)(2,1)S(1)} %bitcast.144), kind=kOutput, calls=%fused_computation | convolution fusion | flops 4831838208 | bytes 14942208 | tf_op jit(solution)/shard_map/dot_general | solution.py:93
  (66 shorter events, 1.0 us)
Async XLA Ops:
  0.6 15.8 %copy-start.5 = (bf16[64,4096]{1,0:T(8,128)(2,1)S(1)}, bf16[64,4096]{1,0:T(8,128)(2,1)}, u32[]{:S(2)}) copy-start(bf16[64,4096]{1,0:T(8,128)(2,1)} %param.18) | copy-start | bytes 1572868
  15.1 2.3 copy-start.1
  295.5 131.6 %copy-start = (f32[128,2048]{1,0:T(8,128)S(1)}, f32[128,2048]{1,0:T(8,128)}, u32[]{:S(2)}) copy-start(f32[128,2048]{1,0:T(8,128)} %get-tuple-element.38) | copy-start | bytes 3145732
  431.6 200.5 %copy-start.2 = (bf16[1,128,2048]{2,1,0:T(8,128)(2,1)S(1)}, bf16[1,128,2048]{2,1,0:T(8,128)(2,1)}, u32[]{:S(2)}) copy-start(bf16[1,128,2048]{2,1,0:T(8,128)(2,1)} %param.15) | copy-start | bytes 1572868
  431.6 200.5 %copy-start.6 = (f32[16,128]{1,0:T(8,128)S(1)}, f32[16,128]{1,0:T(8,128)}, u32[]{:S(2)}) copy-start(f32[16,128]{1,0:T(8,128)} %reduce_sum.107) | copy-start | bytes 24580
  633.5 3.4 copy-start.7
  633.6 5.3 copy-start.3
  638.9 2.6 copy-start.4
  640.3 2.3 copy-start.10
  641.5 11.5 %slice-start.2 = ((s8[6291456]{0:T(1024)(128)(4,1)}), s8[4194304]{0:T(1024)(128)(4,1)S(1)}, s32[]{:S(2)}) async-start(s8[6291456]{0:T(1024)(128)(4,1)} %bitcast.145), calls=%async_computation.2 | async-start | bytes 8388608
  642.5 10.4 %slice-start.3 = ((s8[6291456]{0:T(1024)(128)(4,1)}), s8[2097152]{0:T(1024)(128)(4,1)S(1)}, s32[]{:S(2)}) async-start(s8[6291456]{0:T(1024)(128)(4,1)} %bitcast.145), calls=%async_computation.3 | async-start | bytes 4194304
  642.5 10.4 %copy-start.9 = (bf16[1536,768]{1,0:T(8,128)(2,1)S(1)}, bf16[1536,768]{1,0:T(8,128)(2,1)}, u32[]{:S(2)}) copy-start(bf16[1536,768]{1,0:T(8,128)(2,1)} %get-tuple-element.61) | copy-start | bytes 7077892
  642.5 17.5 %slice-start = ((s8[6291456]{0:T(1024)(128)(4,1)}), s8[4194304]{0:T(1024)(128)(4,1)S(1)}, s32[]{:S(2)}) async-start(s8[6291456]{0:T(1024)(128)(4,1)} %bitcast.143), calls=%async_computation | async-start | bytes 8388608
  653.0 7.1 %slice-start.1 = ((s8[6291456]{0:T(1024)(128)(4,1)}), s8[2097152]{0:T(1024)(128)(4,1)S(1)}, s32[]{:S(2)}) async-start(s8[6291456]{0:T(1024)(128)(4,1)} %bitcast.143), calls=%async_computation.1 | async-start | bytes 4194304
  653.0 7.1 %copy-start.8 = (bf16[1536,768]{1,0:T(8,128)(2,1)S(1)}, bf16[1536,768]{1,0:T(8,128)(2,1)}, u32[]{:S(2)}) copy-start(bf16[1536,768]{1,0:T(8,128)(2,1)} %get-tuple-element.62) | copy-start | bytes 7077892
